TPU v7x, 32 devices: a whole 2x2x4 slice. The times are simulated.
32 devices in a mesh: curve: 8 (over z, y), sub: 4 (over x, core).
Axes of the slice: x: 2, y: 2, z: 4, core: 2. Of those that a mesh axis runs over, the one named last changes fastest.
Arguments:
- prognostic: float32 [4, 192, 32, 4, 4, 128], P(None, 'curve', 'sub'), may hold values from -6 to 6
- layer_mass: float32 [192, 32, 4, 4, 128], P('curve', 'sub'), may hold values from 0.5 to 2
- column_aux: bfloat16 [49152, 1013], P(('curve', 'sub')), may hold values from -6 to 6
- group_owner: int32 [24576, 1], P(('curve', 'sub')), may hold values from 0 to 31; in each aligned block of 768 rows (0 to 767, 768 to 1535, ...) at most 48 rows name the same one
- weight_in: bfloat16 [1525, 2048], replicated, may hold values from -0.15625 to 0.15625
- bias_in: float32 [2048], replicated, may hold values from -3 to 3
- weight_out: bfloat16 [2048, 512], replicated, may hold values from -0.125 to 0.125
- bias_out: float32 [512], replicated, may hold values from -2 to 2
Outputs:
- advanced: float32 [4, 192, 32, 4, 4, 128], P(None, 'curve', 'sub')
Inputs may be any that keep to these rules, and one draw needn't show every extreme that they name: `group_owner`: among the 768 columns of one device, at most 48 name the same owner, and every device owns some column.
All inputs are finite; a program needn't handle non-finite values.
Results may differ from a plain program's by a relative error of at most 0.0035.
Values may be sent and summed in bfloat16 or wider, within the bound.
No kernel may reach another device: no remote copies, remote signals or barrier semaphores. Data moves between devices by JAX's collectives and lax.ppermute only.
A program may use at most 128 MiB of HBM per device.

v0:
```python
import jax
import jax.numpy as jnp
import numpy as np
from jax import lax
from jax.sharding import PartitionSpec as P

section_step = 0.1


def with_halo(cells, sides, width):
    for axis, dim in sides:
        count = lax.axis_size(axis)
        head = lax.slice_in_dim(cells, 0, width, axis=dim)
        tail = lax.slice_in_dim(cells, cells.shape[dim] - width, cells.shape[dim], axis=dim)
        cells = jnp.concatenate(
            [
                lax.ppermute(tail, axis, [(i, (i + 1) % count) for i in range(count)]),
                cells,
                lax.ppermute(head, axis, [((i + 1) % count, i) for i in range(count)]),
            ],
            axis=dim,
        )
    return cells


def node_tables():
    nodes = np.array([-1.0, -1.0 / np.sqrt(5.0), 1.0 / np.sqrt(5.0), 1.0])
    quadrature = np.array([1.0 / 6.0, 5.0 / 6.0, 5.0 / 6.0, 1.0 / 6.0])
    products = np.array(
        [
            np.prod(
                [
                    nodes[left_node] - nodes[other_node]
                    for other_node in range(4)
                    if other_node != left_node
                ]
            )
            for left_node in range(4)
        ]
    )
    derivative = np.zeros((4, 4))
    for left_node in range(4):
        for other_node in range(4):
            if left_node != other_node:
                derivative[left_node, other_node] = products[left_node] / (
                    products[other_node] * (nodes[left_node] - nodes[other_node])
                )
            else:
                derivative[left_node, left_node] = sum(
                    (
                        1.0 / (nodes[left_node] - nodes[third_node])
                        for third_node in range(4)
                        if third_node != left_node
                    )
                )
    return (derivative.astype(np.float32), quadrature.astype(np.float32))


def advect(prognostic, derivative):
    along_first = jnp.einsum(
        "ik,fabkjl->fabijl", derivative, prognostic, precision=lax.Precision.HIGHEST
    )
    along_second = jnp.einsum(
        "jk,fabikl->fabijl", derivative, prognostic, precision=lax.Precision.HIGHEST
    )
    return -(prognostic[0:1] * along_first + prognostic[1:2] * along_second)


def node_mass(layer_mass, quadrature):
    return quadrature[:, None, None] * quadrature[None, :, None] * layer_mass


def cell_average(prognostic, node_weight):
    fields = prognostic.shape[0]
    rows_a, rows_b, levels = (node_weight.shape[0], node_weight.shape[1], node_weight.shape[4])
    weighted = (prognostic * node_weight[None]).reshape(fields, rows_a, rows_b, 2, 2, 2, 2, levels)
    weighted_sum = jnp.sum(weighted, axis=(4, 6))
    mass_sum = jnp.sum(node_weight.reshape(rows_a, rows_b, 2, 2, 2, 2, levels), axis=(3, 5))
    return weighted_sum / mass_sum[None]


def spread_cells(cells):
    return jnp.repeat(jnp.repeat(cells, 2, axis=3), 2, axis=4)


def apply_network(inputs, weight_in, bias_in, weight_out, bias_out):
    hidden = jax.nn.silu(
        jnp.dot(inputs, weight_in, preferred_element_type=jnp.float32) + bias_in
    ).astype(jnp.bfloat16)
    return (jnp.dot(hidden, weight_out, preferred_element_type=jnp.float32) + bias_out).astype(
        jnp.bfloat16
    )


def relay(buffer):
    return lax.all_to_all(buffer, ("curve", "sub"), split_axis=0, concat_axis=0, tiled=True)


def shards(
    prognostic, layer_mass, column_aux, group_owner, weight_in, bias_in, weight_out, bias_out
):
    derivative_np, quadrature_np = node_tables()
    derivative = jnp.asarray(derivative_np)
    quadrature = jnp.asarray(quadrature_np)
    fields = prognostic.shape[0]
    rows_a, rows_b, levels = (prognostic.shape[1], prognostic.shape[2], prognostic.shape[5])
    advection = advect(prognostic, derivative)
    node_weight = node_mass(layer_mass, quadrature)
    stacked = jnp.concatenate([advection * node_weight[None], node_weight[None]], axis=0)
    rims = jnp.stack([stacked[:, :, :, 0], stacked[:, :, :, 3]], axis=3)
    padded = with_halo(rims.astype(jnp.bfloat16), (("curve", 1),), 1).astype(rims.dtype)
    passed = jnp.concatenate(
        [
            (stacked[:, :, :, 0] + padded[:, :-2, :, 1])[:, :, :, None],
            stacked[:, :, :, 1:3],
            (stacked[:, :, :, 3] + padded[:, 2:, :, 0])[:, :, :, None],
        ],
        axis=3,
    )
    rims = jnp.stack([passed[:, :, :, :, 0], passed[:, :, :, :, 3]], axis=4)
    padded = with_halo(rims.astype(jnp.bfloat16), (("sub", 2),), 1).astype(rims.dtype)
    summed = jnp.concatenate(
        [
            (passed[:, :, :, :, 0] + padded[:, :, :-2, :, 1])[:, :, :, :, None],
            passed[:, :, :, :, 1:3],
            (passed[:, :, :, :, 3] + padded[:, :, 2:, :, 0])[:, :, :, :, None],
        ],
        axis=4,
    )
    section = prognostic + section_step * (summed[:fields] / summed[fields:])
    cells = cell_average(prognostic, node_weight)
    col_count = group_owner.shape[0]
    state_cols = (
        cells.transpose(1, 2, 3, 4, 0, 5).reshape(col_count, fields * levels).astype(jnp.bfloat16)
    )
    devices = lax.axis_size("curve") * lax.axis_size("sub")
    capacity = column_aux.shape[0] // devices
    targets = group_owner[:, 0]
    hits = (targets[:, None] == jnp.arange(devices, dtype=jnp.int32)[None]).astype(jnp.float32)
    positions = jnp.arange(col_count, dtype=jnp.int32)
    before = (positions[:, None] > positions[None, :]).astype(jnp.float32)
    earlier = jnp.dot(before, hits, precision=lax.Precision.HIGHEST)
    slot_index = jnp.sum(hits * earlier, axis=1).astype(jnp.int32)
    position = targets * capacity + slot_index
    selector = (position[:, None] == jnp.arange(devices * capacity, dtype=jnp.int32)[None]).astype(
        jnp.bfloat16
    )
    aux_width = column_aux.shape[1]
    aux_home = relay(column_aux.reshape(devices, capacity, aux_width)).reshape(
        devices * capacity, aux_width
    )
    aux_cols = jnp.dot(selector, aux_home, preferred_element_type=jnp.float32).astype(jnp.bfloat16)
    col_increment = apply_network(
        jnp.concatenate([state_cols, aux_cols], axis=1), weight_in, bias_in, weight_out, bias_out
    )
    back = col_increment.reshape(rows_a, rows_b, 2, 2, fields, levels).transpose(4, 0, 1, 2, 3, 5)
    return section + spread_cells(back.astype(jnp.float32))


def solution(mesh):
    return jax.shard_map(
        shards,
        mesh=mesh,
        in_specs=(
            P(None, "curve", "sub", None, None, None),
            P("curve", "sub", None, None, None),
            P(("curve", "sub"), None),
            P(("curve", "sub"), None),
            P(),
            P(),
            P(),
            P(),
        ),
        out_specs=P(None, "curve", "sub", None, None, None),
        check_vma=False,
    )
```

profile of v0, /device:TPU:0, one launch (start us, length us, event | category | flops | bytes accessed | tf_op | source)
XLA Modules:
  0.0 181.0 jit_solution(3857648282454887617)
XLA Ops:
  0.9 3.2 %copy_multiply_fusion.1 = f32[24,8,4,4,128]{4,2,3,1,0:T(4,128)} fusion(f32[24,8,4,4,128]{4,3,2,1,0:T(4,128)} %param.11, f32[4,4]{0,1:T(4,128)S(1)} %broadcast_multiply_fusion), kind=kLoop, calls=%fused_computation.42 | loop fusion | flops 393216 | bytes 3145792 | tf_op jit(solution)/shard_map/mul | solution.py:70
  4.1 3.1 %fusion.47 = f32[1,24,8,4,4,128]{5,3,4,2,1,0:T(4,128)} fusion(f32[24,8,4,4,128]{4,3,2,1,0:T(4,128)} %param.11, f32[4,4]{0,1:T(4,128)S(1)} %broadcast_multiply_fusion), kind=kLoop, calls=%fused_computation.70 | loop fusion | flops 393216 | bytes 3145792 | tf_op jit(solution)/shard_map/broadcast_in_dim | solution.py:109
  9.8 1.7 copy.32
  11.5 13.4 %fusion.40 = f32[4,4,24,8,4,128]{5,0,4,3,2,1:T(4,128)} fusion(f32[4,4,1,1,1,1]{1,0,5,4,3,2:T(4,128)S(1)} %copy-done.14, f32[4,24,8,4,4,128]{5,4,3,2,1,0:T(4,128)S(1)} %copy-done.2), kind=kOutput, calls=%fused_computation.69 | convolution fusion | flops 75497472 | bytes 12582976 | tf_op jit(solution)/shard_map/jk,fabikl->fabijl/dot_general | solution.py:63
  24.8 17.5 %fusion.8 = f32[4,24,8,4,4,128]{5,3,4,2,1,0:T(4,128)S(1)} fusion(f32[4,4,24,8,4,128]{5,0,4,3,2,1:T(4,128)} %fusion.40, f32[24,8,4,4,128]{4,2,3,1,0:T(4,128)} %copy_multiply_fusion.1, f32[24,8,4,4,128]{4,2,3,1,0:T(4,128)} %copy.32, f32[24,8,4,4,128]{4,2,3,1,0:T(4,128)} %copy.30, f32[4,4,1,1,1,1]{1,0,5,4,3,2:T(4,128)S(1)} %copy-done.14, ...), kind=kOutput, calls=%fused_computation.14 | convolution fusion | flops 83361792 | bytes 23593024 | tf_op jit(solution)/shard_map/ik,fabkjl->fabijl/dot_general | solution.py:60
  42.3 8.0 %fusion.37 = (bf16[5,24,8,1,4,128]{5,3,4,2,1,0:T(2,128)(2,1)S(1)}, f32[5,24,8,1,4,128]{5,3,4,2,1,0:T(1,128)}, bf16[5,24,8,1,4,128]{5,3,4,2,1,0:T(2,128)(2,1)S(1)}, f32[5,24,8,1,4,128]{5,3,4,2,1,0:T(1,128)}) fusion(f32[1,24,8,4,4,128]{5,3,4,2,1,0:T(4,128)} %fusion.47, f32[4,24,8,4,4,128]{5,3,4,2,1,0:T(4,128)S(1)} %fusion.8), kind=kLoop, calls=%fused_computation.66 | loop fusion | flops 1966080 | bytes 13762560 | tf_op jit(solution)/shard_map/convert.4
  52.3 3.0 %collective-permute-start = (bf16[5,1,8,2,4,128]{5,3,4,2,1,0:T(2,128)(2,1)S(1)}, bf16[5,1,8,2,4,128]{5,3,4,2,1,0:T(2,128)(2,1)S(1)}, u32[]{:S(2)}, u32[]{:S(2)}) collective-permute-start(bf16[5,1,8,2,4,128]{5,3,4,2,1,0:T(2,128)(2,1)S(1)} %get-tuple-element.19), channel_id=1, source_target_pairs={{0,4},{4,8},{8,12},{12,16},{16,20},{20,24},{24,28},{28,0},{1,5},{5... | collective-permute-start | bytes 245768 | tf_op jit(solution)/shard_map/ppermute | solution.py:17
  55.3 3.0 %collective-permute-start.1 = (bf16[5,1,8,2,4,128]{5,3,4,2,1,0:T(2,128)(2,1)S(1)}, bf16[5,1,8,2,4,128]{5,3,4,2,1,0:T(2,128)(2,1)S(1)}, u32[]{:S(2)}, u32[]{:S(2)}) collective-permute-start(bf16[5,1,8,2,4,128]{5,3,4,2,1,0:T(2,128)(2,1)S(1)} %get-tuple-element.20), channel_id=1, source_target_pairs={{4,0},{8,4},{12,8},{16,12},{20,16},{24,20},{28,24},{0,28},{5,1},{9... | collective-permute-start | bytes 245768 | tf_op jit(solution)/shard_map/ppermute | solution.py:19
  58.3 4.6 %copy.38 = bf16[1536,1013]{1,0:T(8,128)(2,1)} copy(bf16[1536,1013]{0,1:T(8,128)(2,1)} %param.12) | data formatting | bytes 6223872 | tf_op args[2]
  63.0 4.1 %all-to-all-start = ((bf16[32,48,1013]{2,1,0:T(8,128)(2,1)}), bf16[32,48,1013]{2,1,0:T(8,128)(2,1)}, u32[]{:S(2)}, u32[]{:S(2)}) async-start(bf16[32,48,1013]{2,1,0:T(8,128)(2,1)} %bitcast.50), calls=%async_computation | async-start | bytes 6291456 | tf_op jit(solution)/shard_map/all_to_all | solution.py:96
  67.0 9.2 %copy_multiply_fusion = f32[4,24,8,4,4,128]{5,3,4,2,1,0:T(4,128)} fusion(f32[4,24,8,4,4,128]{5,4,3,2,1,0:T(4,128)} %param.10, f32[24,8,4,4,128]{4,2,3,1,0:T(4,128)} %copy_multiply_fusion.1), kind=kLoop, calls=%fused_computation.17 | loop fusion | flops 1572864 | bytes 14155776 | tf_op jit(solution)/shard_map/mul | solution.py:76
  76.2 11.0 %reduce_sum.27 = f32[4,24,8,2,2,128]{5,3,4,2,1,0:T(2,128)} reduce(f32[4,24,8,2,2,2,2,128]{7,4,3,6,5,2,1,0:T(2,128)} %bitcast.47, f32[]{:T(128)} %constant.5.clone.1), dimensions={4,6}, to_apply=%region_0.0 | reduce | flops 1179648 | bytes 7864324 | tf_op jit(solution)/shard_map/reduce_sum | solution.py:77
  87.2 3.0 %reduce_sum.28 = f32[24,8,2,2,128]{4,2,3,1,0:T(2,128)S(1)} reduce(f32[24,8,2,2,2,2,128]{6,3,2,5,4,1,0:T(2,128)} %bitcast.48, f32[]{:T(128)} %constant.5.clone.1), dimensions={3,5}, to_apply=%region_1.0 | reduce | flops 294912 | bytes 1966084 | tf_op jit(solution)/shard_map/reduce_sum | solution.py:78
  90.2 20.9 %convert_add_fusion.1 = (f32[5,24,8,1,4,128]{5,3,4,2,1,0:T(1,128)S(1)}, f32[5,24,8,1,4,128]{5,3,4,2,1,0:T(1,128)S(1)}) fusion(f32[5,24,8,1,4,128]{5,3,4,2,1,0:T(1,128)} %get-tuple-element.6, bf16[5,1,8,2,4,128]{5,3,4,2,1,0:T(2,128)(2,1)S(1)} %collective-permute-done.1, bf16[5,1,8,2,4,128]{5,3,4,2,1,0:T(2,128)(2,1)S(1)} %collective-permute-done, ...), kind=kLoop, calls=%fused_computation.34 | loop fusion | flops 8847360 | bytes 9994240 | tf_op jit(solution)/shard_map/add | solution.py:114
  111.2 5.6 %fusion.1 = f32[5,24,8,4,4,128]{5,3,4,2,1,0:T(4,128)S(1)} fusion(f32[1,24,8,4,4,128]{5,3,4,2,1,0:T(4,128)S(1)} %copy-done.8, f32[4,24,8,4,4,128]{5,3,4,2,1,0:T(4,128)S(1)} %bitcast.46, f32[5,24,8,1,4,128]{5,3,4,2,1,0:T(1,128)S(1)} %get-tuple-element.18, f32[5,24,8,1,4,128]{5,3,4,2,1,0:T(1,128)S(1)} %get-tuple-element.17), kind=kLoop, calls=%fused_computation.4 | loop fusion | flops 15728640 | bytes 19660800 | tf_op jit(solution)/shard_map/concatenate | solution.py:112
  123.3 2.3 %copy.39 = bf16[768,512]{0,1:T(8,128)(2,1)} copy(bf16[768,512]{1,0:T(8,128)(2,1)} %bitcast.54) | data formatting | bytes 1572864 | tf_op jit(solution)/shard_map/convert_element_type | solution.py:134
  126.0 3.0 %slice.78 = f32[5,24,8,4,2,128]{5,3,4,2,1,0:T(4,128)S(1)} slice(f32[5,24,8,4,4,128]{5,3,4,2,1,0:T(4,128)} %copy-done.4), slice={[0:5], [0:24], [0:8], [0:4], [1:3], [0:128]} | slice | bytes 7864320 | tf_op jit(solution)/shard_map/slice | solution.py:125
  130.4 3.2 %convert_add_fusion = (f32[5,24,8,4,1,128]{5,3,4,2,1,0:T(4,128)S(1)}, f32[5,24,8,4,1,128]{5,3,4,2,1,0:T(4,128)S(1)}) fusion(f32[5,24,8,4,4,128]{5,3,4,2,1,0:T(4,128)S(1)} %copy-done.5, bf16[5,24,1,4,2,128]{5,3,4,2,1,0:T(4,128)(2,1)} %collective-permute-done.3, bf16[5,24,1,4,2,128]{5,3,4,2,1,0:T(4,128)(2,1)} %collective-permute-done.2, ...), kind=kLoop, calls=%fused_computation.28 | loop fusion | flops 4915200 | bytes 10321920 | tf_op jit(solution)/shard_map/add | solution.py:124
  135.2 4.2 %pad_maximum_fusion = f32[5,24,8,4,4,128]{5,3,4,2,1,0:T(4,128)} fusion(f32[5,24,8,4,1,128]{5,3,4,2,1,0:T(4,128)S(1)} %get-tuple-element.10, f32[5,24,8,4,2,128]{5,3,4,2,1,0:T(4,128)S(1)} %slice.78, f32[5,24,8,4,1,128]{5,3,4,2,1,0:T(4,128)S(1)} %get-tuple-element.9), kind=kLoop, calls=%fused_computation.5 | loop fusion | flops 3932160 | bytes 15728640 | tf_op jit(solution)/shard_map/concatenate | solution.py:122
  139.4 6.0 %fusion.21 = bf16[768,1013]{0,1:T(8,128)(2,1)} fusion(bf16[1536,1013]{1,0:T(8,128)(2,1)} %bitcast.13, s32[768]{0:T(1024)S(1)} %add_reduce_fusion), kind=kOutput, calls=%fused_computation.40 | convolution fusion | flops 2391924480 | bytes 4670976 | tf_op jit(solution)/shard_map/dot_general | solution.py:152
  145.5 11.8 %fusion.27 = f32[768,512]{1,0:T(8,128)} fusion(bf16[2048,512]{1,0:T(8,128)(2,1)S(1)} %copy-done, bf16[1525,2048]{1,0:T(8,128)(2,1)} %param.14, f32[2048]{0:T(1024)S(1)} %copy-done.15, bf16[768,1013]{0,1:T(8,128)(2,1)} %fusion.21, bf16[768,512]{0,1:T(8,128)(2,1)S(1)} %copy-done.12, f32[512]{0:T(512)S(1)} %copy-done.16), kind=kOutput, calls=%fused_computation.48 | convolution fusion | flops 6423149568 | bytes 12269056 | tf_op jit(solution)/shard_map/dot_general | solution.py:90
  157.2 2.0 %reshape.79 = f32[24,8,2,2,4,128]{5,4,3,2,1,0:T(4,128)S(1)} reshape(f32[768,512]{1,0:T(8,128)} %fusion.27) | data formatting | bytes 3145728 | tf_op jit(solution)/shard_map/convert_element_type | solution.py:157
  163.6 8.4 %fusion.5 = f32[4,24,8,4,4,128]{5,3,4,2,1,0:T(4,128)} fusion(f32[4,24,8,4,4,128]{5,3,4,2,1,0:T(4,128)S(1)} %bitcast.49, f32[5,24,8,4,4,128]{5,3,4,2,1,0:T(4,128)} %pad_maximum_fusion, f32[4,24,8,4,4,128]{5,4,3,2,1,0:T(4,128)S(1)} %bitcast.44, f32[24,8,4,4,128]{4,2,3,1,0:T(4,128)S(1)} %copy-done.10), kind=kLoop, calls=%fused_computation.10 | loop fusion | flops 6291456 | bytes 26738688 | tf_op jit(solution)/shard_map/add | solution.py:157
  172.0 8.7 %copy.41 = f32[4,24,8,4,4,128]{5,4,3,2,1,0:T(4,128)} copy(f32[4,24,8,4,4,128]{5,3,4,2,1,0:T(4,128)} %fusion.5) | data formatting | bytes 12582912 | tf_op jit(solution)/shard_map/add | solution.py:157
  (68 shorter events, 19.5 us)
Async XLA Ops:
  0.0 145.4 %copy-start = (bf16[2048,512]{1,0:T(8,128)(2,1)S(1)}, bf16[2048,512]{1,0:T(8,128)(2,1)}, u32[]{:S(2)}) copy-start(bf16[2048,512]{1,0:T(8,128)(2,1)} %param.16) | copy-start | bytes 6291460
  0.9 6.3 %copy-start.2 = (f32[4,24,8,4,4,128]{5,4,3,2,1,0:T(4,128)S(1)}, f32[4,24,8,4,4,128]{5,4,3,2,1,0:T(4,128)}, u32[]{:S(2)}) copy-start(f32[4,24,8,4,4,128]{5,4,3,2,1,0:T(4,128)} %param.10) | copy-start | bytes 18874372
  42.3 8.0 %copy-start.3 = (f32[4,24,8,4,4,128]{5,3,4,2,1,0:T(4,128)}, f32[4,24,8,4,4,128]{5,3,4,2,1,0:T(4,128)S(1)}, u32[]{:S(2)}) copy-start(f32[4,24,8,4,4,128]{5,3,4,2,1,0:T(4,128)S(1)} %fusion.8) | copy-start | bytes 18874372
  50.4 1.9 %copy-start.7 = (bf16[5,24,8,1,4,128]{5,3,4,2,1,0:T(2,128)(2,1)}, bf16[5,24,8,1,4,128]{5,3,4,2,1,0:T(2,128)(2,1)S(1)}, u32[]{:S(2)}) copy-start(bf16[5,24,8,1,4,128]{5,3,4,2,1,0:T(2,128)(2,1)S(1)} %get-tuple-element.13) | copy-start | bytes 2949124
  52.3 37.9 %collective-permute-start = (bf16[5,1,8,2,4,128]{5,3,4,2,1,0:T(2,128)(2,1)S(1)}, bf16[5,1,8,2,4,128]{5,3,4,2,1,0:T(2,128)(2,1)S(1)}, u32[]{:S(2)}, u32[]{:S(2)}) collective-permute-start(bf16[5,1,8,2,4,128]{5,3,4,2,1,0:T(2,128)(2,1)S(1)} %get-tuple-element.19), channel_id=1, source_target_pairs={{0,4},{4,8},{8,12},{12,16},{16,20},{20,24},{24,28},{28,0},{1,5},{5... | collective-permute-start | bytes 245768 | tf_op jit(solution)/shard_map/ppermute | solution.py:17
  55.3 34.9 %collective-permute-start.1 = (bf16[5,1,8,2,4,128]{5,3,4,2,1,0:T(2,128)(2,1)S(1)}, bf16[5,1,8,2,4,128]{5,3,4,2,1,0:T(2,128)(2,1)S(1)}, u32[]{:S(2)}, u32[]{:S(2)}) collective-permute-start(bf16[5,1,8,2,4,128]{5,3,4,2,1,0:T(2,128)(2,1)S(1)} %get-tuple-element.20), channel_id=1, source_target_pairs={{4,0},{8,4},{12,8},{16,12},{20,16},{24,20},{28,24},{0,28},{5,1},{9... | collective-permute-start | bytes 245768 | tf_op jit(solution)/shard_map/ppermute | solution.py:19
  63.0 76.4 %all-to-all-start = ((bf16[32,48,1013]{2,1,0:T(8,128)(2,1)}), bf16[32,48,1013]{2,1,0:T(8,128)(2,1)}, u32[]{:S(2)}, u32[]{:S(2)}) async-start(bf16[32,48,1013]{2,1,0:T(8,128)(2,1)} %bitcast.50), calls=%async_computation | async-start | bytes 6291456 | tf_op jit(solution)/shard_map/all_to_all | solution.py:96
  90.2 20.9 %slice-start.2 = ((s8[6291456]{0:T(1024)(128)(4,1)}), s8[4194304]{0:T(1024)(128)(4,1)S(1)}, s32[]{:S(2)}) async-start(s8[6291456]{0:T(1024)(128)(4,1)} %bitcast.45), calls=%async_computation.3 | async-start | bytes 8388608
  90.2 20.9 %slice-start.3 = ((s8[6291456]{0:T(1024)(128)(4,1)}), s8[2097152]{0:T(1024)(128)(4,1)S(1)}, s32[]{:S(2)}) async-start(s8[6291456]{0:T(1024)(128)(4,1)} %bitcast.45), calls=%async_computation.4 | async-start | bytes 4194304
  90.2 20.9 %copy-start.8 = (f32[1,24,8,4,4,128]{5,3,4,2,1,0:T(4,128)S(1)}, f32[1,24,8,4,4,128]{5,3,4,2,1,0:T(4,128)}, u32[]{:S(2)}) copy-start(f32[1,24,8,4,4,128]{5,3,4,2,1,0:T(4,128)} %fusion.47) | copy-start | bytes 4718596
  116.7 6.5 %copy-start.4 = (f32[5,24,8,4,4,128]{5,3,4,2,1,0:T(4,128)}, f32[5,24,8,4,4,128]{5,3,4,2,1,0:T(4,128)S(1)}, u32[]{:S(2)}) copy-start(f32[5,24,8,4,4,128]{5,3,4,2,1,0:T(4,128)S(1)} %fusion.1) | copy-start | bytes 23592964
  117.4 3.8 %copy-start.9 = (bf16[5,24,8,4,1,128]{5,3,4,2,1,0:T(4,128)(2,1)}, bf16[5,24,8,4,1,128]{5,3,4,2,1,0:T(4,128)(2,1)S(1)}, u32[]{:S(2)}) copy-start(bf16[5,24,8,4,1,128]{5,3,4,2,1,0:T(4,128)(2,1)S(1)} %get-tuple-element.12) | copy-start | bytes 2949124
  117.4 2.9 %copy-start.11 = (f32[4,24,8,2,2,128]{5,3,4,2,1,0:T(2,128)S(1)}, f32[4,24,8,2,2,128]{5,3,4,2,1,0:T(2,128)}, u32[]{:S(2)}) copy-start(f32[4,24,8,2,2,128]{5,3,4,2,1,0:T(2,128)} %reduce_sum.27) | copy-start | bytes 4718596
  118.6 10.5 %collective-permute-start.2 = (bf16[5,24,1,4,2,128]{5,3,4,2,1,0:T(4,128)(2,1)}, bf16[5,24,1,4,2,128]{5,3,4,2,1,0:T(4,128)(2,1)}, u32[]{:S(2)}, u32[]{:S(2)}) collective-permute-start(bf16[5,24,1,4,2,128]{5,3,4,2,1,0:T(4,128)(2,1)} %get-tuple-element.21), channel_id=1, source_target_pairs={{0,1},{1,2},{2,3},{3,0},{4,5},{5,6},{6,7},{7,4},{8,9},{9,10},{10,1... | collective-permute-start | bytes 737288 | tf_op jit(solution)/shard_map/ppermute | solution.py:17
  118.8 10.2 %collective-permute-start.3 = (bf16[5,24,1,4,2,128]{5,3,4,2,1,0:T(4,128)(2,1)}, bf16[5,24,1,4,2,128]{5,3,4,2,1,0:T(4,128)(2,1)}, u32[]{:S(2)}, u32[]{:S(2)}) collective-permute-start(bf16[5,24,1,4,2,128]{5,3,4,2,1,0:T(4,128)(2,1)} %get-tuple-element.22), channel_id=1, source_target_pairs={{1,0},{2,1},{3,2},{0,3},{5,4},{6,5},{7,6},{4,7},{9,8},{10,9},{11,1... | collective-permute-start | bytes 737288 | tf_op jit(solution)/shard_map/ppermute | solution.py:19
  122.2 3.3 %copy-start.13 = (s32[768,1]{0,1:T(1,128)S(1)}, s32[768,1]{0,1:T(1,128)}, u32[]{:S(2)}) copy-start(s32[768,1]{0,1:T(1,128)} %param.13) | copy-start | bytes 9220
  126.0 4.4 %copy-start.5 = (f32[5,24,8,4,4,128]{5,3,4,2,1,0:T(4,128)S(1)}, f32[5,24,8,4,4,128]{5,3,4,2,1,0:T(4,128)}, u32[]{:S(2)}) copy-start(f32[5,24,8,4,4,128]{5,3,4,2,1,0:T(4,128)} %copy-done.4) | copy-start | bytes 23592964
  139.4 6.1 %copy-start.12 = (bf16[768,512]{0,1:T(8,128)(2,1)S(1)}, bf16[768,512]{0,1:T(8,128)(2,1)}, u32[]{:S(2)}) copy-start(bf16[768,512]{0,1:T(8,128)(2,1)} %copy.39) | copy-start | bytes 2359300
  139.4 6.1 %copy-start.15 = (f32[2048]{0:T(1024)S(1)}, f32[2048]{0:T(1024)}, u32[]{:S(2)}) copy-start(f32[2048]{0:T(1024)} %param.15) | copy-start | bytes 24580
  139.4 6.1 %copy-start.16 = (f32[512]{0:T(512)S(1)}, f32[512]{0:T(512)}, u32[]{:S(2)}) copy-start(f32[512]{0:T(512)} %param.17) | copy-start | bytes 6148
  160.1 2.2 %slice-start = ((s8[6291456]{0:T(1024)(128)(4,1)}), s8[4194304]{0:T(1024)(128)(4,1)S(1)}, s32[]{:S(2)}) async-start(s8[6291456]{0:T(1024)(128)(4,1)} %bitcast.43), calls=%async_computation.1 | async-start | bytes 8388608
  161.3 1.9 %slice-start.1 = ((s8[6291456]{0:T(1024)(128)(4,1)}), s8[2097152]{0:T(1024)(128)(4,1)S(1)}, s32[]{:S(2)}) async-start(s8[6291456]{0:T(1024)(128)(4,1)} %bitcast.43), calls=%async_computation.2 | async-start | bytes 4194304
  161.3 2.3 %copy-start.10 = (f32[24,8,4,4,128]{4,2,3,1,0:T(4,128)S(1)}, f32[24,8,4,4,128]{4,2,3,1,0:T(4,128)}, u32[]{:S(2)}) copy-start(f32[24,8,4,4,128]{4,2,3,1,0:T(4,128)} %maximum_bitcast_fusion) | copy-start | bytes 4718596
  172.0 8.7 %copy-start.1 = (bf16[2048,512]{1,0:T(8,128)(2,1)S(1)}, bf16[2048,512]{1,0:T(8,128)(2,1)}, u32[]{:S(2)}) copy-start(bf16[2048,512]{1,0:T(8,128)(2,1)} %param.16) | copy-start | bytes 6291460
  (2 other events, 3.0 us)
where the time goes:
time: 184 us; the launch traced here: 181 us
  other arithmetic  84.6 us (46%)
  matrix products  49 us (27%)
  local copies, waits for them, and re-layouts  34.8 us (19%)
  starting transfers between devices  11.9 us (6%)
    add x1, other arithmetic, shards(): stacked[:, :, :, 0] + padded[:, :-2, :, 1]  20.9 us
    dot_general x1, matrix products, advect(): jnp.einsum('ik,fabkjl->fabijl', derivative, prognostic, precision=lax.Pre...  17.5 us
    dot_general x1, matrix products, advect(): jnp.einsum('jk,fabikl->fabijl', derivative, prognostic, precision=lax.Pre...  13.4 us
    dot_general x1, matrix products, apply_network(): jnp.dot(hidden, weight_out, preferred_element_type=jnp.float32) + bias_out  11.8 us
    reduce_sum x1, other arithmetic, cell_average(): weighted_sum = jnp.sum(weighted, axis=(4, 6))  11 us
    unnamed x44, local copies, waits for them, and re-layouts  9.87 us
    mul x1, other arithmetic, cell_average(): prognostic * node_weight[None]  9.15 us
    add x1, local copies, waits for them, and re-layouts, shards(): return section + spread_cells(back.astype(jnp.float32))  8.67 us
  transfers between devices with their start and end apart: 5, of which 0 were waited for; matrix products, arithmetic and copies ran while one was open for 41% of the time, Pallas kernels for 0%

commit v1 on v0

v1 whole, which is shorter than its diff:
```python
import jax
import jax.numpy as jnp
import numpy as np
from jax import lax
from jax.experimental import pallas as pl
from jax.experimental.pallas import tpu as pltpu
from jax.sharding import PartitionSpec as P

section_step = 0.1
AXES = ("curve", "sub")
F32 = jnp.float32
BF16 = jnp.bfloat16


def node_tables():
    nodes = np.array([-1.0, -1.0 / np.sqrt(5.0), 1.0 / np.sqrt(5.0), 1.0])
    quadrature = np.array([1.0 / 6.0, 5.0 / 6.0, 5.0 / 6.0, 1.0 / 6.0])
    products = np.array(
        [np.prod([nodes[i] - nodes[k] for k in range(4) if k != i]) for i in range(4)]
    )
    derivative = np.zeros((4, 4))
    for i in range(4):
        for k in range(4):
            if i != k:
                derivative[i, k] = products[i] / (products[k] * (nodes[i] - nodes[k]))
            else:
                derivative[i, i] = sum(1.0 / (nodes[i] - nodes[m]) for m in range(4) if m != i)
    return derivative.astype(np.float32), quadrature.astype(np.float32)


def row_tables():
    d, w = node_tables()
    s = np.arange(8)
    i, j = s // 4, s % 4
    tables = []
    for half in (0, 2):
        for column in (i, 1 - i, 2 + i, 3 - i):
            tables.append(-d[half + i, column])
    for shift in range(4):
        tables.append(-d[j, (j - shift) % 4])
    for half in (0, 2):
        tables.append(w[half + i] * w[j])
    return np.repeat(np.stack(tables)[:, :, None], 128, axis=2).astype(np.float32)


def lane_rows(x):
    return lax.broadcasted_iota(jnp.int32, x, len(x) - 2)


def roll(x, shift):
    return pltpu.roll(x, shift % 8, axis=1)


def turn_body(x_ref, o_ref):
    n = x_ref.shape[1]
    width = x_ref.shape[0]
    eye = (
        lax.broadcasted_iota(jnp.int32, (n, n), 0) == lax.broadcasted_iota(jnp.int32, (n, n), 1)
    ).astype(BF16)
    y = lax.dot_general(eye, x_ref[...], (((1,), (1,)), ((), ())), preferred_element_type=F32)
    o_ref[:, :width] = y.astype(BF16)
    o_ref[:, width:] = jnp.zeros((n, o_ref.shape[1] - width), BF16)


def turn(aux_t, padded):
    width, rows = aux_t.shape
    block = 256
    return pl.pallas_call(
        turn_body,
        grid=(rows // block,),
        in_specs=[pl.BlockSpec((width, block), lambda i: (0, i))],
        out_specs=pl.BlockSpec((block, padded), lambda i: (i, 0)),
        out_shape=jax.ShapeDtypeStruct((rows, padded), BF16),
        name="turn",
    )(aux_t)


def tend_body(x_ref, m_ref, t_ref, pick_ref, o_ref, c_ref):
    fields = x_ref.shape[0]
    rows = x_ref.shape[1]
    group = 128
    sub = lax.broadcasted_iota(jnp.int32, (group // 16, 8, 128), 1) % 4
    tab = [t_ref[k][None] for k in range(14)]

    def step(g, carry):
        at = pl.multiple_of(g * group, group)

        def halves(v):
            v = v.reshape(group // 16, 2, 8, 128)
            return v[:, 0], v[:, 1]

        def keep(f, y0, y1):
            o_ref[f, pl.ds(at, group), :] = jnp.stack([y0, y1], axis=1).reshape(group, 128)

        m0, m1 = halves(m_ref[pl.ds(at, group), :])
        w = (m0 * tab[12], m1 * tab[13])

        def pool(v):
            v = v + roll(v, 4)
            return v + roll(v, 7)

        inv = [1.0 / pool(v) for v in w]
        u = halves(x_ref[0, pl.ds(at, group), :])
        v = halves(x_ref[1, pl.ds(at, group), :])
        uw = (u[0] * w[0], u[1] * w[1])
        vw = (v[0] * w[0], v[1] * w[1])
        for f in range(fields):
            x = u if f == 0 else v if f == 1 else halves(x_ref[f, pl.ds(at, group), :])
            r4 = (roll(x[0], 4), roll(x[1], 4))
            out = []
            means = []
            for h in range(2):
                da = (
                    tab[4 * h] * x[0]
                    + tab[4 * h + 1] * r4[0]
                    + tab[4 * h + 2] * x[1]
                    + tab[4 * h + 3] * r4[1]
                )
                db = tab[8] * x[h]
                for k in (1, 2, 3):
                    turned = jnp.where(sub >= k, roll(x[h], k), roll(r4[h], k))
                    db = db + tab[8 + k] * turned
                out.append(uw[h] * da + vw[h] * db)
                means.append(pool(x[h] * w[h]) * inv[h])
            keep(f, out[0], out[1])
            means = jnp.stack(means, axis=1).reshape(group, 128).astype(BF16)
            c_ref[pl.ds(pl.multiple_of(g * (group // 4), group // 4), group // 4), f * 128 : (f + 1) * 128] = jnp.dot(
                pick_ref[...], means, preferred_element_type=F32
            ).astype(BF16)
        return carry

    lax.fori_loop(0, rows // group, step, 0)


def pick_table(group):
    rows = np.arange(group)
    pick = np.zeros((group // 4, group), np.float32)
    for c in range(group // 4):
        element, p, q = c // 4, (c // 2) % 2, c % 2
        pick[c, element * 16 + p * 8 + q * 2] = 1.0
    return pick


def tendencies(x, mass):
    fields, rows, levels = x.shape
    block = 384
    return pl.pallas_call(
        tend_body,
        grid=(rows // block,),
        in_specs=[
            pl.BlockSpec((fields, block, levels), lambda i: (0, i, 0)),
            pl.BlockSpec((block, levels), lambda i: (i, 0)),
            pl.BlockSpec((14, 8, 128), lambda i: (0, 0, 0)),
            pl.BlockSpec((32, 128), lambda i: (0, 0)),
        ],
        out_specs=[
            pl.BlockSpec((fields, block, levels), lambda i: (0, i, 0)),
            pl.BlockSpec((block // 4, fields * levels), lambda i: (i, 0)),
        ],
        out_shape=[
            jax.ShapeDtypeStruct((fields, rows, levels), F32),
            jax.ShapeDtypeStruct((rows // 4, fields * levels), BF16),
        ],
        name="tendencies",
    )(x, mass, jnp.asarray(row_tables()), jnp.asarray(pick_table(128), BF16))


def section_body(t_ref, x_ref, m_ref, q_ref, top_ref, bottom_ref, left_ref, right_ref, o_ref, inv_ref):
    rows = x_ref.shape[1]
    per = top_ref.shape[1] // 8
    span = per * 16
    count = rows // span
    s = lax.broadcasted_iota(jnp.int32, (per, 8, 128), 1)
    low = s < 4
    first = s % 4 == 0
    last = s % 4 == 3
    zero = jnp.zeros((1, 8, 128), F32)
    f = pl.program_id(0)

    def halves(v):
        v = v.reshape(per, 2, 8, 128)
        return v[:, 0], v[:, 1]

    def sums(a, load, k):
        here = load(a)
        above = load(jnp.maximum(a - 1, 0))[1]
        below = load(jnp.minimum(a + 1, count - 1))[0]
        top = top_ref[k].reshape(per, 8, 128)
        bottom = bottom_ref[k].reshape(per, 8, 128)
        add0 = jnp.where(a == 0, top, jnp.where(low, roll(above, 4), 0.0))
        add1 = jnp.where(a == count - 1, bottom, jnp.where(low, 0.0, roll(below, 4)))
        at = pl.multiple_of(a * 16, 16)
        left = halves_one(left_ref[k, pl.ds(at, 16), :])
        right = halves_one(right_ref[k, pl.ds(at, 16), :])
        result = []
        for h, p in enumerate((here[0] + add0, here[1] + add1)):
            up = jnp.where(last, roll(p, 3), 0.0)
            down = jnp.where(first, roll(p, 5), 0.0)
            up = jnp.concatenate([up_shift(up), right[h]], axis=0)
            down = jnp.concatenate([left[h], down[:-1]], axis=0)
            result.append(p + up + down)
        return result

    def halves_one(v):
        v = v.reshape(1, 2, 8, 128)
        return v[:, 0], v[:, 1]

    def up_shift(v):
        return v[1:]

    def window(a):
        return pl.ds(pl.multiple_of(a * span, span), span)

    def mass_at(a):
        m0, m1 = halves(m_ref[window(a), :])
        return m0 * q_ref[0][None], m1 * q_ref[1][None]

    @pl.when(f == 0)
    def _():
        def step(a, carry):
            w0, w1 = sums(a, mass_at, 4)
            inv_ref[window(a), :] = jnp.stack(
                [section_step / w0, section_step / w1], axis=1
            ).reshape(span, 128)
            return carry

        lax.fori_loop(0, count, step, 0)

    def step(a, carry):
        y0, y1 = sums(a, lambda b: halves(t_ref[0, window(b), :]), f)
        y = jnp.stack([y0, y1], axis=1).reshape(span, 128)
        o_ref[0, window(a), :] = x_ref[0, window(a), :] + y * inv_ref[window(a), :]
        return carry

    lax.fori_loop(0, count, step, 0)


def section_of(t, x, mass, top, bottom, left, right):
    fields, rows, levels = x.shape
    whole = lambda a: pl.BlockSpec(a.shape, lambda f: (0,) * a.ndim)
    quad = jnp.asarray(row_tables()[12:14])
    one = pl.BlockSpec((1, rows, levels), lambda f: (f, 0, 0))
    return pl.pallas_call(
        section_body,
        grid=(fields,),
        in_specs=[one, one] + [whole(a) for a in (mass, quad, top, bottom, left, right)],
        out_specs=one,
        out_shape=jax.ShapeDtypeStruct(x.shape, F32),
        scratch_shapes=[pltpu.VMEM((rows, levels), F32)],
        name="section",
    )(t, x, mass, quad, top, bottom, left, right)


def places_body(owner_ref, o_ref, *, devices, capacity):
    cols = owner_ref.shape[0]
    owner = owner_ref[...]
    hits = owner == lax.broadcasted_iota(jnp.int32, (cols, devices), 1)
    hits = jnp.where(hits, 1.0, 0.0)
    before = lax.broadcasted_iota(jnp.int32, (cols, cols), 0) > lax.broadcasted_iota(
        jnp.int32, (cols, cols), 1
    )
    before = jnp.where(before, 1.0, 0.0).astype(BF16)
    earlier = jnp.dot(before, hits.astype(BF16), preferred_element_type=F32)
    slot = jnp.sum(hits * earlier, axis=1, keepdims=True).astype(jnp.int32)
    place = owner * capacity + slot
    wide = lax.broadcasted_iota(jnp.int32, (cols, devices * capacity), 1)
    o_ref[...] = jnp.where(place == wide, 1.0, 0.0).astype(BF16)


def places(owner, devices, capacity):
    return pl.pallas_call(
        lambda a, o: places_body(a, o, devices=devices, capacity=capacity),
        out_shape=jax.ShapeDtypeStruct((owner.shape[0], devices * capacity), BF16),
        name="places",
    )(owner)


def first_body(s_ref, w_ref, b_ref, o_ref):
    o_ref[...] = jnp.dot(s_ref[...], w_ref[...], preferred_element_type=F32) + b_ref[...]


def first_part(state, weight, bias):
    cols, width = state.shape
    hidden = weight.shape[1]
    block = 512
    return pl.pallas_call(
        first_body,
        grid=(hidden // block,),
        in_specs=[
            pl.BlockSpec((cols, width), lambda i: (0, 0)),
            pl.BlockSpec((width, block), lambda i: (0, i)),
            pl.BlockSpec((1, block), lambda i: (0, i)),
        ],
        out_specs=pl.BlockSpec((cols, block), lambda i: (0, i)),
        out_shape=jax.ShapeDtypeStruct((cols, hidden), F32),
        name="first_part",
    )(state, weight, bias)


def finish_body(sel_ref, aux_ref, w_ref, part_ref, wo_ref, bo_ref, spread_ref, x_ref, o_ref):
    fields = x_ref.shape[0]
    levels = x_ref.shape[2]
    aux = jnp.dot(sel_ref[...], aux_ref[...], preferred_element_type=F32).astype(BF16)
    v = part_ref[...] + jnp.dot(aux, w_ref[...], preferred_element_type=F32)
    hidden = (v / (1.0 + jnp.exp(-v))).astype(BF16)
    inc = jnp.dot(hidden, wo_ref[...], preferred_element_type=F32) + bo_ref[...]
    inc = inc.astype(BF16)
    group = spread_ref.shape[1]
    for g in range(inc.shape[0] // group):
        wide = jnp.dot(
            spread_ref[...], inc[g * group : (g + 1) * group], preferred_element_type=F32
        )
        at = pl.ds(g * group * 4, group * 4)
        for f in range(fields):
            o_ref[f, at, :] = x_ref[f, at, :] + wide[:, f * levels : (f + 1) * levels]


def spread_table(group):
    spread = np.zeros((group * 4, group), np.float32)
    for r in range(group * 4):
        e, i, j = r // 16, (r // 4) % 4, r % 4
        spread[r, e * 4 + (i // 2) * 2 + j // 2] = 1.0
    return spread


def finish(sel, aux, weight, part, weight_out, bias_out, x):
    cols, slots = sel.shape
    fields, rows, levels = x.shape
    block = 256
    spread = jnp.asarray(spread_table(128), BF16)
    whole = lambda a: pl.BlockSpec(a.shape, lambda i: (0,) * a.ndim)
    return pl.pallas_call(
        finish_body,
        grid=(cols // block,),
        in_specs=[
            pl.BlockSpec((block, slots), lambda i: (i, 0)),
            whole(aux),
            whole(weight),
            pl.BlockSpec((block, weight.shape[1]), lambda i: (i, 0)),
            whole(weight_out),
            whole(bias_out),
            whole(spread),
            pl.BlockSpec((fields, block * 4, levels), lambda i: (0, i, 0)),
        ],
        out_specs=pl.BlockSpec((fields, block * 4, levels), lambda i: (0, i, 0)),
        out_shape=jax.ShapeDtypeStruct(x.shape, F32),
        name="finish",
    )(sel, aux, weight, part, weight_out, bias_out, spread, x)


def shards(
    prognostic, layer_mass, column_aux, group_owner, weight_in, bias_in, weight_out, bias_out
):
    fields, rows_a, rows_b, _, _, levels = prognostic.shape
    n_curve, n_sub = lax.axis_size("curve"), lax.axis_size("sub")
    devices = n_curve * n_sub
    capacity = column_aux.shape[0] // devices
    aux_width = column_aux.shape[1]
    padded = -(-aux_width // 128) * 128
    state_width = fields * levels
    rows = rows_a * rows_b * 16

    home = turn(column_aux.T, padded).reshape(devices, capacity, padded)
    home = lax.all_to_all(home, AXES, split_axis=0, concat_axis=0, tiled=True)
    home = home.reshape(devices * capacity, padded)

    x = prognostic.reshape(fields, rows, levels)
    mass = layer_mass.reshape(rows, levels)
    tend, state = tendencies(x, mass)

    quadrature = node_tables()[1]
    def ahead(n):
        return [(i, (i + 1) % n) for i in range(n)]
    def back(n):
        return [((i + 1) % n, i) for i in range(n)]

    t6 = tend.reshape(fields, rows_a, rows_b, 4, 4, levels)
    w_edge = (quadrature[0] * quadrature)[:, None]
    head = jnp.concatenate([t6[:, 0, :, 0], (layer_mass[0, :, 0] * w_edge)[None]], axis=0)
    tail = jnp.concatenate([t6[:, -1, :, 3], (layer_mass[-1, :, 3] * w_edge)[None]], axis=0)
    above = lax.ppermute(tail.astype(BF16), "curve", ahead(n_curve)).astype(F32)
    below = lax.ppermute(head.astype(BF16), "curve", back(n_curve)).astype(F32)
    top = jnp.pad(above, ((0, 0), (0, 0), (0, 4), (0, 0))).reshape(fields + 1, rows_b * 8, levels)
    bottom = jnp.pad(below, ((0, 0), (0, 0), (4, 0), (0, 0))).reshape(fields + 1, rows_b * 8, levels)

    def edge(b, j):
        e = jnp.concatenate(
            [t6[:, :, b, :, j], (layer_mass[:, b, :, j] * (quadrature[j] * quadrature)[:, None])[None]],
            axis=0,
        )
        before = jnp.concatenate([above[:, None, b, j], e[:, :-1, 3]], axis=1)
        after = jnp.concatenate([e[:, 1:, 0], below[:, None, b, j]], axis=1)
        return jnp.stack([e[:, :, 0] + before, e[:, :, 1], e[:, :, 2], e[:, :, 3] + after], axis=2)

    right_out = edge(rows_b - 1, 3)
    left_out = edge(0, 0)
    left = lax.ppermute(right_out.astype(BF16), "sub", ahead(n_sub)).astype(F32)
    right = lax.ppermute(left_out.astype(BF16), "sub", back(n_sub)).astype(F32)
    left = jnp.pad(left[:, :, :, None], ((0, 0), (0, 0), (0, 0), (0, 3), (0, 0)))
    right = jnp.pad(right[:, :, :, None], ((0, 0), (0, 0), (0, 0), (3, 0), (0, 0)))
    left = left.reshape(fields + 1, rows_a * 16, levels)
    right = right.reshape(fields + 1, rows_a * 16, levels)
    section = section_of(tend, x, mass, top, bottom, left, right)

    sel = places(group_owner, devices, capacity)
    part = first_part(state, weight_in[:state_width], bias_in[None])
    weight_aux = jnp.pad(weight_in[state_width:], ((0, padded - aux_width), (0, 0)))
    out = finish(sel, home, weight_aux, part, weight_out, bias_out[None], section)
    return out.reshape(prognostic.shape)


def solution(mesh):
    return jax.shard_map(
        shards,
        mesh=mesh,
        in_specs=(
            P(None, "curve", "sub", None, None, None),
            P("curve", "sub", None, None, None),
            P(("curve", "sub"), None),
            P(("curve", "sub"), None),
            P(),
            P(),
            P(),
            P(),
        ),
        out_specs=P(None, "curve", "sub", None, None, None),
        check_vma=False,
    )
```

time: 184 us -> 127 us (0.69)
  the two profiles are of different devices: /device:TPU:0 before, /device:TPU:16 now
where the time goes in v1:
time: 127 us; the launch traced here: 125 us
  Pallas kernels  56.1 us (44%)
  local copies, waits for them, and re-layouts  27 us (21%)
  waiting for transfers between devices  23.8 us (19%)
  starting transfers between devices  10.7 us (8%)
  other arithmetic  7.59 us (6%)
    ppermute x1, waiting for transfers between devices, shards(): above = lax.ppermute(tail.astype(BF16), 'curve', ahead(n_curve)).astype(F32)  22.3 us
    pallas_call x1, Pallas kernels, finish(): pl.pallas_call(finish_body, grid=(cols // block,), in_specs=[pl.BlockSpec...  16.2 us
    pallas_call x1, Pallas kernels, tendencies(): pl.pallas_call(tend_body, grid=(rows // block,), in_specs=[pl.BlockSpec((...  13.1 us
    pallas_call x1, Pallas kernels, section_of(): pl.pallas_call(section_body, grid=(fields,), in_specs=[one, one] + [whole...  10.8 us
    pallas_call x1, Pallas kernels, first_part(): pl.pallas_call(first_body, grid=(hidden // block,), in_specs=[pl.BlockSpe...  6.16 us
    pallas_call x1, Pallas kernels, turn(): pl.pallas_call(turn_body, grid=(rows // block,), in_specs=[pl.BlockSpec((...  5.98 us
    all_to_all x1, starting transfers between devices, shards(): home = lax.all_to_all(home, AXES, split_axis=0, concat_axis=0, tiled=True)  5.94 us
    reshape x1, local copies, waits for them, and re-layouts, shards(): t6 = tend.reshape(fields, rows_a, rows_b, 4, 4, levels)  5.45 us
  transfers between devices with their start and end apart: 5, of which 2 were waited for; matrix products, arithmetic and copies ran while one was open for 26% of the time, Pallas kernels for 27%

profile of v1, /device:TPU:16, one launch (start us, length us, event | category | flops | bytes accessed | tf_op | source)
XLA Modules:
  0.0 125.4 jit_solution(6401126250651349434)
XLA Ops:
  0.0 6.0 %turn.1 = bf16[1536,1024]{1,0:T(8,128)(2,1)} custom-call(bf16[1013,1536]{1,0:T(8,128)(2,1)} %bitcast.57), custom_call_target="tpu_custom_call" | custom-call | tf_op jit(solution)/shard_map/turn/pallas_call | solution.py:68
  6.0 5.9 %all-to-all-start = ((bf16[32,48,1024]{2,1,0:T(8,128)(2,1)}), bf16[32,48,1024]{2,1,0:T(8,128)(2,1)S(1)}, u32[]{:S(2)}, u32[]{:S(2)}) async-start(bf16[32,48,1024]{2,1,0:T(8,128)(2,1)} %bitcast.50), calls=%async_computation | async-start | bytes 6291456 | tf_op jit(solution)/shard_map/all_to_all | solution.py:364
  11.9 13.1 %tendencies.1 = (f32[4,3072,128]{2,1,0:T(8,128)}, bf16[768,512]{1,0:T(8,128)(2,1)}) custom-call(f32[4,3072,128]{2,1,0:T(8,128)} %bitcast.47, f32[3072,128]{1,0:T(8,128)} %bitcast.51, f32[14,8,128]{2,1,0:T(8,128)} %constant.16.clone.t_ref, bf16[32,128]{1,0:T(8,128)(2,1)} %constant.17.clone.pick_ref), custom_call_target="tpu_custom_call" | custom-call | tf_op jit(solution)/shard_map/tendencies/pallas_call | solution.py:147
  25.0 5.4 %copy.61 = bf16[4,24,8,4,4,128]{5,2,4,0,3,1:T(8,128)(2,1)S(1)} copy(f32[4,24,8,4,4,128]{5,4,3,2,1,0:T(4,128)} %bitcast.45) | data formatting | bytes 9437184 | tf_op jit(solution)/shard_map/reshape | solution.py:377
  31.9 1.5 %collective-permute-start = (bf16[5,8,4,128]{3,1,2,0:T(8,128)(2,1)}, bf16[5,8,4,128]{3,1,2,0:T(8,128)(2,1)}, u32[]{:S(2)}, u32[]{:S(2)}) collective-permute-start(bf16[5,8,4,128]{3,1,2,0:T(8,128)(2,1)} %pad_maximum_fusion.4), channel_id=1, source_target_pairs={{0,4},{4,8},{8,12},{12,16},{16,20},{20,24},{24,28},{28,0},{1,5},{5... | collective-permute-start | bytes 122888 | tf_op jit(solution)/shard_map/ppermute | solution.py:381
  34.0 1.4 %collective-permute-start.1 = (bf16[5,8,4,128]{3,1,2,0:T(8,128)(2,1)}, bf16[5,8,4,128]{3,1,2,0:T(8,128)(2,1)}, u32[]{:S(2)}, u32[]{:S(2)}) collective-permute-start(bf16[5,8,4,128]{3,1,2,0:T(8,128)(2,1)} %pad_maximum_fusion.5), channel_id=1, source_target_pairs={{4,0},{8,4},{12,8},{16,12},{20,16},{24,20},{28,24},{0,28},{5,1},{9... | collective-permute-start | bytes 122888 | tf_op jit(solution)/shard_map/ppermute | solution.py:382
  35.5 1.1 fusion.27
  36.7 1.8 %fusion.26 = (f32[4,24,1,4,1,128]{5,4,3,2,1,0:T(1,128)S(1)}, f32[4,24,1,4,1,128]{5,4,3,2,1,0:T(1,128)S(1)}) fusion(f32[4,24,8,4,4,128]{5,4,3,2,1,0:T(4,128)} %bitcast.46), kind=kLoop, calls=%fused_computation.61 | loop fusion | bytes 786432 | tf_op jit(solution)/shard_map/slice | solution.py:388
  41.0 1.5 %slice.81.w_ref = bf16[512,2048]{1,0:T(8,128)(2,1)} slice(bf16[1525,2048]{1,0:T(8,128)(2,1)S(1)} %bitcast.54), slice={[0:512], [0:2048]} | slice | bytes 4194304 | tf_op jit(solution)/shard_map/slice | solution.py:406
  42.6 2.2 %slice.80 = bf16[1013,2048]{1,0:T(8,128)(2,1)} slice(bf16[1525,2048]{1,0:T(8,128)(2,1)S(1)} %bitcast.54), slice={[512:1525], [0:2048]} | slice | bytes 8298496 | tf_op jit(solution)/shard_map/slice | solution.py:407
  44.8 0.9 copy.22.a
  45.7 3.9 %places.1.sel_ref = bf16[768,1536]{1,0:T(8,128)(2,1)} custom-call(s32[768,1]{1,0:T(8,128)} %copy.22.a), custom_call_target="tpu_custom_call" | custom-call | tf_op jit(solution)/shard_map/places/pallas_call | solution.py:271
  49.7 4.7 %pad.22.w_ref = bf16[1024,2048]{1,0:T(8,128)(2,1)} pad(bf16[1013,2048]{1,0:T(8,128)(2,1)} %slice.80, bf16[]{:T(256)} %constant.14.clone.1), padding=0_11x0_0 | pad | bytes 8343554 | tf_op jit(solution)/shard_map/jit(_pad)/pad | solution.py:407
  54.4 6.2 %first_part.1.part_ref = f32[768,2048]{1,0:T(8,128)} custom-call(bf16[768,512]{1,0:T(8,128)(2,1)} %get-tuple-element.7.s_ref, bf16[512,2048]{1,0:T(8,128)(2,1)} %slice.81.w_ref, f32[1,2048]{1,0:T(1,128)} %bitcast.60), custom_call_target="tpu_custom_call" | custom-call | tf_op jit(solution)/shard_map/first_part/pallas_call | solution.py:286
  60.5 22.3 %collective-permute-done = bf16[5,8,4,128]{3,1,2,0:T(8,128)(2,1)} collective-permute-done((bf16[5,8,4,128]{3,1,2,0:T(8,128)(2,1)}, bf16[5,8,4,128]{3,1,2,0:T(8,128)(2,1)}, u32[]{:S(2)}, u32[]{:S(2)}) %collective-permute-start) | collective-permute-done | bytes 40992 | tf_op jit(solution)/shard_map/ppermute | solution.py:381
  84.3 0.9 fusion.9
  86.1 1.8 %collective-permute-start.3 = (bf16[5,24,4,128]{3,1,2,0:T(8,128)(2,1)S(1)}, bf16[5,24,4,128]{3,1,2,0:T(8,128)(2,1)S(1)}, u32[]{:S(2)}, u32[]{:S(2)}) collective-permute-start(bf16[5,24,4,128]{3,1,2,0:T(8,128)(2,1)S(1)} %pad_maximum_fusion.1), channel_id=1, source_target_pairs={{1,0},{2,1},{3,2},{0,3},{5,4},{6,5},{7,6},{4,7},{9,8},{10,9},{11,1... | collective-permute-start | bytes 368648 | tf_op jit(solution)/shard_map/ppermute | solution.py:398
  88.6 0.9 fusion.16
  92.7 1.2 copy.33
  93.9 1.5 %collective-permute-done.2 = bf16[5,24,4,128]{3,1,2,0:T(8,128)(2,1)S(1)} collective-permute-done((bf16[5,24,4,128]{3,1,2,0:T(8,128)(2,1)S(1)}, bf16[5,24,4,128]{3,1,2,0:T(8,128)(2,1)S(1)}, u32[]{:S(2)}, u32[]{:S(2)}) %collective-permute-start.2) | collective-permute-done | bytes 122912 | tf_op jit(solution)/shard_map/ppermute | solution.py:397
  95.6 1.2 copy.30
  96.8 10.8 %section.1.x_ref = f32[4,3072,128]{2,1,0:T(8,128)} custom-call(f32[4,3072,128]{2,1,0:T(8,128)} %get-tuple-element.8.t_ref, f32[4,3072,128]{2,1,0:T(8,128)} %bitcast.48, f32[3072,128]{1,0:T(8,128)} %bitcast.52, f32[2,8,128]{2,1,0:T(8,128)} %constant.19.clone.q_ref, f32[5,64,128]{2,1,0:T(8,128)} %pad_bitcast_fusion.1.top_ref, ...), custom_call_target="tpu_custom_call" | custom-call | tf_op jit(solution)/shard_map/section/pallas_call | solution.py:243
  107.6 1.6 %copy-done = bf16[32,48,1024]{2,1,0:T(8,128)(2,1)} copy-done((bf16[32,48,1024]{2,1,0:T(8,128)(2,1)}, bf16[32,48,1024]{2,1,0:T(8,128)(2,1)S(1)}, u32[]{:S(2)}) %copy-start) | copy-done | bytes 3145752
  109.2 16.2 %finish.1 = f32[4,3072,128]{2,1,0:T(8,128)} custom-call(bf16[768,1536]{1,0:T(8,128)(2,1)} %places.1.sel_ref, bf16[1536,1024]{1,0:T(8,128)(2,1)} %bitcast.49, bf16[1024,2048]{1,0:T(8,128)(2,1)} %pad.22.w_ref, f32[768,2048]{1,0:T(8,128)} %first_part.1.part_ref, bf16[2048,512]{1,0:T(8,128)(2,1)} %wo_ref.1, f32[1,512]{1,0:T(1,128)} %bitcast.61, ...), custom_call_target="tpu_custom_call" | custom-call | tf_op jit(solution)/shard_map/finish/pallas_call | solution.py:332
  (39 shorter events, 11.1 us)
Async XLA Ops:
  6.0 101.6 %all-to-all-start = ((bf16[32,48,1024]{2,1,0:T(8,128)(2,1)}), bf16[32,48,1024]{2,1,0:T(8,128)(2,1)S(1)}, u32[]{:S(2)}, u32[]{:S(2)}) async-start(bf16[32,48,1024]{2,1,0:T(8,128)(2,1)} %bitcast.50), calls=%async_computation | async-start | bytes 6291456 | tf_op jit(solution)/shard_map/all_to_all | solution.py:364
  25.0 16.0 %slice-start = ((s8[6258688]{0:T(1024)(128)(4,1)}), s8[4194304]{0:T(1024)(128)(4,1)S(1)}, s32[]{:S(2)}) async-start(s8[6258688]{0:T(1024)(128)(4,1)} %bitcast.53), calls=%async_computation.1 | async-start | bytes 8388608
  25.0 6.2 %copy-start.4 = (f32[4]{0:T(128)S(1)}, f32[4]{0:T(128)}, u32[]{:S(2)}) copy-start(f32[4]{0:T(128)} %constant.31) | copy-start | bytes 52
  25.0 16.0 %slice-start.1 = ((s8[6258688]{0:T(1024)(128)(4,1)}), s8[2064384]{0:T(1024)(128)(4,1)S(1)}, s32[]{:S(2)}) async-start(s8[6258688]{0:T(1024)(128)(4,1)} %bitcast.53), calls=%async_computation.2 | async-start | bytes 4128768
  31.9 50.9 %collective-permute-start = (bf16[5,8,4,128]{3,1,2,0:T(8,128)(2,1)}, bf16[5,8,4,128]{3,1,2,0:T(8,128)(2,1)}, u32[]{:S(2)}, u32[]{:S(2)}) collective-permute-start(bf16[5,8,4,128]{3,1,2,0:T(8,128)(2,1)} %pad_maximum_fusion.4), channel_id=1, source_target_pairs={{0,4},{4,8},{8,12},{12,16},{16,20},{20,24},{24,28},{28,0},{1,5},{5... | collective-permute-start | bytes 122888 | tf_op jit(solution)/shard_map/ppermute | solution.py:381
  34.0 49.6 %collective-permute-start.1 = (bf16[5,8,4,128]{3,1,2,0:T(8,128)(2,1)}, bf16[5,8,4,128]{3,1,2,0:T(8,128)(2,1)}, u32[]{:S(2)}, u32[]{:S(2)}) collective-permute-start(bf16[5,8,4,128]{3,1,2,0:T(8,128)(2,1)} %pad_maximum_fusion.5), channel_id=1, source_target_pairs={{4,0},{8,4},{12,8},{16,12},{20,16},{24,20},{28,24},{0,28},{5,1},{9... | collective-permute-start | bytes 122888 | tf_op jit(solution)/shard_map/ppermute | solution.py:382
  36.7 2.5 %copy-start.2 = (f32[1,24,4,128]{3,1,2,0:T(8,128)}, f32[1,24,4,128]{3,1,2,0:T(8,128)S(1)}, u32[]{:S(2)}) copy-start(f32[1,24,4,128]{3,1,2,0:T(8,128)S(1)} %get-tuple-element.25) | copy-start | bytes 147460
  36.7 3.7 %copy-start.1 = (f32[1,24,4,128]{3,1,2,0:T(8,128)}, f32[1,24,4,128]{3,1,2,0:T(8,128)S(1)}, u32[]{:S(2)}) copy-start(f32[1,24,4,128]{3,1,2,0:T(8,128)S(1)} %get-tuple-element.26) | copy-start | bytes 147460
  42.6 2.2 %copy-start.3 = (s32[768,1]{0,1:T(1,128)S(1)}, s32[768,1]{0,1:T(1,128)}, u32[]{:S(2)}) copy-start(s32[768,1]{0,1:T(1,128)} %param.18) | copy-start | bytes 9220
  86.1 6.6 %collective-permute-start.3 = (bf16[5,24,4,128]{3,1,2,0:T(8,128)(2,1)S(1)}, bf16[5,24,4,128]{3,1,2,0:T(8,128)(2,1)S(1)}, u32[]{:S(2)}, u32[]{:S(2)}) collective-permute-start(bf16[5,24,4,128]{3,1,2,0:T(8,128)(2,1)S(1)} %pad_maximum_fusion.1), channel_id=1, source_target_pairs={{1,0},{2,1},{3,2},{0,3},{5,4},{6,5},{7,6},{4,7},{9,8},{10,9},{11,1... | collective-permute-start | bytes 368648 | tf_op jit(solution)/shard_map/ppermute | solution.py:398
  91.1 4.4 %collective-permute-start.2 = (bf16[5,24,4,128]{3,1,2,0:T(8,128)(2,1)S(1)}, bf16[5,24,4,128]{3,1,2,0:T(8,128)(2,1)S(1)}, u32[]{:S(2)}, u32[]{:S(2)}) collective-permute-start(bf16[5,24,4,128]{3,1,2,0:T(8,128)(2,1)S(1)} %pad_maximum_fusion), channel_id=1, source_target_pairs={{0,1},{1,2},{2,3},{3,0},{4,5},{5,6},{6,7},{7,4},{8,9},{9,10},{10,1... | collective-permute-start | bytes 368648 | tf_op jit(solution)/shard_map/ppermute | solution.py:397
  107.6 1.6 %copy-start = (bf16[32,48,1024]{2,1,0:T(8,128)(2,1)}, bf16[32,48,1024]{2,1,0:T(8,128)(2,1)S(1)}, u32[]{:S(2)}) copy-start(bf16[32,48,1024]{2,1,0:T(8,128)(2,1)S(1)} %all-to-all-done) | copy-start | bytes 9437188

commit v2 on v1

v2 whole, which is shorter than its diff:
```python
import jax
import jax.numpy as jnp
import numpy as np
from jax import lax
from jax.experimental import pallas as pl
from jax.experimental.pallas import tpu as pltpu
from jax.sharding import PartitionSpec as P

section_step = 0.1
AXES = ("curve", "sub")
F32 = jnp.float32
BF16 = jnp.bfloat16


def node_tables():
    nodes = np.array([-1.0, -1.0 / np.sqrt(5.0), 1.0 / np.sqrt(5.0), 1.0])
    quadrature = np.array([1.0 / 6.0, 5.0 / 6.0, 5.0 / 6.0, 1.0 / 6.0])
    products = np.array(
        [np.prod([nodes[i] - nodes[k] for k in range(4) if k != i]) for i in range(4)]
    )
    derivative = np.zeros((4, 4))
    for i in range(4):
        for k in range(4):
            if i != k:
                derivative[i, k] = products[i] / (products[k] * (nodes[i] - nodes[k]))
            else:
                derivative[i, i] = sum(1.0 / (nodes[i] - nodes[m]) for m in range(4) if m != i)
    return derivative.astype(np.float32), quadrature.astype(np.float32)


def row_tables():
    d, w = node_tables()
    s = np.arange(8)
    i, j = s // 4, s % 4
    tables = []
    for half in (0, 2):
        for column in (i, 1 - i, 2 + i, 3 - i):
            tables.append(-d[half + i, column])
    for shift in range(4):
        tables.append(-d[j, (j - shift) % 4])
    for half in (0, 2):
        tables.append(w[half + i] * w[j])
    return np.repeat(np.stack(tables)[:, :, None], 128, axis=2).astype(np.float32)


def lane_rows(x):
    return lax.broadcasted_iota(jnp.int32, x, len(x) - 2)


def roll(x, shift):
    return pltpu.roll(x, shift % 8, axis=1)


def turn_body(x_ref, o_ref):
    width = x_ref.shape[0]
    o_ref[:, :width] = x_ref[...].T
    o_ref[:, width:] = jnp.zeros((o_ref.shape[0], o_ref.shape[1] - width), BF16)


def turn(aux_t, padded):
    width, rows = aux_t.shape
    block = rows // 2
    return pl.pallas_call(
        turn_body,
        grid=(rows // block,),
        in_specs=[pl.BlockSpec((width, block), lambda i: (0, i))],
        out_specs=pl.BlockSpec((block, padded), lambda i: (i, 0)),
        out_shape=jax.ShapeDtypeStruct((rows, padded), BF16),
        name="turn",
        compiler_params=pltpu.CompilerParams(vmem_limit_bytes=60 << 20),
    )(aux_t)


def tend_body(x_ref, m_ref, t_ref, pick_ref, o_ref, c_ref, l_ref, r_ref, mean_ref, *, per):
    fields = x_ref.shape[0]
    rows = x_ref.shape[1]
    span = per * 16
    part = 4
    group = part * 16
    sub = lax.broadcasted_iota(jnp.int32, (part, 8, 128), 1) % 4
    row8 = lax.broadcasted_iota(jnp.int32, (8, 128), 0) % 4
    tab = [t_ref[k][None] for k in range(14)]

    def step(a, carry):
        edge_at = pl.ds(pl.multiple_of(a * 8, 8), 8)
        for q in range(per // part):
            at = pl.ds(pl.multiple_of(a * span + q * group, group), group)

            def halves(v):
                v = v.reshape(part, 2, 8, 128)
                return v[:, 0], v[:, 1]

            def edges(f, y):
                if q == 0:
                    p = jnp.where(row8 == 0, y[0][0], 0.0) + jnp.where(
                        row8 == 1, pltpu.roll(y[1][0], 1, axis=0), 0.0
                    )
                    l_ref[f, edge_at, :] = p.astype(BF16)
                if q == per // part - 1:
                    p = jnp.where(row8 == 0, pltpu.roll(y[0][part - 1], 5, axis=0), 0.0) + jnp.where(
                        row8 == 1, pltpu.roll(y[1][part - 1], 6, axis=0), 0.0
                    )
                    r_ref[f, edge_at, :] = p.astype(BF16)

            m0, m1 = halves(m_ref[at, :])
            w = (m0 * tab[12], m1 * tab[13])
            edges(fields, w)

            def pool(v):
                v = v + roll(v, 4)
                return v + roll(v, 7)

            inv = [1.0 / pool(v) for v in w]
            u = halves(x_ref[0, at, :])
            v = halves(x_ref[1, at, :])
            uw = (u[0] * w[0], u[1] * w[1])
            vw = (v[0] * w[0], v[1] * w[1])
            for f in range(fields):
                x = u if f == 0 else v if f == 1 else halves(x_ref[f, at, :])
                r4 = (roll(x[0], 4), roll(x[1], 4))
                out = []
                means = []
                for h in range(2):
                    da = (
                        tab[4 * h] * x[0]
                        + tab[4 * h + 1] * r4[0]
                        + tab[4 * h + 2] * x[1]
                        + tab[4 * h + 3] * r4[1]
                    )
                    db = tab[8] * x[h]
                    for k in (1, 2, 3):
                        turned = jnp.where(sub >= k, roll(x[h], k), roll(r4[h], k))
                        db = db + tab[8 + k] * turned
                    out.append(uw[h] * da + vw[h] * db)
                    means.append(pool(x[h] * w[h]) * inv[h])
                edges(f, out)
                o_ref[f, at, :] = jnp.stack(out, axis=1).reshape(group, 128)
                mean_ref[at, f * 128 : (f + 1) * 128] = (
                    jnp.stack(means, axis=1).reshape(group, 128).astype(BF16)
                )
        return carry

    lax.fori_loop(0, rows // span, step, 0)
    c_ref[...] = jnp.dot(pick_ref[...], mean_ref[...], preferred_element_type=F32).astype(BF16)


def pick_table(group):
    pick = np.zeros((group // 4, group), np.float32)
    for c in range(group // 4):
        element, p, q = c // 4, (c // 2) % 2, c % 2
        pick[c, element * 16 + p * 8 + q * 2] = 1.0
    return pick


def tendencies(x, mass, rows_a):
    fields, rows, levels = x.shape
    span = rows // rows_a
    lot = 3
    block = lot * span
    edge = jax.ShapeDtypeStruct((fields + 1, rows_a * 8, levels), BF16)
    return pl.pallas_call(
        lambda *refs: tend_body(*refs, per=span // 16),
        grid=(rows // block,),
        in_specs=[
            pl.BlockSpec((fields, block, levels), lambda i: (0, i, 0)),
            pl.BlockSpec((block, levels), lambda i: (i, 0)),
            pl.BlockSpec((14, 8, 128), lambda i: (0, 0, 0)),
            pl.BlockSpec((block // 4, block), lambda i: (0, 0)),
        ],
        out_specs=[
            pl.BlockSpec((fields, block, levels), lambda i: (0, i, 0)),
            pl.BlockSpec((block // 4, fields * levels), lambda i: (i, 0)),
            pl.BlockSpec((fields + 1, lot * 8, levels), lambda i: (0, i, 0)),
            pl.BlockSpec((fields + 1, lot * 8, levels), lambda i: (0, i, 0)),
        ],
        out_shape=[
            jax.ShapeDtypeStruct((fields, rows, levels), F32),
            jax.ShapeDtypeStruct((rows // 4, fields * levels), BF16),
            edge,
            edge,
        ],
        scratch_shapes=[pltpu.VMEM((block, fields * levels), BF16)],
        name="tendencies",
        compiler_params=pltpu.CompilerParams(vmem_limit_bytes=60 << 20),
    )(x, mass, jnp.asarray(row_tables()), jnp.asarray(pick_table(block), BF16))


def section_body(
    t_ref, x_ref, m_ref, q_ref, left_ref, right_ref, o_ref, rim_ref, head_ref, tail_ref, inv_ref, *, per
):
    rows = x_ref.shape[1]
    span = per * 16
    count = rows // span
    fields = head_ref.shape[0] - 1
    s = lax.broadcasted_iota(jnp.int32, (per, 8, 128), 1)
    low = s < 4
    first = s % 4 == 0
    last = s % 4 == 3
    f = pl.program_id(0)

    def halves(v):
        v = v.reshape(per, 2, 8, 128)
        return v[:, 0], v[:, 1]

    def window(a):
        return pl.ds(pl.multiple_of(a * span, span), span)

    def across(here, a, k):
        at = pl.ds(pl.multiple_of(a * 8, 8), 8)
        left = left_ref[k, at, :].astype(F32)[None]
        right = right_ref[k, at, :].astype(F32)[None]
        result = []
        for h, p in enumerate(here):
            near = jnp.where(first[:1], left if h == 0 else roll(left, 7), 0.0)
            far = jnp.where(last[:1], roll(right, 3 - h), 0.0)
            up = jnp.where(last, roll(p, 3), 0.0)
            down = jnp.where(first, roll(p, 5), 0.0)
            up = jnp.concatenate([up[1:], far], axis=0)
            down = jnp.concatenate([near, down[:-1]], axis=0)
            result.append(p + up + down)
        return result

    def rims(k, p0, p1):
        rim_ref[k, 0] = p0.reshape(per * 8, 128)
        rim_ref[k, 1] = p1.reshape(per * 8, 128)
        p0 = p0.reshape(per // 2, 2, 8, 128)
        p1 = p1.reshape(per // 2, 2, 8, 128)
        half = low[: per // 2]
        head_ref[k] = (
            jnp.where(half, p0[:, 0], roll(p0[:, 1], 4)).reshape(per * 4, 128).astype(BF16)
        )
        tail_ref[k] = (
            jnp.where(half, roll(p1[:, 0], 4), p1[:, 1]).reshape(per * 4, 128).astype(BF16)
        )

    def sweep(load, k, put0, put1):
        p0, p1 = across(load(0), 0, k)
        start = p0
        put0(0, p0, True)

        def step(a, before):
            p0, p1 = across(load(a), a, k)
            put0(a, p0 + jnp.where(low, roll(before, 4), 0.0), False)
            put1(a - 1, before + jnp.where(low, 0.0, roll(p0, 4)), False)
            return p1

        p1 = lax.fori_loop(1, count, step, p1)
        put1(count - 1, p1, True)
        rims(k, start, p1)

    @pl.when(f == 0)
    def _():
        def mass_at(a):
            m0, m1 = halves(m_ref[window(a), :])
            return m0 * q_ref[0][None], m1 * q_ref[1][None]

        def put(h):
            def run(a, v, rim):
                inv_ref[a, :, h] = jnp.zeros_like(v) if rim else section_step / v
            return run

        sweep(mass_at, fields, put(0), put(1))

    def put(h):
        def run(a, v, rim):
            x = halves(x_ref[0, window(a), :])[h]
            o_ref[0, a, :, h] = x + v * inv_ref[a, :, h]
        return run

    sweep(lambda a: halves(t_ref[0, window(a), :]), f, put(0), put(1))


def section_of(t, x, mass, left, right, rows_a):
    fields, rows, levels = x.shape
    per = rows // rows_a // 16
    whole = lambda a: pl.BlockSpec(a.shape, lambda f: (0,) * a.ndim)
    quad = jnp.asarray(row_tables()[12:14])
    one = pl.BlockSpec((1, rows, levels), lambda f: (f, 0, 0))
    edge = jax.ShapeDtypeStruct((fields + 1, per * 4, levels), BF16)
    rim = jax.ShapeDtypeStruct((fields + 1, 2, per * 8, levels), F32)
    section, rim, head, tail = pl.pallas_call(
        lambda *refs: section_body(*refs, per=per),
        grid=(fields,),
        in_specs=[one, one] + [whole(a) for a in (mass, quad, left, right)],
        out_specs=[
            pl.BlockSpec((1, rows_a, per, 2, 8, levels), lambda f: (f, 0, 0, 0, 0, 0)),
            whole(rim),
            whole(edge),
            whole(edge),
        ],
        out_shape=[
            jax.ShapeDtypeStruct((fields, rows_a, per, 2, 8, levels), F32),
            rim,
            edge,
            edge,
        ],
        scratch_shapes=[pltpu.VMEM((rows_a, per, 2, 8, levels), F32)],
        name="section",
        compiler_params=pltpu.CompilerParams(vmem_limit_bytes=60 << 20),
    )(t, x, mass, quad, left, right)
    return section.reshape(fields, rows, levels), rim, head, tail


def places_body(owner_ref, o_ref, *, devices, capacity):
    cols = owner_ref.shape[0]
    owner = owner_ref[...]
    hits = owner == lax.broadcasted_iota(jnp.int32, (cols, devices), 1)
    hits = jnp.where(hits, 1.0, 0.0)
    before = lax.broadcasted_iota(jnp.int32, (cols, cols), 0) > lax.broadcasted_iota(
        jnp.int32, (cols, cols), 1
    )
    before = jnp.where(before, 1.0, 0.0).astype(BF16)
    earlier = jnp.dot(before, hits.astype(BF16), preferred_element_type=F32)
    slot = jnp.sum(hits * earlier, axis=1, keepdims=True).astype(jnp.int32)
    place = owner * capacity + slot
    wide = lax.broadcasted_iota(jnp.int32, (cols, devices * capacity), 1)
    o_ref[...] = jnp.where(place == wide, 1.0, 0.0).astype(BF16)


def places(owner, devices, capacity):
    return pl.pallas_call(
        lambda a, o: places_body(a, o, devices=devices, capacity=capacity),
        out_shape=jax.ShapeDtypeStruct((owner.shape[0], devices * capacity), BF16),
        name="places",
        compiler_params=pltpu.CompilerParams(vmem_limit_bytes=60 << 20),
    )(owner)


def first_body(s_ref, w_ref, b_ref, o_ref, w2_ref):
    width = s_ref.shape[1]
    rest = w_ref.shape[0] - width
    o_ref[...] = jnp.dot(s_ref[...], w_ref[:width, :], preferred_element_type=F32) + b_ref[...]
    w2_ref[:rest, :] = w_ref[width:, :]
    w2_ref[rest:, :] = jnp.zeros((w2_ref.shape[0] - rest, w2_ref.shape[1]), BF16)


def first_part(state, weight, bias, padded):
    cols = state.shape[0]
    hidden = weight.shape[1]
    return pl.pallas_call(
        first_body,
        out_shape=[jax.ShapeDtypeStruct((cols, hidden), F32), jax.ShapeDtypeStruct((padded, hidden), BF16)],
        name="first_part",
        compiler_params=pltpu.CompilerParams(vmem_limit_bytes=60 << 20),
    )(state, weight, bias)


def finish_body(
    sel_ref, aux_ref, w_ref, part_ref, wo_ref, bo_ref, spread_ref, x_ref, rim_ref, above_ref, below_ref, o_ref
):
    fields = x_ref.shape[0]
    levels = x_ref.shape[2]
    block = x_ref.shape[1] // 4
    i = pl.program_id(0)
    at = pl.ds(pl.multiple_of(i * block, block), block)
    aux = jnp.dot(sel_ref[at, :], aux_ref[...], preferred_element_type=F32).astype(BF16)
    v = part_ref[at, :] + jnp.dot(aux, w_ref[...], preferred_element_type=F32)
    hidden = (v / (1.0 + jnp.exp(-v))).astype(BF16)
    inc = jnp.dot(hidden, wo_ref[...], preferred_element_type=F32) + bo_ref[...]
    inc = inc.astype(BF16)
    group = spread_ref.shape[1]
    for g in range(block // group):
        wide = jnp.dot(
            spread_ref[...], inc[g * group : (g + 1) * group], preferred_element_type=F32
        )
        to = pl.ds(g * group * 4, group * 4)
        for f in range(fields):
            o_ref[f, to, :] = x_ref[f, to, :] + wide[:, f * levels : (f + 1) * levels]

    per = rim_ref.shape[2] // 8
    low = lax.broadcasted_iota(jnp.int32, (per // 2, 8, 128), 1) < 4

    def patch(h, halo, start):
        def total(k):
            p = halo[k].astype(F32).reshape(per // 2, 8, 128)
            q = roll(p, 4)
            if h == 0:
                add = jnp.stack([jnp.where(low, p, 0.0), jnp.where(low, q, 0.0)], axis=1)
            else:
                add = jnp.stack([jnp.where(low, 0.0, q), jnp.where(low, 0.0, p)], axis=1)
            return rim_ref[k, h].reshape(per, 8, 128) + add.reshape(per, 8, 128)

        scale = section_step / total(fields)
        to = pl.ds(start, per * 16)
        for f in range(fields):
            gain = total(f) * scale
            none = jnp.zeros_like(gain)
            both = jnp.stack([gain, none] if h == 0 else [none, gain], axis=1)
            o_ref[f, to, :] = o_ref[f, to, :] + both.reshape(per * 16, 128)

    @pl.when(i == 0)
    def _():
        patch(0, above_ref, 0)

    @pl.when(i == pl.num_programs(0) - 1)
    def _():
        patch(1, below_ref, block * 4 - per * 16)


def spread_table(group):
    spread = np.zeros((group * 4, group), np.float32)
    for r in range(group * 4):
        e, i, j = r // 16, (r // 4) % 4, r % 4
        spread[r, e * 4 + (i // 2) * 2 + j // 2] = 1.0
    return spread


def finish(sel, aux, weight, part, weight_out, bias_out, x, rim, above, below):
    cols = sel.shape[0]
    fields, rows, levels = x.shape
    block = 256
    spread = jnp.asarray(spread_table(128), BF16)
    full = lambda a: pl.BlockSpec(a.shape, lambda i: (0,) * a.ndim)
    moving = pl.BlockSpec((fields, block * 4, levels), lambda i: (0, i, 0))
    before = (sel, aux, weight, part, weight_out, bias_out, spread)
    after = (rim, above, below)
    return pl.pallas_call(
        finish_body,
        grid=(cols // block,),
        in_specs=[full(a) for a in before] + [moving] + [full(a) for a in after],
        out_specs=moving,
        out_shape=jax.ShapeDtypeStruct(x.shape, F32),
        name="finish",
        compiler_params=pltpu.CompilerParams(vmem_limit_bytes=60 << 20),
    )(*before, x, *after)


def shards(
    prognostic, layer_mass, column_aux, group_owner, weight_in, bias_in, weight_out, bias_out
):
    fields, rows_a, rows_b, _, _, levels = prognostic.shape
    n_curve, n_sub = lax.axis_size("curve"), lax.axis_size("sub")
    devices = n_curve * n_sub
    capacity = column_aux.shape[0] // devices
    aux_width = column_aux.shape[1]
    padded = -(-aux_width // 128) * 128
    rows = rows_a * rows_b * 16

    home = turn(column_aux.T, padded).reshape(devices, capacity, padded)
    home = lax.all_to_all(home, AXES, split_axis=0, concat_axis=0, tiled=True)
    home = home.reshape(devices * capacity, padded)

    x = prognostic.reshape(fields, rows, levels)
    mass = layer_mass.reshape(rows, levels)
    tend, state, left_out, right_out = tendencies(x, mass, rows_a)

    def ahead(n):
        return [(i, (i + 1) % n) for i in range(n)]

    def back(n):
        return [((i + 1) % n, i) for i in range(n)]

    left = lax.ppermute(right_out, "sub", ahead(n_sub))
    right = lax.ppermute(left_out, "sub", back(n_sub))
    section, rim, head, tail = section_of(tend, x, mass, left, right, rows_a)
    above = lax.ppermute(tail, "curve", ahead(n_curve))
    below = lax.ppermute(head, "curve", back(n_curve))

    sel = places(group_owner, devices, capacity)
    part, weight_aux = first_part(state, weight_in, bias_in[None], padded)
    out = finish(sel, home, weight_aux, part, weight_out, bias_out[None], section, rim, above, below)
    return out.reshape(prognostic.shape)


def solution(mesh):
    return jax.shard_map(
        shards,
        mesh=mesh,
        in_specs=(
            P(None, "curve", "sub", None, None, None),
            P("curve", "sub", None, None, None),
            P(("curve", "sub"), None),
            P(("curve", "sub"), None),
            P(),
            P(),
            P(),
            P(),
        ),
        out_specs=P(None, "curve", "sub", None, None, None),
        check_vma=False,
    )
```

time: 127 us -> 103 us (0.81)
  the two profiles are of different devices: /device:TPU:16 before, /device:TPU:0 now
where the time goes in v2:
time: 103 us; the launch traced here: 102 us
  Pallas kernels  57 us (55%)
  waiting for transfers between devices  25 us (24%)
  starting transfers between devices  16.9 us (16%)
  local copies, waits for them, and re-layouts  3.38 us (3%)
    pallas_call x1, Pallas kernels, finish(): pl.pallas_call(finish_body, grid=(cols // block,), in_specs=[full(a) for...  18 us
    ppermute x1, waiting for transfers between devices, shards(): left = lax.ppermute(right_out, 'sub', ahead(n_sub))  13.5 us
    pallas_call x1, Pallas kernels, tendencies(): pl.pallas_call(lambda *refs: tend_body(*refs, per=span // 16), grid=(rows...  12.8 us
    all_to_all x1, waiting for transfers between devices, shards(): home = lax.all_to_all(home, AXES, split_axis=0, concat_axis=0, tiled=True)  11.5 us
    pallas_call x1, Pallas kernels, section_of(): pl.pallas_call(lambda *refs: section_body(*refs, per=per), grid=(fields,)...  10 us
    pallas_call x1, Pallas kernels, first_part(): pl.pallas_call(first_body, out_shape=[jax.ShapeDtypeStruct((cols, hidden)...  8.67 us
    all_to_all x1, starting transfers between devices, shards(): home = lax.all_to_all(home, AXES, split_axis=0, concat_axis=0, tiled=True)  7.33 us
    ppermute x1, starting transfers between devices, shards(): below = lax.ppermute(head, 'curve', back(n_curve))  5.02 us
  transfers between devices with their start and end apart: 5, of which 2 were waited for; matrix products, arithmetic and copies ran while one was open for 1% of the time, Pallas kernels for 35%

profile of v2, /device:TPU:0, one launch (start us, length us, event | category | flops | bytes accessed | tf_op | source)
XLA Modules:
  0.0 102.4 jit_solution(15358782599770229054)
XLA Ops:
  0.0 3.6 %turn.1 = bf16[1536,1024]{1,0:T(8,128)(2,1)} custom-call(bf16[1013,1536]{1,0:T(8,128)(2,1)} %bitcast.16), custom_call_target="tpu_custom_call" | custom-call | tf_op jit(solution)/shard_map/turn/pallas_call | solution.py:63
  3.6 7.3 %all-to-all-start = ((bf16[32,48,1024]{2,1,0:T(8,128)(2,1)}), bf16[32,48,1024]{2,1,0:T(8,128)(2,1)S(1)}, u32[]{:S(2)}, u32[]{:S(2)}) async-start(bf16[32,48,1024]{2,1,0:T(8,128)(2,1)} %bitcast.12), calls=%async_computation | async-start | bytes 6291456 | tf_op jit(solution)/shard_map/all_to_all | solution.py:440
  11.0 12.8 %tendencies.1 = (f32[4,3072,128]{2,1,0:T(8,128)}, bf16[768,512]{1,0:T(8,128)(2,1)}, bf16[5,192,128]{2,1,0:T(8,128)(2,1)}, bf16[5,192,128]{2,1,0:T(8,128)(2,1)}) custom-call(f32[4,3072,128]{2,1,0:T(8,128)} %bitcast.9, f32[3072,128]{1,0:T(8,128)} %bitcast.14, f32[14,8,128]{2,1,0:T(8,128)} %constant.8.clone.refs_2_, bf16[96,384]{1,0:T(8,128)(2,1)} %constant.9.clone.refs_3_), custom_call_target="tpu_custom_call" | custom-call | tf_op jit(solution)/shard_map/tendencies/pallas_call | solution.py:161
  23.7 0.3 collective-permute-start
  24.0 1.5 %collective-permute-start.1 = (bf16[5,192,128]{2,1,0:T(8,128)(2,1)}, bf16[5,192,128]{2,1,0:T(8,128)(2,1)S(1)}, u32[]{:S(2)}, u32[]{:S(2)}) collective-permute-start(bf16[5,192,128]{2,1,0:T(8,128)(2,1)} %get-tuple-element.20), channel_id=1, source_target_pairs={{1,0},{2,1},{3,2},{0,3},{5,4},{6,5},{7,6},{4,7},{9,8},{10,9},{11,1... | collective-permute-start | bytes 737288 | tf_op jit(solution)/shard_map/ppermute | solution.py:454
  25.5 13.5 %collective-permute-done.refs_4_ = bf16[5,192,128]{2,1,0:T(8,128)(2,1)S(1)} collective-permute-done((bf16[5,192,128]{2,1,0:T(8,128)(2,1)}, bf16[5,192,128]{2,1,0:T(8,128)(2,1)S(1)}, u32[]{:S(2)}, u32[]{:S(2)}) %collective-permute-start) | collective-permute-done | bytes 245792 | tf_op jit(solution)/shard_map/ppermute | solution.py:453
  39.1 0.0 collective-permute-done.1.refs_5_
  39.1 0.7 copy-done.1
  39.8 0.1 copy-done.2
  39.9 10.0 %section.1 = (f32[4,24,8,2,8,128]{5,4,3,2,1,0:T(8,128)}, f32[5,2,64,128]{3,2,1,0:T(8,128)}, bf16[5,32,128]{2,1,0:T(8,128)(2,1)}, bf16[5,32,128]{2,1,0:T(8,128)(2,1)}) custom-call(f32[4,3072,128]{2,1,0:T(8,128)} %get-tuple-element.18.refs_0_, f32[4,3072,128]{2,1,0:T(8,128)} %bitcast.10, f32[3072,128]{1,0:T(8,128)} %bitcast.15, ...), custom_call_target="tpu_custom_call" | custom-call | tf_op jit(solution)/shard_map/section/pallas_call | solution.py:281
  49.9 2.8 %collective-permute-start.2 = (bf16[5,32,128]{2,1,0:T(8,128)(2,1)}, bf16[5,32,128]{2,1,0:T(8,128)(2,1)S(1)}, u32[]{:S(2)}, u32[]{:S(2)}) collective-permute-start(bf16[5,32,128]{2,1,0:T(8,128)(2,1)} %get-tuple-element.23), channel_id=1, source_target_pairs={{0,4},{4,8},{8,12},{12,16},{16,20},{20,24},{24,28},{28,0},{1,5},{5... | collective-permute-start | bytes 122888 | tf_op jit(solution)/shard_map/ppermute | solution.py:456
  52.7 5.0 %collective-permute-start.3 = (bf16[5,32,128]{2,1,0:T(8,128)(2,1)}, bf16[5,32,128]{2,1,0:T(8,128)(2,1)S(1)}, u32[]{:S(2)}, u32[]{:S(2)}) collective-permute-start(bf16[5,32,128]{2,1,0:T(8,128)(2,1)} %get-tuple-element.24), channel_id=1, source_target_pairs={{4,0},{8,4},{12,8},{16,12},{20,16},{24,20},{28,24},{0,28},{5,1},{9... | collective-permute-start | bytes 122888 | tf_op jit(solution)/shard_map/ppermute | solution.py:457
  57.8 0.0 copy-done.5
  57.8 0.9 copy.13.a
  58.7 4.0 %places.1.sel_ref = bf16[768,1536]{1,0:T(8,128)(2,1)} custom-call(s32[768,1]{1,0:T(8,128)} %copy.13.a), custom_call_target="tpu_custom_call" | custom-call | tf_op jit(solution)/shard_map/places/pallas_call | solution.py:321
  62.7 8.7 %first_part.1 = (f32[768,2048]{1,0:T(8,128)}, bf16[1024,2048]{1,0:T(8,128)(2,1)}) custom-call(bf16[768,512]{1,0:T(8,128)(2,1)} %get-tuple-element.15.s_ref, bf16[1525,2048]{1,0:T(8,128)(2,1)} %w_ref.1, f32[1,2048]{1,0:T(1,128)} %bitcast.17), custom_call_target="tpu_custom_call" | custom-call | tf_op jit(solution)/shard_map/first_part/pallas_call | solution.py:340
  71.3 0.0 collective-permute-done.2.above_ref
  71.3 0.0 collective-permute-done.3.below_ref
  71.4 0.0 copy-start.4
  71.4 11.5 %all-to-all-done = bf16[32,48,1024]{2,1,0:T(8,128)(2,1)S(1)} async-done(((bf16[32,48,1024]{2,1,0:T(8,128)(2,1)}), bf16[32,48,1024]{2,1,0:T(8,128)(2,1)S(1)}, u32[]{:S(2)}, u32[]{:S(2)}) %all-to-all-start) | async-done | bytes 3145760 | tf_op jit(solution)/shard_map/all_to_all | solution.py:440
  82.8 0.0 copy-done.3
  82.8 0.0 copy-done.4
  82.8 1.6 %copy-done = bf16[32,48,1024]{2,1,0:T(8,128)(2,1)} copy-done((bf16[32,48,1024]{2,1,0:T(8,128)(2,1)}, bf16[32,48,1024]{2,1,0:T(8,128)(2,1)S(1)}, u32[]{:S(2)}) %copy-start) | copy-done | bytes 3145752
  84.5 18.0 %finish.1 = f32[4,3072,128]{2,1,0:T(8,128)} custom-call(bf16[768,1536]{1,0:T(8,128)(2,1)} %places.1.sel_ref, bf16[1536,1024]{1,0:T(8,128)(2,1)} %bitcast.11, bf16[1024,2048]{1,0:T(8,128)(2,1)} %get-tuple-element.16.w_ref, f32[768,2048]{1,0:T(8,128)} %get-tuple-element.17.part_ref, bf16[2048,512]{1,0:T(8,128)(2,1)} %wo_ref.1, f32[1,512]{1,0:T(1,128)} %bitcast.18, ...), custom_call_target="tpu_custom_call" | custom-call | tf_op jit(solution)/shard_map/finish/pallas_call | solution.py:417
  (5 shorter events, 0.0 us)
Async XLA Ops:
  3.6 79.2 %all-to-all-start = ((bf16[32,48,1024]{2,1,0:T(8,128)(2,1)}), bf16[32,48,1024]{2,1,0:T(8,128)(2,1)S(1)}, u32[]{:S(2)}, u32[]{:S(2)}) async-start(bf16[32,48,1024]{2,1,0:T(8,128)(2,1)} %bitcast.12), calls=%async_computation | async-start | bytes 6291456 | tf_op jit(solution)/shard_map/all_to_all | solution.py:440
  23.7 15.3 %collective-permute-start = (bf16[5,192,128]{2,1,0:T(8,128)(2,1)}, bf16[5,192,128]{2,1,0:T(8,128)(2,1)S(1)}, u32[]{:S(2)}, u32[]{:S(2)}) collective-permute-start(bf16[5,192,128]{2,1,0:T(8,128)(2,1)} %get-tuple-element.19), channel_id=1, source_target_pairs={{0,1},{1,2},{2,3},{3,0},{4,5},{5,6},{6,7},{7,4},{8,9},{9,10},{10,1... | collective-permute-start | bytes 737288 | tf_op jit(solution)/shard_map/ppermute | solution.py:453
  24.0 15.1 %collective-permute-start.1 = (bf16[5,192,128]{2,1,0:T(8,128)(2,1)}, bf16[5,192,128]{2,1,0:T(8,128)(2,1)S(1)}, u32[]{:S(2)}, u32[]{:S(2)}) collective-permute-start(bf16[5,192,128]{2,1,0:T(8,128)(2,1)} %get-tuple-element.20), channel_id=1, source_target_pairs={{1,0},{2,1},{3,2},{0,3},{5,4},{6,5},{7,6},{4,7},{9,8},{10,9},{11,1... | collective-permute-start | bytes 737288 | tf_op jit(solution)/shard_map/ppermute | solution.py:454
  39.1 0.7 copy-start.1
  39.1 0.8 copy-start.2
  39.9 17.9 %copy-start.5 = (s32[768,1]{0,1:T(1,128)S(1)}, s32[768,1]{0,1:T(1,128)}, u32[]{:S(2)}) copy-start(s32[768,1]{0,1:T(1,128)} %param.15) | copy-start | bytes 9220
  49.9 21.4 %collective-permute-start.2 = (bf16[5,32,128]{2,1,0:T(8,128)(2,1)}, bf16[5,32,128]{2,1,0:T(8,128)(2,1)S(1)}, u32[]{:S(2)}, u32[]{:S(2)}) collective-permute-start(bf16[5,32,128]{2,1,0:T(8,128)(2,1)} %get-tuple-element.23), channel_id=1, source_target_pairs={{0,4},{4,8},{8,12},{12,16},{16,20},{20,24},{24,28},{28,0},{1,5},{5... | collective-permute-start | bytes 122888 | tf_op jit(solution)/shard_map/ppermute | solution.py:456
  52.7 18.6 %collective-permute-start.3 = (bf16[5,32,128]{2,1,0:T(8,128)(2,1)}, bf16[5,32,128]{2,1,0:T(8,128)(2,1)S(1)}, u32[]{:S(2)}, u32[]{:S(2)}) collective-permute-start(bf16[5,32,128]{2,1,0:T(8,128)(2,1)} %get-tuple-element.24), channel_id=1, source_target_pairs={{4,0},{8,4},{12,8},{16,12},{20,16},{24,20},{28,24},{0,28},{5,1},{9... | collective-permute-start | bytes 122888 | tf_op jit(solution)/shard_map/ppermute | solution.py:457
  71.3 11.5 %copy-start.3 = (bf16[5,32,128]{2,1,0:T(8,128)(2,1)}, bf16[5,32,128]{2,1,0:T(8,128)(2,1)S(1)}, u32[]{:S(2)}) copy-start(bf16[5,32,128]{2,1,0:T(8,128)(2,1)S(1)} %collective-permute-done.2.above_ref) | copy-start | bytes 122884
  71.4 11.5 %copy-start.4 = (bf16[5,32,128]{2,1,0:T(8,128)(2,1)}, bf16[5,32,128]{2,1,0:T(8,128)(2,1)S(1)}, u32[]{:S(2)}) copy-start(bf16[5,32,128]{2,1,0:T(8,128)(2,1)S(1)} %collective-permute-done.3.below_ref) | copy-start | bytes 122884
  82.8 1.6 %copy-start = (bf16[32,48,1024]{2,1,0:T(8,128)(2,1)}, bf16[32,48,1024]{2,1,0:T(8,128)(2,1)S(1)}, u32[]{:S(2)}) copy-start(bf16[32,48,1024]{2,1,0:T(8,128)(2,1)S(1)} %all-to-all-done) | copy-start | bytes 9437188

commit v3 on v2

v3 whole, which is shorter than its diff:
```python
import jax
import jax.numpy as jnp
import numpy as np
from jax import lax
from jax.experimental import pallas as pl
from jax.experimental.pallas import tpu as pltpu
from jax.sharding import PartitionSpec as P

section_step = 0.1
AXES = ("curve", "sub")
F32 = jnp.float32
BF16 = jnp.bfloat16


def node_tables():
    nodes = np.array([-1.0, -1.0 / np.sqrt(5.0), 1.0 / np.sqrt(5.0), 1.0])
    quadrature = np.array([1.0 / 6.0, 5.0 / 6.0, 5.0 / 6.0, 1.0 / 6.0])
    products = np.array(
        [np.prod([nodes[i] - nodes[k] for k in range(4) if k != i]) for i in range(4)]
    )
    derivative = np.zeros((4, 4))
    for i in range(4):
        for k in range(4):
            if i != k:
                derivative[i, k] = products[i] / (products[k] * (nodes[i] - nodes[k]))
            else:
                derivative[i, i] = sum(1.0 / (nodes[i] - nodes[m]) for m in range(4) if m != i)
    return derivative.astype(np.float32), quadrature.astype(np.float32)


def row_tables():
    d, w = node_tables()
    s = np.arange(8)
    i, j = s // 4, s % 4
    tables = []
    for half in (0, 2):
        for column in (i, 1 - i, 2 + i, 3 - i):
            tables.append(-d[half + i, column])
    for shift in range(4):
        tables.append(-d[j, (j - shift) % 4])
    for half in (0, 2):
        tables.append(w[half + i] * w[j])
    return np.repeat(np.stack(tables)[:, :, None], 128, axis=2).astype(np.float32)


def lane_rows(x):
    return lax.broadcasted_iota(jnp.int32, x, len(x) - 2)


def roll(x, shift):
    return pltpu.roll(x, shift % 8, axis=1)


def turn_body(x_ref, o_ref):
    width = x_ref.shape[0]
    o_ref[:, :width] = x_ref[...].T
    o_ref[:, width:] = jnp.zeros((o_ref.shape[0], o_ref.shape[1] - width), BF16)


def turn(aux_t, padded):
    width, rows = aux_t.shape
    block = rows // 2
    return pl.pallas_call(
        turn_body,
        grid=(rows // block,),
        in_specs=[pl.BlockSpec((width, block), lambda i: (0, i))],
        out_specs=pl.BlockSpec((block, padded), lambda i: (i, 0)),
        out_shape=jax.ShapeDtypeStruct((rows, padded), BF16),
        name="turn",
        compiler_params=pltpu.CompilerParams(vmem_limit_bytes=56 << 20),
    )(aux_t)


def tend_body(x_ref, m_ref, q_ref, deriv_ref, pick_ref, o_ref, c_ref, l_ref, r_ref):
    fields, rows, levels = x_ref.shape
    group = q_ref.shape[0]
    cells = group // 4
    lines = (pick_ref.shape[0] - cells) // 2

    for g in range(rows // group):
        at = pl.ds(g * group, group)
        cell_at = pl.ds(g * cells, cells)
        line_at = pl.ds(g * lines, lines)

        def picked(first, second):
            y = jnp.dot(
                pick_ref[...], jnp.concatenate([first, second], axis=1), preferred_element_type=F32
            )
            return y[:cells, :levels], y[cells:, levels:].astype(BF16)

        w = m_ref[at, :] * q_ref[...]
        wb = w.astype(BF16)
        mass, edge = picked(wb, wb)
        inv = 1.0 / mass
        l_ref[fields, line_at, :] = edge[:lines]
        r_ref[fields, line_at, :] = edge[lines:]
        uw = x_ref[0, at, :] * w
        vw = x_ref[1, at, :] * w
        for pair in range(0, fields, 2):
            both = (x_ref[pair, at, :], x_ref[pair + 1, at, :])
            d = jnp.dot(
                deriv_ref[...],
                jnp.concatenate([x.astype(BF16) for x in both], axis=1),
                preferred_element_type=F32,
            )
            for k, x in enumerate(both):
                f = pair + k
                lanes = slice(k * levels, (k + 1) * levels)
                out = (uw * d[:group, lanes] + vw * d[group:, lanes]).astype(BF16)
                xw = (uw if f == 0 else vw if f == 1 else x * w).astype(BF16)
                o_ref[f, at, :] = out
                mean, edge = picked(xw, out)
                c_ref[cell_at, f * levels : (f + 1) * levels] = (mean * inv).astype(BF16)
                l_ref[f, line_at, :] = edge[:lines]
                r_ref[f, line_at, :] = edge[lines:]


def derivative_table(group):
    d = node_tables()[0]
    r = np.arange(group)
    same = (r[:, None] // 16) == (r[None, :] // 16)
    i, j = (r // 4) % 4, r % 4
    along_first = np.where(same & (j[:, None] == j[None, :]), d[i[:, None], i[None, :]], 0.0)
    along_second = np.where(same & (i[:, None] == i[None, :]), d[j[:, None], j[None, :]], 0.0)
    return -np.concatenate([along_first, along_second], axis=0)


def pick_table(group, span):
    r = np.arange(group)
    cells = np.zeros((group // 4, group), np.float32)
    cells[(r // 16) * 4 + ((r // 8) % 2) * 2 + (r % 4) // 2, r] = 1.0
    lines = [np.zeros((group // span * 8, group), np.float32) for _ in range(2)]
    for a in range(group // span):
        for i in range(4):
            to = a * 8 + (i % 2) * 4 + i // 2
            lines[0][to, a * span + i * 4] = 1.0
            lines[1][to, (a + 1) * span - 16 + i * 4 + 3] = 1.0
    return np.concatenate([cells] + lines, axis=0)


def tendencies(x, mass, rows_a):
    fields, rows, levels = x.shape
    span = rows // rows_a
    group = 2 * span
    lot = 4
    block = lot * span
    quad = np.tile(row_tables()[12:14].reshape(16, 128), (group // 16, 1))
    deriv = jnp.asarray(derivative_table(group), BF16)
    pick = jnp.asarray(pick_table(group, span), BF16)
    edge = jax.ShapeDtypeStruct((fields + 1, rows_a * 8, levels), BF16)
    whole = lambda a: pl.BlockSpec(a.shape, lambda i: (0, 0))
    return pl.pallas_call(
        tend_body,
        grid=(rows // block,),
        in_specs=[
            pl.BlockSpec((fields, block, levels), lambda i: (0, i, 0)),
            pl.BlockSpec((block, levels), lambda i: (i, 0)),
            whole(quad),
            whole(deriv),
            whole(pick),
        ],
        out_specs=[
            pl.BlockSpec((fields, block, levels), lambda i: (0, i, 0)),
            pl.BlockSpec((block // 4, fields * levels), lambda i: (i, 0)),
            pl.BlockSpec((fields + 1, lot * 8, levels), lambda i: (0, i, 0)),
            pl.BlockSpec((fields + 1, lot * 8, levels), lambda i: (0, i, 0)),
        ],
        out_shape=[
            jax.ShapeDtypeStruct((fields, rows, levels), BF16),
            jax.ShapeDtypeStruct((rows // 4, fields * levels), BF16),
            edge,
            edge,
        ],
        name="tendencies",
        compiler_params=pltpu.CompilerParams(vmem_limit_bytes=56 << 20),
    )(x, mass, jnp.asarray(quad), deriv, pick)


def section_body(
    t_ref, x_ref, m_ref, q_ref, left_ref, right_ref, o_ref, rim_ref, head_ref, tail_ref, inv_ref, *, per
):
    rows = x_ref.shape[1]
    span = per * 16
    count = rows // span
    fields = head_ref.shape[0] - 1
    s = lax.broadcasted_iota(jnp.int32, (per, 8, 128), 1)
    low = s < 4
    first = s % 4 == 0
    last = s % 4 == 3
    f = pl.program_id(0)

    def halves(v):
        v = v.reshape(per, 2, 8, 128)
        return v[:, 0], v[:, 1]

    def window(a):
        return pl.ds(pl.multiple_of(a * span, span), span)

    def across(here, a, k):
        at = pl.ds(pl.multiple_of(a * 8, 8), 8)
        left = left_ref[k, at, :].astype(F32)[None]
        right = right_ref[k, at, :].astype(F32)[None]
        result = []
        for h, p in enumerate(here):
            near = jnp.where(first[:1], left if h == 0 else roll(left, 7), 0.0)
            far = jnp.where(last[:1], roll(right, 3 - h), 0.0)
            up = jnp.where(last, roll(p, 3), 0.0)
            down = jnp.where(first, roll(p, 5), 0.0)
            up = jnp.concatenate([up[1:], far], axis=0)
            down = jnp.concatenate([near, down[:-1]], axis=0)
            result.append(p + up + down)
        return result

    def rims(k, p0, p1):
        rim_ref[k, 0] = p0.reshape(per * 8, 128)
        rim_ref[k, 1] = p1.reshape(per * 8, 128)
        p0 = p0.reshape(per // 2, 2, 8, 128)
        p1 = p1.reshape(per // 2, 2, 8, 128)
        half = low[: per // 2]
        head_ref[k] = (
            jnp.where(half, p0[:, 0], roll(p0[:, 1], 4)).reshape(per * 4, 128).astype(BF16)
        )
        tail_ref[k] = (
            jnp.where(half, roll(p1[:, 0], 4), p1[:, 1]).reshape(per * 4, 128).astype(BF16)
        )

    def sweep(load, k, put):
        start, p1 = across(load(0), 0, k)

        def step(a, carry):
            y0, before = carry
            p0, p1 = across(load(a), a, k)
            put(a - 1, y0, before + jnp.where(low, 0.0, roll(p0, 4)))
            return p0 + jnp.where(low, roll(before, 4), 0.0), p1

        y0, p1 = lax.fori_loop(1, count, step, (start, p1))
        put(count - 1, y0, p1)
        rims(k, start, p1)

    def joined(y0, y1):
        return jnp.stack([y0, y1], axis=1).reshape(span, 128)

    @pl.when(f == 0)
    def _():
        def mass_at(a):
            m0, m1 = halves(m_ref[window(a), :])
            return m0 * q_ref[0][None], m1 * q_ref[1][None]

        def put(a, y0, y1):
            inv_ref[window(a), :] = section_step / joined(y0, y1)

        sweep(mass_at, fields, put)
        top = pl.ds(0, span)
        v0, v1 = halves(inv_ref[top, :])
        inv_ref[top, :] = joined(jnp.zeros_like(v0), v1)
        end = pl.ds(rows - span, span)
        v0, v1 = halves(inv_ref[end, :])
        inv_ref[end, :] = joined(v0, jnp.zeros_like(v1))

    def put(a, y0, y1):
        y = x_ref[0, window(a), :] + joined(y0, y1) * inv_ref[window(a), :]
        o_ref[0, window(a), :] = y.astype(o_ref.dtype)

    sweep(lambda a: halves(t_ref[0, window(a), :].astype(F32)), f, put)


def section_of(t, x, mass, left, right, rows_a):
    fields, rows, levels = x.shape
    per = rows // rows_a // 16
    whole = lambda a: pl.BlockSpec(a.shape, lambda f: (0,) * a.ndim)
    quad = jnp.asarray(row_tables()[12:14])
    one = pl.BlockSpec((1, rows, levels), lambda f: (f, 0, 0))
    edge = jax.ShapeDtypeStruct((fields + 1, per * 4, levels), BF16)
    rim = jax.ShapeDtypeStruct((fields + 1, 2, per * 8, levels), F32)
    section, rim, head, tail = pl.pallas_call(
        lambda *refs: section_body(*refs, per=per),
        grid=(fields,),
        in_specs=[one, one] + [whole(a) for a in (mass, quad, left, right)],
        out_specs=[
            one,
            whole(rim),
            whole(edge),
            whole(edge),
        ],
        out_shape=[
            jax.ShapeDtypeStruct(x.shape, BF16),
            rim,
            edge,
            edge,
        ],
        scratch_shapes=[pltpu.VMEM((rows, levels), F32)],
        name="section",
        compiler_params=pltpu.CompilerParams(vmem_limit_bytes=56 << 20),
    )(t, x, mass, quad, left, right)
    return section, rim, head, tail


def places_body(owner_ref, o_ref, *, devices, capacity):
    cols = owner_ref.shape[0]
    owner = owner_ref[...]
    hits = owner == lax.broadcasted_iota(jnp.int32, (cols, devices), 1)
    hits = jnp.where(hits, 1.0, 0.0)
    before = lax.broadcasted_iota(jnp.int32, (cols, cols), 0) > lax.broadcasted_iota(
        jnp.int32, (cols, cols), 1
    )
    before = jnp.where(before, 1.0, 0.0).astype(BF16)
    earlier = jnp.dot(before, hits.astype(BF16), preferred_element_type=F32)
    slot = jnp.sum(hits * earlier, axis=1, keepdims=True).astype(jnp.int32)
    place = owner * capacity + slot
    wide = lax.broadcasted_iota(jnp.int32, (cols, devices * capacity), 1)
    o_ref[...] = jnp.where(place == wide, 1.0, 0.0).astype(BF16)


def places(owner, devices, capacity):
    return pl.pallas_call(
        lambda a, o: places_body(a, o, devices=devices, capacity=capacity),
        out_shape=jax.ShapeDtypeStruct((owner.shape[0], devices * capacity), BF16),
        name="places",
        compiler_params=pltpu.CompilerParams(vmem_limit_bytes=56 << 20),
    )(owner)


def first_body(s_ref, w_ref, b_ref, o_ref, w2_ref):
    width = s_ref.shape[1]
    rest = w_ref.shape[0] - width
    y = jnp.dot(s_ref[...], w_ref[:width, :], preferred_element_type=F32) + b_ref[...]
    o_ref[...] = y.astype(BF16)
    w2_ref[:rest, :] = w_ref[width:, :]
    w2_ref[rest:, :] = jnp.zeros((w2_ref.shape[0] - rest, w2_ref.shape[1]), BF16)


def first_part(state, weight, bias, padded):
    cols, width = state.shape
    depth, hidden = weight.shape
    block = 512
    return pl.pallas_call(
        first_body,
        grid=(hidden // block,),
        in_specs=[
            pl.BlockSpec((cols, width), lambda i: (0, 0)),
            pl.BlockSpec((depth, block), lambda i: (0, i)),
            pl.BlockSpec((1, block), lambda i: (0, i)),
        ],
        out_specs=[
            pl.BlockSpec((cols, block), lambda i: (0, i)),
            pl.BlockSpec((padded, block), lambda i: (0, i)),
        ],
        out_shape=[
            jax.ShapeDtypeStruct((cols, hidden), BF16),
            jax.ShapeDtypeStruct((padded, hidden), BF16),
        ],
        name="first_part",
        compiler_params=pltpu.CompilerParams(vmem_limit_bytes=56 << 20),
    )(state, weight, bias)


def finish_body(
    sel_hbm, w_hbm, part_hbm, wo_hbm, x_hbm, home_ref, bo_ref, spread_ref, rim_ref, above_ref, below_ref, out_hbm,
    sel_ref, w_ref, part_ref, wo_ref, x_ref, aux_ref, o_ref, sem, out_sem, *, block
):
    fields, rows, levels = x_ref.shape
    cols = sel_ref.shape[0]
    steps = cols // block

    copies = {}

    def fetch(name, src, dst):
        copies[name] = pltpu.make_async_copy(src, dst, sem.at[len(copies)])
        copies[name].start()

    def rows_of(k, scale=1):
        return pl.ds(k * block * scale, block * scale)

    fetch("sel", sel_hbm, sel_ref)
    fetch("w", w_hbm, w_ref)
    fetch("part0", part_hbm.at[rows_of(0), :], part_ref.at[rows_of(0), :])
    fetch("wo", wo_hbm, wo_ref)
    fetch("x0", x_hbm.at[:, rows_of(0, 4), :], x_ref.at[:, rows_of(0, 4), :])
    for k in range(1, steps):
        fetch(f"part{k}", part_hbm.at[rows_of(k), :], part_ref.at[rows_of(k), :])
        fetch(f"x{k}", x_hbm.at[:, rows_of(k, 4), :], x_ref.at[:, rows_of(k, 4), :])

    per = rim_ref.shape[2] // 8
    low = lax.broadcasted_iota(jnp.int32, (per // 2, 8, 128), 1) < 4

    def patch(h, halo, start):
        def total(k):
            p = halo[k].astype(F32).reshape(per // 2, 8, 128)
            q = roll(p, 4)
            if h == 0:
                add = jnp.stack([jnp.where(low, p, 0.0), jnp.where(low, q, 0.0)], axis=1)
            else:
                add = jnp.stack([jnp.where(low, 0.0, q), jnp.where(low, 0.0, p)], axis=1)
            return rim_ref[k, h].reshape(per, 8, 128) + add.reshape(per, 8, 128)

        scale = section_step / total(fields)
        to = pl.ds(start, per * 16)
        for f in range(fields):
            gain = total(f) * scale
            none = jnp.zeros_like(gain)
            both = jnp.stack([gain, none] if h == 0 else [none, gain], axis=1)
            o_ref[f, to, :] = o_ref[f, to, :] + both.reshape(per * 16, 128)

    copies["sel"].wait()
    aux_ref[...] = jnp.dot(sel_ref[...], home_ref[...], preferred_element_type=F32).astype(BF16)
    copies["w"].wait()
    group = spread_ref.shape[1]
    outs = []
    for k in range(steps):
        at = rows_of(k)
        copies[f"part{k}"].wait()
        v = part_ref[at, :].astype(F32) + jnp.dot(aux_ref[at, :], w_ref[...], preferred_element_type=F32)
        half = 0.5 * v
        hidden = (half + half * jnp.tanh(half)).astype(BF16)
        if k == 0:
            copies["wo"].wait()
        inc = jnp.dot(hidden, wo_ref[...], preferred_element_type=F32) + bo_ref[...]
        inc = inc.astype(BF16)
        copies[f"x{k}"].wait()
        for g in range(block // group):
            wide = jnp.dot(
                spread_ref[...], inc[g * group : (g + 1) * group], preferred_element_type=F32
            )
            to = pl.ds((k * block + g * group) * 4, group * 4)
            for f in range(fields):
                o_ref[f, to, :] = x_ref[f, to, :].astype(F32) + wide[:, f * levels : (f + 1) * levels]
        if k == 0:
            patch(0, above_ref, 0)
        if k == steps - 1:
            patch(1, below_ref, rows - per * 16)
        done = pltpu.make_async_copy(
            o_ref.at[:, rows_of(k, 4), :], out_hbm.at[:, rows_of(k, 4), :], out_sem.at[k]
        )
        done.start()
        outs.append(done)
    for done in outs:
        done.wait()


def spread_table(group):
    spread = np.zeros((group * 4, group), np.float32)
    for r in range(group * 4):
        e, i, j = r // 16, (r // 4) % 4, r % 4
        spread[r, e * 4 + (i // 2) * 2 + j // 2] = 1.0
    return spread


def finish(sel, home, weight, part, weight_out, bias_out, x, rim, above, below):
    cols = sel.shape[0]
    fields, rows, levels = x.shape
    block = 256
    steps = cols // block
    spread = jnp.asarray(spread_table(128), BF16)
    far = pl.BlockSpec(memory_space=pltpu.HBM)
    full = lambda a: pl.BlockSpec(a.shape, lambda: (0,) * a.ndim)
    large = (sel, weight, part, weight_out, x)
    small = (home, bias_out, spread, rim, above, below)
    return pl.pallas_call(
        lambda *refs: finish_body(*refs, block=block),
        in_specs=[far] * len(large)
        + [pl.BlockSpec(memory_space=pltpu.VMEM)]
        + [full(a) for a in small[1:]],
        out_specs=far,
        out_shape=jax.ShapeDtypeStruct(x.shape, F32),
        scratch_shapes=[pltpu.VMEM(a.shape, a.dtype) for a in large]
        + [
            pltpu.VMEM((cols, home.shape[1]), BF16),
            pltpu.VMEM(x.shape, F32),
            pltpu.SemaphoreType.DMA((3 + 2 * steps,)),
            pltpu.SemaphoreType.DMA((steps,)),
        ],
        name="finish",
        compiler_params=pltpu.CompilerParams(vmem_limit_bytes=50 << 20),
    )(*large, *small)


def shards(
    prognostic, layer_mass, column_aux, group_owner, weight_in, bias_in, weight_out, bias_out
):
    fields, rows_a, rows_b, _, _, levels = prognostic.shape
    n_curve, n_sub = lax.axis_size("curve"), lax.axis_size("sub")
    devices = n_curve * n_sub
    capacity = column_aux.shape[0] // devices
    aux_width = column_aux.shape[1]
    padded = -(-aux_width // 128) * 128
    rows = rows_a * rows_b * 16

    home = turn(column_aux.T, padded).reshape(devices, capacity, padded)
    home = lax.all_to_all(home, AXES, split_axis=0, concat_axis=0, tiled=True)
    home = home.reshape(devices * capacity, padded)

    x = prognostic.reshape(fields, rows, levels)
    mass = layer_mass.reshape(rows, levels)
    tend, state, left_out, right_out = tendencies(x, mass, rows_a)

    def ahead(n):
        return [(i, (i + 1) % n) for i in range(n)]

    def back(n):
        return [((i + 1) % n, i) for i in range(n)]

    left = lax.ppermute(right_out, "sub", ahead(n_sub))
    right = lax.ppermute(left_out, "sub", back(n_sub))
    section, rim, head, tail = section_of(tend, x, mass, left, right, rows_a)
    above = lax.ppermute(tail, "curve", ahead(n_curve))
    below = lax.ppermute(head, "curve", back(n_curve))

    sel = places(group_owner, devices, capacity)
    part, weight_aux = first_part(state, weight_in, bias_in[None], padded)
    out = finish(sel, home, weight_aux, part, weight_out, bias_out[None], section, rim, above, below)
    return out.reshape(prognostic.shape)


def solution(mesh):
    return jax.shard_map(
        shards,
        mesh=mesh,
        in_specs=(
            P(None, "curve", "sub", None, None, None),
            P("curve", "sub", None, None, None),
            P(("curve", "sub"), None),
            P(("curve", "sub"), None),
            P(),
            P(),
            P(),
            P(),
        ),
        out_specs=P(None, "curve", "sub", None, None, None),
        check_vma=False,
    )
```

time: 103 us -> 98.6 us (0.957)
  Pallas kernels: 57 us -> 50.1 us
  waiting for transfers between devices: 25 us -> 28.7 us
  local copies, waits for them, and re-layouts: 3.38 us -> 1.73 us
    pallas_call x3, Pallas kernels: 39.4 us -> 33.6 us  [the longest x1 15.1 us: finish(): pl.pallas_call(lambda *refs: finish_body(*refs, block=block), in_specs=[f...]
    all_to_all x1, waiting for transfers between devices: 11.5 us -> 13.5 us  [shards(): home = lax.all_to_all(home, AXES, split_axis=0, concat_axis=0, tiled=True)]
    ppermute x1, waiting for transfers between devices: 13.5 us -> 15.2 us  [shards(): left = lax.ppermute(right_out, 'sub', ahead(n_sub))]
    unnamed x13 -> x15, local copies, waits for them, and re-layouts: 3.38 us -> 1.73 us
    pallas_call x1, Pallas kernels: 10 us -> 8.91 us  [section_of(): pl.pallas_call(lambda *refs: section_body(*refs, per=per), grid=(fields,)...]
  transfers between devices with their start and end apart: 5 -> 5, of which waited for: 2 -> 2; matrix products, arithmetic and copies ran while one was open for 1% -> 1% of each run, Pallas kernels for 35% -> 32%
where the time goes in v3:
time: 98.6 us; the launch traced here: 98.1 us
  Pallas kernels  50.1 us (51%)
  waiting for transfers between devices  28.7 us (29%)
  starting transfers between devices  17.5 us (18%)
  local copies, waits for them, and re-layouts  1.73 us (2%)
    ppermute x1, waiting for transfers between devices, shards(): left = lax.ppermute(right_out, 'sub', ahead(n_sub))  15.2 us
    pallas_call x1, Pallas kernels, finish(): pl.pallas_call(lambda *refs: finish_body(*refs, block=block), in_specs=[f...  15.1 us
    all_to_all x1, waiting for transfers between devices, shards(): home = lax.all_to_all(home, AXES, split_axis=0, concat_axis=0, tiled=True)  13.5 us
    pallas_call x1, Pallas kernels, tendencies(): pl.pallas_call(tend_body, grid=(rows // block,), in_specs=[pl.BlockSpec((...  10.5 us
    pallas_call x1, Pallas kernels, section_of(): pl.pallas_call(lambda *refs: section_body(*refs, per=per), grid=(fields,)...  8.91 us
    pallas_call x1, Pallas kernels, first_part(): pl.pallas_call(first_body, grid=(hidden // block,), in_specs=[pl.BlockSpe...  7.96 us
    all_to_all x1, starting transfers between devices, shards(): home = lax.all_to_all(home, AXES, split_axis=0, concat_axis=0, tiled=True)  7.44 us
    ppermute x1, starting transfers between devices, shards(): below = lax.ppermute(head, 'curve', back(n_curve))  5.01 us
  transfers between devices with their start and end apart: 5, of which 2 were waited for; matrix products, arithmetic and copies ran while one was open for 1% of the time, Pallas kernels for 32%

profile of v3, /device:TPU:0, one launch (start us, length us, event | category | flops | bytes accessed | tf_op | source)
XLA Modules:
  0.0 98.1 jit_solution(9591326582475142071)
XLA Ops:
  0.0 3.7 %turn.1 = bf16[1536,1024]{1,0:T(8,128)(2,1)} custom-call(bf16[1013,1536]{1,0:T(8,128)(2,1)} %bitcast.14), custom_call_target="tpu_custom_call" | custom-call | tf_op jit(solution)/shard_map/turn/pallas_call | solution.py:63
  3.7 7.4 %all-to-all-start = ((bf16[32,48,1024]{2,1,0:T(8,128)(2,1)}), bf16[32,48,1024]{2,1,0:T(8,128)(2,1)}, u32[]{:S(2)}, u32[]{:S(2)}) async-start(bf16[32,48,1024]{2,1,0:T(8,128)(2,1)} %bitcast.11), calls=%async_computation | async-start | bytes 6291456 | tf_op jit(solution)/shard_map/all_to_all | solution.py:489
  11.1 10.5 %tendencies.1 = (bf16[4,3072,128]{2,1,0:T(8,128)(2,1)}, bf16[768,512]{1,0:T(8,128)(2,1)}, bf16[5,192,128]{2,1,0:T(8,128)(2,1)}, bf16[5,192,128]{2,1,0:T(8,128)(2,1)}) custom-call(f32[4,3072,128]{2,1,0:T(8,128)} %bitcast.9, f32[3072,128]{1,0:T(8,128)} %bitcast.12, f32[256,128]{1,0:T(8,128)} %constant.12.clone.q_ref, ...), custom_call_target="tpu_custom_call" | custom-call | tf_op jit(solution)/shard_map/tendencies/pallas_call | solution.py:152
  21.6 0.2 collective-permute-start
  21.8 1.6 %collective-permute-start.1 = (bf16[5,192,128]{2,1,0:T(8,128)(2,1)}, bf16[5,192,128]{2,1,0:T(8,128)(2,1)S(1)}, u32[]{:S(2)}, u32[]{:S(2)}) collective-permute-start(bf16[5,192,128]{2,1,0:T(8,128)(2,1)} %get-tuple-element.20), channel_id=1, source_target_pairs={{1,0},{2,1},{3,2},{0,3},{5,4},{6,5},{7,6},{4,7},{9,8},{10,9},{11,1... | collective-permute-start | bytes 737288 | tf_op jit(solution)/shard_map/ppermute | solution.py:503
  23.4 15.2 %collective-permute-done.refs_4_ = bf16[5,192,128]{2,1,0:T(8,128)(2,1)S(1)} collective-permute-done((bf16[5,192,128]{2,1,0:T(8,128)(2,1)}, bf16[5,192,128]{2,1,0:T(8,128)(2,1)S(1)}, u32[]{:S(2)}, u32[]{:S(2)}) %collective-permute-start) | collective-permute-done | bytes 245792 | tf_op jit(solution)/shard_map/ppermute | solution.py:502
  38.6 0.0 collective-permute-done.1.refs_5_
  38.6 0.7 copy-done.4
  39.3 0.1 copy-done.5
  39.4 8.9 %section.1 = (bf16[4,3072,128]{2,1,0:T(8,128)(2,1)}, f32[5,2,64,128]{3,2,1,0:T(8,128)}, bf16[5,32,128]{2,1,0:T(8,128)(2,1)}, bf16[5,32,128]{2,1,0:T(8,128)(2,1)}) custom-call(bf16[4,3072,128]{2,1,0:T(8,128)(2,1)} %get-tuple-element.18.refs_0_, f32[4,3072,128]{2,1,0:T(8,128)} %bitcast.10, f32[3072,128]{1,0:T(8,128)} %bitcast.13, ...), custom_call_target="tpu_custom_call" | custom-call | tf_op jit(solution)/shard_map/section/pallas_call | solution.py:275
  48.3 3.3 %collective-permute-start.2 = (bf16[5,32,128]{2,1,0:T(8,128)(2,1)}, bf16[5,32,128]{2,1,0:T(8,128)(2,1)S(1)}, u32[]{:S(2)}, u32[]{:S(2)}) collective-permute-start(bf16[5,32,128]{2,1,0:T(8,128)(2,1)} %get-tuple-element.23), channel_id=1, source_target_pairs={{0,4},{4,8},{8,12},{12,16},{16,20},{20,24},{24,28},{28,0},{1,5},{5... | collective-permute-start | bytes 122888 | tf_op jit(solution)/shard_map/ppermute | solution.py:505
  51.6 5.0 %collective-permute-start.3 = (bf16[5,32,128]{2,1,0:T(8,128)(2,1)}, bf16[5,32,128]{2,1,0:T(8,128)(2,1)S(1)}, u32[]{:S(2)}, u32[]{:S(2)}) collective-permute-start(bf16[5,32,128]{2,1,0:T(8,128)(2,1)} %get-tuple-element.24), channel_id=1, source_target_pairs={{4,0},{8,4},{12,8},{16,12},{20,16},{24,20},{28,24},{0,28},{5,1},{9... | collective-permute-start | bytes 122888 | tf_op jit(solution)/shard_map/ppermute | solution.py:506
  56.6 0.0 copy-done.6
  56.6 0.9 copy.14.a
  57.5 3.9 %places.1.refs_0_ = bf16[768,1536]{1,0:T(8,128)(2,1)} custom-call(s32[768,1]{1,0:T(8,128)} %copy.14.a), custom_call_target="tpu_custom_call" | custom-call | tf_op jit(solution)/shard_map/places/pallas_call | solution.py:315
  61.5 8.0 %first_part.1 = (bf16[768,2048]{1,0:T(8,128)(2,1)}, bf16[1024,2048]{1,0:T(8,128)(2,1)}) custom-call(bf16[768,512]{1,0:T(8,128)(2,1)} %get-tuple-element.15.s_ref, bf16[1525,2048]{1,0:T(8,128)(2,1)} %w_ref.1, f32[1,2048]{1,0:T(1,128)} %bitcast.15), custom_call_target="tpu_custom_call" | custom-call | tf_op jit(solution)/shard_map/first_part/pallas_call | solution.py:336
  69.4 0.0 collective-permute-done.2.refs_9_
  69.4 0.0 collective-permute-done.3.refs_10_
  69.4 13.5 %all-to-all-done = bf16[32,48,1024]{2,1,0:T(8,128)(2,1)} async-done(((bf16[32,48,1024]{2,1,0:T(8,128)(2,1)}), bf16[32,48,1024]{2,1,0:T(8,128)(2,1)}, u32[]{:S(2)}, u32[]{:S(2)}) %all-to-all-start) | async-done | bytes 3145760 | tf_op jit(solution)/shard_map/all_to_all | solution.py:489
  83.0 0.0 copy-done
  83.0 0.0 copy-done.1
  83.0 0.0 copy-done.2
  83.0 0.0 copy-done.3
  83.0 15.1 %finish.1 = f32[4,3072,128]{2,1,0:T(8,128)} custom-call(bf16[768,1536]{1,0:T(8,128)(2,1)} %places.1.refs_0_, bf16[1024,2048]{1,0:T(8,128)(2,1)} %get-tuple-element.16.refs_1_, bf16[768,2048]{1,0:T(8,128)(2,1)} %get-tuple-element.17.refs_2_, bf16[2048,512]{1,0:T(8,128)(2,1)S(1)} %copy-done, bf16[4,3072,128]{2,1,0:T(8,128)(2,1)} %get-tuple-element.21.refs_4_, ...), custom_call_target="tpu_custom_call" | custom-call | tf_op jit(solution)/shard_map/finish/pallas_call | solution.py:458
  (7 shorter events, 0.0 us)
Async XLA Ops:
  3.7 79.3 %all-to-all-start = ((bf16[32,48,1024]{2,1,0:T(8,128)(2,1)}), bf16[32,48,1024]{2,1,0:T(8,128)(2,1)}, u32[]{:S(2)}, u32[]{:S(2)}) async-start(bf16[32,48,1024]{2,1,0:T(8,128)(2,1)} %bitcast.11), calls=%async_computation | async-start | bytes 6291456 | tf_op jit(solution)/shard_map/all_to_all | solution.py:489
  21.6 17.0 %collective-permute-start = (bf16[5,192,128]{2,1,0:T(8,128)(2,1)}, bf16[5,192,128]{2,1,0:T(8,128)(2,1)S(1)}, u32[]{:S(2)}, u32[]{:S(2)}) collective-permute-start(bf16[5,192,128]{2,1,0:T(8,128)(2,1)} %get-tuple-element.19), channel_id=1, source_target_pairs={{0,1},{1,2},{2,3},{3,0},{4,5},{5,6},{6,7},{7,4},{8,9},{9,10},{10,1... | collective-permute-start | bytes 737288 | tf_op jit(solution)/shard_map/ppermute | solution.py:502
  21.8 16.8 %collective-permute-start.1 = (bf16[5,192,128]{2,1,0:T(8,128)(2,1)}, bf16[5,192,128]{2,1,0:T(8,128)(2,1)S(1)}, u32[]{:S(2)}, u32[]{:S(2)}) collective-permute-start(bf16[5,192,128]{2,1,0:T(8,128)(2,1)} %get-tuple-element.20), channel_id=1, source_target_pairs={{1,0},{2,1},{3,2},{0,3},{5,4},{6,5},{7,6},{4,7},{9,8},{10,9},{11,1... | collective-permute-start | bytes 737288 | tf_op jit(solution)/shard_map/ppermute | solution.py:503
  38.6 0.7 copy-start.4
  38.6 0.8 copy-start.5
  39.4 17.2 %copy-start.6 = (s32[768,1]{0,1:T(1,128)S(1)}, s32[768,1]{0,1:T(1,128)}, u32[]{:S(2)}) copy-start(s32[768,1]{0,1:T(1,128)} %param.16) | copy-start | bytes 9220
  48.3 21.1 %collective-permute-start.2 = (bf16[5,32,128]{2,1,0:T(8,128)(2,1)}, bf16[5,32,128]{2,1,0:T(8,128)(2,1)S(1)}, u32[]{:S(2)}, u32[]{:S(2)}) collective-permute-start(bf16[5,32,128]{2,1,0:T(8,128)(2,1)} %get-tuple-element.23), channel_id=1, source_target_pairs={{0,4},{4,8},{8,12},{12,16},{16,20},{20,24},{24,28},{28,0},{1,5},{5... | collective-permute-start | bytes 122888 | tf_op jit(solution)/shard_map/ppermute | solution.py:505
  51.6 17.9 %collective-permute-start.3 = (bf16[5,32,128]{2,1,0:T(8,128)(2,1)}, bf16[5,32,128]{2,1,0:T(8,128)(2,1)S(1)}, u32[]{:S(2)}, u32[]{:S(2)}) collective-permute-start(bf16[5,32,128]{2,1,0:T(8,128)(2,1)} %get-tuple-element.24), channel_id=1, source_target_pairs={{4,0},{8,4},{12,8},{16,12},{20,16},{24,20},{28,24},{0,28},{5,1},{9... | collective-permute-start | bytes 122888 | tf_op jit(solution)/shard_map/ppermute | solution.py:506
  61.5 21.5 %copy-start = (bf16[2048,512]{1,0:T(8,128)(2,1)S(1)}, bf16[2048,512]{1,0:T(8,128)(2,1)}, u32[]{:S(2)}) copy-start(bf16[2048,512]{1,0:T(8,128)(2,1)} %refs_3_.2) | copy-start | bytes 6291460
  61.5 21.5 %copy-start.1 = (f32[5,2,64,128]{3,2,1,0:T(8,128)S(1)}, f32[5,2,64,128]{3,2,1,0:T(8,128)}, u32[]{:S(2)}) copy-start(f32[5,2,64,128]{3,2,1,0:T(8,128)} %get-tuple-element.22.refs_8_) | copy-start | bytes 983044
  61.5 21.5 %copy-start.2 = (bf16[512,128]{1,0:T(8,128)(2,1)S(1)}, bf16[512,128]{1,0:T(8,128)(2,1)}, u32[]{:S(2)}) copy-start(bf16[512,128]{1,0:T(8,128)(2,1)} %constant.14.clone.refs_7_) | copy-start | bytes 393220
  61.5 21.5 %copy-start.3 = (f32[512]{0:T(512)S(1)}, f32[512]{0:T(512)}, u32[]{:S(2)}) copy-start(f32[512]{0:T(512)} %param.20) | copy-start | bytes 6148

commit v4 on v3

--- a/solution.py
+++ b/solution.py
@@ -98,10 +98,10 @@
         vw = x_ref[1, at, :] * w
         for pair in range(0, fields, 2):
             both = (x_ref[pair, at, :], x_ref[pair + 1, at, :])
+            high = jnp.concatenate([x.astype(BF16) for x in both], axis=1)
+            low = jnp.concatenate([(x - x.astype(BF16).astype(F32)).astype(BF16) for x in both], axis=1)
             d = jnp.dot(
-                deriv_ref[...],
-                jnp.concatenate([x.astype(BF16) for x in both], axis=1),
-                preferred_element_type=F32,
+                deriv_ref[...], jnp.concatenate([high, high, low], axis=0), preferred_element_type=F32
             )
             for k, x in enumerate(both):
                 f = pair + k
@@ -145,7 +145,9 @@
     lot = 4
     block = lot * span
     quad = np.tile(row_tables()[12:14].reshape(16, 128), (group // 16, 1))
-    deriv = jnp.asarray(derivative_table(group), BF16)
+    deriv = derivative_table(group)
+    top = deriv.astype(jnp.bfloat16)
+    deriv = jnp.asarray(np.concatenate([top, (deriv - top.astype(np.float64)).astype(jnp.bfloat16), top], axis=1))
     pick = jnp.asarray(pick_table(group, span), BF16)
     edge = jax.ShapeDtypeStruct((fields + 1, rows_a * 8, levels), BF16)
     whole = lambda a: pl.BlockSpec(a.shape, lambda i: (0, 0))
@@ -306,17 +308,15 @@
     before = jnp.where(before, 1.0, 0.0).astype(BF16)
     earlier = jnp.dot(before, hits.astype(BF16), preferred_element_type=F32)
     slot = jnp.sum(hits * earlier, axis=1, keepdims=True).astype(jnp.int32)
-    place = owner * capacity + slot
-    wide = lax.broadcasted_iota(jnp.int32, (cols, devices * capacity), 1)
-    o_ref[...] = jnp.where(place == wide, 1.0, 0.0).astype(BF16)
+    o_ref[...] = owner * capacity + slot
 
 
 def places(owner, devices, capacity):
     return pl.pallas_call(
         lambda a, o: places_body(a, o, devices=devices, capacity=capacity),
-        out_shape=jax.ShapeDtypeStruct((owner.shape[0], devices * capacity), BF16),
+        out_shape=jax.ShapeDtypeStruct(owner.shape, jnp.int32),
         name="places",
-        compiler_params=pltpu.CompilerParams(vmem_limit_bytes=56 << 20),
+        compiler_params=pltpu.CompilerParams(vmem_limit_bytes=60 << 20),
     )(owner)
 
 
@@ -355,12 +355,15 @@
 
 
 def finish_body(
-    sel_hbm, w_hbm, part_hbm, wo_hbm, x_hbm, home_ref, bo_ref, spread_ref, rim_ref, above_ref, below_ref, out_hbm,
-    sel_ref, w_ref, part_ref, wo_ref, x_ref, aux_ref, o_ref, sem, out_sem, *, block
+    place_hbm, home_hbm, w_hbm, part_hbm, wo_hbm, x_hbm, rim_hbm, bo_ref, spread_hbm, above_hbm, below_hbm, out_hbm,
+    place_ref, home_ref, w_ref, part_ref, wo_ref, x_ref, rim_ref, spread_ref, above_ref, below_ref,
+    sel_ref, aux_ref, o_ref, sem, out_sem, *, block
 ):
     fields, rows, levels = x_ref.shape
-    cols = sel_ref.shape[0]
+    cols = place_ref.shape[0]
     steps = cols // block
+    half = home_ref.shape[1] // 2
+    hidden_half = w_ref.shape[1] // 2
 
     copies = {}
 
@@ -371,14 +374,12 @@
     def rows_of(k, scale=1):
         return pl.ds(k * block * scale, block * scale)
 
-    fetch("sel", sel_hbm, sel_ref)
-    fetch("w", w_hbm, w_ref)
-    fetch("part0", part_hbm.at[rows_of(0), :], part_ref.at[rows_of(0), :])
-    fetch("wo", wo_hbm, wo_ref)
-    fetch("x0", x_hbm.at[:, rows_of(0, 4), :], x_ref.at[:, rows_of(0, 4), :])
-    for k in range(1, steps):
-        fetch(f"part{k}", part_hbm.at[rows_of(k), :], part_ref.at[rows_of(k), :])
-        fetch(f"x{k}", x_hbm.at[:, rows_of(k, 4), :], x_ref.at[:, rows_of(k, 4), :])
+    def columns(k, width):
+        return pl.ds(k * width, width)
+
+    fetch("place", place_hbm, place_ref)
+    for k in (0, 1):
+        fetch(f"home{k}", home_hbm.at[:, columns(k, half)], home_ref.at[:, columns(k, half)])
 
     per = rim_ref.shape[2] // 8
     low = lax.broadcasted_iota(jnp.int32, (per // 2, 8, 128), 1) < 4
@@ -401,22 +402,46 @@
             both = jnp.stack([gain, none] if h == 0 else [none, gain], axis=1)
             o_ref[f, to, :] = o_ref[f, to, :] + both.reshape(per * 16, 128)
 
-    copies["sel"].wait()
-    aux_ref[...] = jnp.dot(sel_ref[...], home_ref[...], preferred_element_type=F32).astype(BF16)
-    copies["w"].wait()
+    copies["place"].wait()
+    wide = lax.broadcasted_iota(jnp.int32, (block, sel_ref.shape[1]), 1)
+    for k in range(steps):
+        sel_ref[rows_of(k), :] = jnp.where(place_ref[rows_of(k), :] == wide, 1.0, 0.0).astype(BF16)
+    for k in (0, 1):
+        copies[f"home{k}"].wait()
+        if k == 0:
+            for n in (0, 1):
+                fetch(f"w{n}", w_hbm.at[:, columns(n, hidden_half)], w_ref.at[:, columns(n, hidden_half)])
+            fetch("part0", part_hbm.at[rows_of(0), :], part_ref.at[rows_of(0), :])
+            fetch("wo", wo_hbm, wo_ref)
+        else:
+            fetch("spread", spread_hbm, spread_ref)
+            fetch("x0", x_hbm.at[:, rows_of(0, 4), :], x_ref.at[:, rows_of(0, 4), :])
+            fetch("rim", rim_hbm, rim_ref)
+            fetch("above", above_hbm, above_ref)
+            fetch("below", below_hbm, below_ref)
+            for m in range(1, steps):
+                fetch(f"part{m}", part_hbm.at[rows_of(m), :], part_ref.at[rows_of(m), :])
+                fetch(f"x{m}", x_hbm.at[:, rows_of(m, 4), :], x_ref.at[:, rows_of(m, 4), :])
+        aux_ref[:, k * half : (k + 1) * half] = jnp.dot(
+            sel_ref[...], home_ref[:, k * half : (k + 1) * half], preferred_element_type=F32
+        ).astype(BF16)
     group = spread_ref.shape[1]
     outs = []
     for k in range(steps):
         at = rows_of(k)
         copies[f"part{k}"].wait()
+        if k == 0:
+            for name in ("w0", "w1", "wo"):
+                copies[name].wait()
         v = part_ref[at, :].astype(F32) + jnp.dot(aux_ref[at, :], w_ref[...], preferred_element_type=F32)
-        half = 0.5 * v
-        hidden = (half + half * jnp.tanh(half)).astype(BF16)
-        if k == 0:
-            copies["wo"].wait()
+        v = 0.5 * v
+        hidden = (v + v * jnp.tanh(v)).astype(BF16)
         inc = jnp.dot(hidden, wo_ref[...], preferred_element_type=F32) + bo_ref[...]
         inc = inc.astype(BF16)
         copies[f"x{k}"].wait()
+        if k == 0:
+            for name in ("spread", "rim", "above", "below"):
+                copies[name].wait()
         for g in range(block // group):
             wide = jnp.dot(
                 spread_ref[...], inc[g * group : (g + 1) * group], preferred_element_type=F32
@@ -445,33 +470,31 @@
     return spread
 
 
-def finish(sel, home, weight, part, weight_out, bias_out, x, rim, above, below):
-    cols = sel.shape[0]
+def finish(place, home, weight, part, weight_out, bias_out, x, rim, above, below):
+    cols, slots = place.shape[0], home.shape[0]
     fields, rows, levels = x.shape
     block = 256
     steps = cols // block
     spread = jnp.asarray(spread_table(128), BF16)
     far = pl.BlockSpec(memory_space=pltpu.HBM)
-    full = lambda a: pl.BlockSpec(a.shape, lambda: (0,) * a.ndim)
-    large = (sel, weight, part, weight_out, x)
-    small = (home, bias_out, spread, rim, above, below)
+    first = (place, home, weight, part, weight_out, x, rim)
+    after = (spread, above, below)
     return pl.pallas_call(
         lambda *refs: finish_body(*refs, block=block),
-        in_specs=[far] * len(large)
-        + [pl.BlockSpec(memory_space=pltpu.VMEM)]
-        + [full(a) for a in small[1:]],
+        in_specs=[far] * len(first) + [pl.BlockSpec(bias_out.shape, lambda: (0, 0))] + [far] * len(after),
         out_specs=far,
         out_shape=jax.ShapeDtypeStruct(x.shape, F32),
-        scratch_shapes=[pltpu.VMEM(a.shape, a.dtype) for a in large]
+        scratch_shapes=[pltpu.VMEM(a.shape, a.dtype) for a in (*first, *after)]
         + [
+            pltpu.VMEM((cols, slots), BF16),
             pltpu.VMEM((cols, home.shape[1]), BF16),
             pltpu.VMEM(x.shape, F32),
-            pltpu.SemaphoreType.DMA((3 + 2 * steps,)),
+            pltpu.SemaphoreType.DMA((10 + 2 * steps,)),
             pltpu.SemaphoreType.DMA((steps,)),
         ],
         name="finish",
-        compiler_params=pltpu.CompilerParams(vmem_limit_bytes=50 << 20),
-    )(*large, *small)
+        compiler_params=pltpu.CompilerParams(vmem_limit_bytes=52 << 20),
+    )(*first, bias_out, *after)
 
 
 def shards(
@@ -505,9 +528,9 @@
     above = lax.ppermute(tail, "curve", ahead(n_curve))
     below = lax.ppermute(head, "curve", back(n_curve))
 
-    sel = places(group_owner, devices, capacity)
+    place = places(group_owner, devices, capacity)
     part, weight_aux = first_part(state, weight_in, bias_in[None], padded)
-    out = finish(sel, home, weight_aux, part, weight_out, bias_out[None], section, rim, above, below)
+    out = finish(place, home, weight_aux, part, weight_out, bias_out[None], section, rim, above, below)
     return out.reshape(prognostic.shape)
 
 

time: 98.6 us -> 96.9 us (0.983)
  waiting for transfers between devices: 28.7 us -> 23.8 us
  Pallas kernels: 50.1 us -> 53.2 us
    pallas_call x1, Pallas kernels: 10.5 us -> 16.8 us  [tendencies(): pl.pallas_call(tend_body, grid=(rows // block,), in_specs=[pl.BlockSpec((...]
    ppermute x1, waiting for transfers between devices: 15.2 us -> 8.98 us  [shards(): left = lax.ppermute(right_out, 'sub', ahead(n_sub))]
    pallas_call x1, Pallas kernels: 3.95 us -> 2.42 us  [places(): pl.pallas_call(lambda a, o: places_body(a, o, devices=devices, capacity=c...]
    pallas_call x1, Pallas kernels: 15.1 us -> 13.6 us  [finish(): pl.pallas_call(lambda *refs: finish_body(*refs, block=block), in_specs=[f...]
  transfers between devices with their start and end apart: 5 -> 5, of which waited for: 2 -> 3; matrix products, arithmetic and copies ran while one was open for 1% -> 1% of each run, Pallas kernels for 32% -> 37%
where the time goes in v4:
time: 96.9 us; the launch traced here: 96.5 us
  Pallas kernels  53.2 us (55%)
  waiting for transfers between devices  23.8 us (25%)
  starting transfers between devices  17.7 us (18%)
  local copies, waits for them, and re-layouts  1.79 us (2%)
    pallas_call x1, Pallas kernels, tendencies(): pl.pallas_call(tend_body, grid=(rows // block,), in_specs=[pl.BlockSpec((...  16.8 us
    all_to_all x1, waiting for transfers between devices, shards(): home = lax.all_to_all(home, AXES, split_axis=0, concat_axis=0, tiled=True)  14.1 us
    pallas_call x1, Pallas kernels, finish(): pl.pallas_call(lambda *refs: finish_body(*refs, block=block), in_specs=[f...  13.6 us
    ppermute x1, waiting for transfers between devices, shards(): left = lax.ppermute(right_out, 'sub', ahead(n_sub))  8.98 us
    pallas_call x1, Pallas kernels, section_of(): pl.pallas_call(lambda *refs: section_body(*refs, per=per), grid=(fields,)...  8.85 us
    pallas_call x1, Pallas kernels, first_part(): pl.pallas_call(first_body, grid=(hidden // block,), in_specs=[pl.BlockSpe...  7.91 us
    all_to_all x1, starting transfers between devices, shards(): home = lax.all_to_all(home, AXES, split_axis=0, concat_axis=0, tiled=True)  7.44 us
    ppermute x1, starting transfers between devices, shards(): below = lax.ppermute(head, 'curve', back(n_curve))  4.96 us
  transfers between devices with their start and end apart: 5, of which 3 were waited for; matrix products, arithmetic and copies ran while one was open for 1% of the time, Pallas kernels for 37%

profile of v4, /device:TPU:0, one launch (start us, length us, event | category | flops | bytes accessed | tf_op | source)
XLA Modules:
  0.0 96.5 jit_solution(10361307095599407086)
XLA Ops:
  0.0 3.6 %turn.1 = bf16[1536,1024]{1,0:T(8,128)(2,1)} custom-call(bf16[1013,1536]{1,0:T(8,128)(2,1)} %bitcast.14), custom_call_target="tpu_custom_call" | custom-call | tf_op jit(solution)/shard_map/turn/pallas_call | solution.py:63
  3.6 7.4 %all-to-all-start = ((bf16[32,48,1024]{2,1,0:T(8,128)(2,1)}), bf16[32,48,1024]{2,1,0:T(8,128)(2,1)}, u32[]{:S(2)}, u32[]{:S(2)}) async-start(bf16[32,48,1024]{2,1,0:T(8,128)(2,1)} %bitcast.11), calls=%async_computation | async-start | bytes 6291456 | tf_op jit(solution)/shard_map/all_to_all | solution.py:512
  11.1 16.8 %tendencies.1 = (bf16[4,3072,128]{2,1,0:T(8,128)(2,1)}, bf16[768,512]{1,0:T(8,128)(2,1)}, bf16[5,192,128]{2,1,0:T(8,128)(2,1)}, bf16[5,192,128]{2,1,0:T(8,128)(2,1)}) custom-call(f32[4,3072,128]{2,1,0:T(8,128)} %bitcast.9, f32[3072,128]{1,0:T(8,128)} %bitcast.12, f32[256,128]{1,0:T(8,128)} %constant.12.clone.q_ref, ...), custom_call_target="tpu_custom_call" | custom-call | tf_op jit(solution)/shard_map/tendencies/pallas_call | solution.py:154
  27.8 0.2 collective-permute-start
  28.0 1.6 %collective-permute-start.1 = (bf16[5,192,128]{2,1,0:T(8,128)(2,1)}, bf16[5,192,128]{2,1,0:T(8,128)(2,1)S(1)}, u32[]{:S(2)}, u32[]{:S(2)}) collective-permute-start(bf16[5,192,128]{2,1,0:T(8,128)(2,1)} %get-tuple-element.20), channel_id=1, source_target_pairs={{1,0},{2,1},{3,2},{0,3},{5,4},{6,5},{7,6},{4,7},{9,8},{10,9},{11,1... | collective-permute-start | bytes 737288 | tf_op jit(solution)/shard_map/ppermute | solution.py:526
  29.6 9.0 %collective-permute-done.refs_4_ = bf16[5,192,128]{2,1,0:T(8,128)(2,1)S(1)} collective-permute-done((bf16[5,192,128]{2,1,0:T(8,128)(2,1)}, bf16[5,192,128]{2,1,0:T(8,128)(2,1)S(1)}, u32[]{:S(2)}, u32[]{:S(2)}) %collective-permute-start) | collective-permute-done | bytes 245792 | tf_op jit(solution)/shard_map/ppermute | solution.py:525
  38.6 0.0 collective-permute-done.1.refs_5_
  38.6 0.7 copy-done.4
  39.3 0.1 copy-done.5
  39.4 8.9 %section.1 = (bf16[4,3072,128]{2,1,0:T(8,128)(2,1)}, f32[5,2,64,128]{3,2,1,0:T(8,128)}, bf16[5,32,128]{2,1,0:T(8,128)(2,1)}, bf16[5,32,128]{2,1,0:T(8,128)(2,1)}) custom-call(bf16[4,3072,128]{2,1,0:T(8,128)(2,1)} %get-tuple-element.18.refs_0_, f32[4,3072,128]{2,1,0:T(8,128)} %bitcast.10, f32[3072,128]{1,0:T(8,128)} %bitcast.13, ...), custom_call_target="tpu_custom_call" | custom-call | tf_op jit(solution)/shard_map/section/pallas_call | solution.py:277
  48.3 3.5 %collective-permute-start.2 = (bf16[5,32,128]{2,1,0:T(8,128)(2,1)}, bf16[5,32,128]{2,1,0:T(8,128)(2,1)S(1)}, u32[]{:S(2)}, u32[]{:S(2)}) collective-permute-start(bf16[5,32,128]{2,1,0:T(8,128)(2,1)} %get-tuple-element.23), channel_id=1, source_target_pairs={{0,4},{4,8},{8,12},{12,16},{16,20},{20,24},{24,28},{28,0},{1,5},{5... | collective-permute-start | bytes 122888 | tf_op jit(solution)/shard_map/ppermute | solution.py:528
  51.8 5.0 %collective-permute-start.3 = (bf16[5,32,128]{2,1,0:T(8,128)(2,1)}, bf16[5,32,128]{2,1,0:T(8,128)(2,1)S(1)}, u32[]{:S(2)}, u32[]{:S(2)}) collective-permute-start(bf16[5,32,128]{2,1,0:T(8,128)(2,1)} %get-tuple-element.24), channel_id=1, source_target_pairs={{4,0},{8,4},{12,8},{16,12},{20,16},{24,20},{28,24},{0,28},{5,1},{9... | collective-permute-start | bytes 122888 | tf_op jit(solution)/shard_map/ppermute | solution.py:529
  56.7 0.0 copy-done.6
  56.7 1.0 copy.14.a
  57.7 2.4 %places.1.refs_0_ = s32[768,1]{1,0:T(8,128)} custom-call(s32[768,1]{1,0:T(8,128)} %copy.14.a), custom_call_target="tpu_custom_call" | custom-call | tf_op jit(solution)/shard_map/places/pallas_call | solution.py:315
  60.1 7.9 %first_part.1 = (bf16[768,2048]{1,0:T(8,128)(2,1)}, bf16[1024,2048]{1,0:T(8,128)(2,1)}) custom-call(bf16[768,512]{1,0:T(8,128)(2,1)} %get-tuple-element.15.s_ref, bf16[1525,2048]{1,0:T(8,128)(2,1)} %w_ref.1, f32[1,2048]{1,0:T(1,128)} %bitcast.15), custom_call_target="tpu_custom_call" | custom-call | tf_op jit(solution)/shard_map/first_part/pallas_call | solution.py:336
  68.0 0.8 collective-permute-done.2.refs_9_
  68.8 0.0 collective-permute-done.3.refs_10_
  68.8 14.1 %all-to-all-done = bf16[32,48,1024]{2,1,0:T(8,128)(2,1)} async-done(((bf16[32,48,1024]{2,1,0:T(8,128)(2,1)}), bf16[32,48,1024]{2,1,0:T(8,128)(2,1)}, u32[]{:S(2)}, u32[]{:S(2)}) %all-to-all-start) | async-done | bytes 3145760 | tf_op jit(solution)/shard_map/all_to_all | solution.py:512
  82.9 0.0 copy-done
  82.9 0.0 copy-done.1
  82.9 0.0 copy-done.2
  82.9 0.0 copy-done.3
  82.9 13.6 %finish.1 = f32[4,3072,128]{2,1,0:T(8,128)} custom-call(s32[768,1]{1,0:T(8,128)S(1)} %copy-done, bf16[1536,1024]{1,0:T(8,128)(2,1)} %bitcast.2.refs_1_, bf16[1024,2048]{1,0:T(8,128)(2,1)} %get-tuple-element.16.refs_2_, bf16[768,2048]{1,0:T(8,128)(2,1)} %get-tuple-element.17.refs_3_, bf16[2048,512]{1,0:T(8,128)(2,1)} %refs_4_.1, ...), custom_call_target="tpu_custom_call" | custom-call | tf_op jit(solution)/shard_map/finish/pallas_call | solution.py:482
  (7 shorter events, 0.0 us)
Async XLA Ops:
  3.6 79.3 %all-to-all-start = ((bf16[32,48,1024]{2,1,0:T(8,128)(2,1)}), bf16[32,48,1024]{2,1,0:T(8,128)(2,1)}, u32[]{:S(2)}, u32[]{:S(2)}) async-start(bf16[32,48,1024]{2,1,0:T(8,128)(2,1)} %bitcast.11), calls=%async_computation | async-start | bytes 6291456 | tf_op jit(solution)/shard_map/all_to_all | solution.py:512
  27.8 10.7 %collective-permute-start = (bf16[5,192,128]{2,1,0:T(8,128)(2,1)}, bf16[5,192,128]{2,1,0:T(8,128)(2,1)S(1)}, u32[]{:S(2)}, u32[]{:S(2)}) collective-permute-start(bf16[5,192,128]{2,1,0:T(8,128)(2,1)} %get-tuple-element.19), channel_id=1, source_target_pairs={{0,1},{1,2},{2,3},{3,0},{4,5},{5,6},{6,7},{7,4},{8,9},{9,10},{10,1... | collective-permute-start | bytes 737288 | tf_op jit(solution)/shard_map/ppermute | solution.py:525
  28.0 10.5 %collective-permute-start.1 = (bf16[5,192,128]{2,1,0:T(8,128)(2,1)}, bf16[5,192,128]{2,1,0:T(8,128)(2,1)S(1)}, u32[]{:S(2)}, u32[]{:S(2)}) collective-permute-start(bf16[5,192,128]{2,1,0:T(8,128)(2,1)} %get-tuple-element.20), channel_id=1, source_target_pairs={{1,0},{2,1},{3,2},{0,3},{5,4},{6,5},{7,6},{4,7},{9,8},{10,9},{11,1... | collective-permute-start | bytes 737288 | tf_op jit(solution)/shard_map/ppermute | solution.py:526
  38.6 0.7 copy-start.4
  38.6 0.8 copy-start.5
  39.4 17.3 %copy-start.6 = (s32[768,1]{0,1:T(1,128)S(1)}, s32[768,1]{0,1:T(1,128)}, u32[]{:S(2)}) copy-start(s32[768,1]{0,1:T(1,128)} %param.16) | copy-start | bytes 9220
  48.3 20.5 %collective-permute-start.2 = (bf16[5,32,128]{2,1,0:T(8,128)(2,1)}, bf16[5,32,128]{2,1,0:T(8,128)(2,1)S(1)}, u32[]{:S(2)}, u32[]{:S(2)}) collective-permute-start(bf16[5,32,128]{2,1,0:T(8,128)(2,1)} %get-tuple-element.23), channel_id=1, source_target_pairs={{0,4},{4,8},{8,12},{12,16},{16,20},{20,24},{24,28},{28,0},{1,5},{5... | collective-permute-start | bytes 122888 | tf_op jit(solution)/shard_map/ppermute | solution.py:528
  51.8 17.0 %collective-permute-start.3 = (bf16[5,32,128]{2,1,0:T(8,128)(2,1)}, bf16[5,32,128]{2,1,0:T(8,128)(2,1)S(1)}, u32[]{:S(2)}, u32[]{:S(2)}) collective-permute-start(bf16[5,32,128]{2,1,0:T(8,128)(2,1)} %get-tuple-element.24), channel_id=1, source_target_pairs={{4,0},{8,4},{12,8},{16,12},{20,16},{24,20},{28,24},{0,28},{5,1},{9... | collective-permute-start | bytes 122888 | tf_op jit(solution)/shard_map/ppermute | solution.py:529
  60.1 22.8 %copy-start = (s32[768,1]{1,0:T(8,128)S(1)}, s32[768,1]{1,0:T(8,128)}, u32[]{:S(2)}) copy-start(s32[768,1]{1,0:T(8,128)} %places.1.refs_0_) | copy-start | bytes 9220
  60.1 22.8 %copy-start.1 = (f32[5,2,64,128]{3,2,1,0:T(8,128)S(1)}, f32[5,2,64,128]{3,2,1,0:T(8,128)}, u32[]{:S(2)}) copy-start(f32[5,2,64,128]{3,2,1,0:T(8,128)} %get-tuple-element.22.refs_6_) | copy-start | bytes 983044
  60.1 22.8 %copy-start.2 = (bf16[512,128]{1,0:T(8,128)(2,1)S(1)}, bf16[512,128]{1,0:T(8,128)(2,1)}, u32[]{:S(2)}) copy-start(bf16[512,128]{1,0:T(8,128)(2,1)} %constant.14.clone.refs_8_) | copy-start | bytes 393220
  60.1 22.8 %copy-start.3 = (f32[512]{0:T(512)S(1)}, f32[512]{0:T(512)}, u32[]{:S(2)}) copy-start(f32[512]{0:T(512)} %param.20) | copy-start | bytes 6148

commit v5 on v4

--- a/solution.py
+++ b/solution.py
@@ -179,7 +179,7 @@
 
 
 def section_body(
-    t_ref, x_ref, m_ref, q_ref, left_ref, right_ref, o_ref, rim_ref, head_ref, tail_ref, inv_ref, *, per
+    t_ref, x_ref, m_ref, q_ref, left_ref, right_ref, o_ref, head_ref, tail_ref, inv_ref, rim_ref, *, per
 ):
     rows = x_ref.shape[1]
     span = per * 16
@@ -214,8 +214,12 @@
         return result
 
     def rims(k, p0, p1):
-        rim_ref[k, 0] = p0.reshape(per * 8, 128)
-        rim_ref[k, 1] = p1.reshape(per * 8, 128)
+        both = jnp.concatenate([p0.reshape(per * 8, 128), p1.reshape(per * 8, 128)], axis=0).astype(BF16)
+        if isinstance(k, int):
+            rim_ref[...] = both
+        else:
+            o_ref[0, rows : rows + per * 16, :] = both
+            o_ref[0, rows + per * 16 :, :] = rim_ref[...]
         p0 = p0.reshape(per // 2, 2, 8, 128)
         p1 = p1.reshape(per // 2, 2, 8, 128)
         half = low[: per // 2]
@@ -273,28 +277,25 @@
     quad = jnp.asarray(row_tables()[12:14])
     one = pl.BlockSpec((1, rows, levels), lambda f: (f, 0, 0))
     edge = jax.ShapeDtypeStruct((fields + 1, per * 4, levels), BF16)
-    rim = jax.ShapeDtypeStruct((fields + 1, 2, per * 8, levels), F32)
-    section, rim, head, tail = pl.pallas_call(
+    tall = rows + per * 32
+    return pl.pallas_call(
         lambda *refs: section_body(*refs, per=per),
         grid=(fields,),
         in_specs=[one, one] + [whole(a) for a in (mass, quad, left, right)],
         out_specs=[
-            one,
-            whole(rim),
+            pl.BlockSpec((1, tall, levels), lambda f: (f, 0, 0)),
             whole(edge),
             whole(edge),
         ],
         out_shape=[
-            jax.ShapeDtypeStruct(x.shape, BF16),
-            rim,
+            jax.ShapeDtypeStruct((fields, tall, levels), BF16),
             edge,
             edge,
         ],
-        scratch_shapes=[pltpu.VMEM((rows, levels), F32)],
+        scratch_shapes=[pltpu.VMEM((rows, levels), F32), pltpu.VMEM((per * 16, levels), BF16)],
         name="section",
         compiler_params=pltpu.CompilerParams(vmem_limit_bytes=56 << 20),
     )(t, x, mass, quad, left, right)
-    return section, rim, head, tail
 
 
 def places_body(owner_ref, o_ref, *, devices, capacity):
@@ -320,68 +321,83 @@
     )(owner)
 
 
-def first_body(s_ref, w_ref, b_ref, o_ref, w2_ref):
+def first_body(s_ref, w_ref, b_ref, wo_ref, o_ref, w2_ref, *, padded):
     width = s_ref.shape[1]
     rest = w_ref.shape[0] - width
     y = jnp.dot(s_ref[...], w_ref[:width, :], preferred_element_type=F32) + b_ref[...]
     o_ref[...] = y.astype(BF16)
     w2_ref[:rest, :] = w_ref[width:, :]
-    w2_ref[rest:, :] = jnp.zeros((w2_ref.shape[0] - rest, w2_ref.shape[1]), BF16)
-
-
-def first_part(state, weight, bias, padded):
+    w2_ref[rest:padded, :] = jnp.zeros((padded - rest, w2_ref.shape[1]), BF16)
+    w2_ref[padded:, :] = wo_ref[...]
+
+
+def first_part(state, weight, bias, weight_out, padded):
     cols, width = state.shape
     depth, hidden = weight.shape
-    block = 512
+    block = weight_out.shape[1]
+    tall = padded + block
     return pl.pallas_call(
-        first_body,
+        lambda *refs: first_body(*refs, padded=padded),
         grid=(hidden // block,),
         in_specs=[
             pl.BlockSpec((cols, width), lambda i: (0, 0)),
             pl.BlockSpec((depth, block), lambda i: (0, i)),
             pl.BlockSpec((1, block), lambda i: (0, i)),
+            pl.BlockSpec((block, block), lambda i: (i, 0)),
         ],
         out_specs=[
             pl.BlockSpec((cols, block), lambda i: (0, i)),
-            pl.BlockSpec((padded, block), lambda i: (0, i)),
+            pl.BlockSpec((tall, block), lambda i: (0, i)),
         ],
         out_shape=[
             jax.ShapeDtypeStruct((cols, hidden), BF16),
-            jax.ShapeDtypeStruct((padded, hidden), BF16),
+            jax.ShapeDtypeStruct((tall, hidden), BF16),
         ],
         name="first_part",
         compiler_params=pltpu.CompilerParams(vmem_limit_bytes=56 << 20),
-    )(state, weight, bias)
+    )(state, weight, bias, weight_out)
 
 
 def finish_body(
-    place_hbm, home_hbm, w_hbm, part_hbm, wo_hbm, x_hbm, rim_hbm, bo_ref, spread_hbm, above_hbm, below_hbm, out_hbm,
-    place_ref, home_ref, w_ref, part_ref, wo_ref, x_ref, rim_ref, spread_ref, above_ref, below_ref,
-    sel_ref, aux_ref, o_ref, sem, out_sem, *, block
+    home_ref, place_ref, w_hbm, part_hbm, bo_ref, x_hbm, above_ref, below_ref, out_hbm,
+    w_ref, part_ref, x_ref, sel_ref, aux_ref, spread_ref, o_ref, sem, out_sem, *, block
 ):
-    fields, rows, levels = x_ref.shape
+    fields, rows, levels = o_ref.shape
     cols = place_ref.shape[0]
+    per = above_ref.shape[1] // 4
+    edge_rows = pl.ds(rows, per * 32)
     steps = cols // block
     half = home_ref.shape[1] // 2
     hidden_half = w_ref.shape[1] // 2
 
-    copies = {}
-
-    def fetch(name, src, dst):
-        copies[name] = pltpu.make_async_copy(src, dst, sem.at[len(copies)])
-        copies[name].start()
-
     def rows_of(k, scale=1):
         return pl.ds(k * block * scale, block * scale)
 
     def columns(k, width):
         return pl.ds(k * width, width)
 
-    fetch("place", place_hbm, place_ref)
-    for k in (0, 1):
-        fetch(f"home{k}", home_hbm.at[:, columns(k, half)], home_ref.at[:, columns(k, half)])
-
-    per = rim_ref.shape[2] // 8
+    def jobs():
+        for k in (0, 1):
+            yield f"w{k}", w_hbm.at[:, columns(k, hidden_half)], w_ref.at[:, columns(k, hidden_half)]
+        yield "edge", x_hbm.at[:, edge_rows, :], x_ref.at[:, edge_rows, :]
+        for k in range(steps):
+            yield f"part{k}", part_hbm.at[rows_of(k), :], part_ref.at[rows_of(k), :]
+            yield f"x{k}", x_hbm.at[:, rows_of(k, 4), :], x_ref.at[:, rows_of(k, 4), :]
+
+    def each(names, act):
+        for n, (name, src, dst) in enumerate(jobs()):
+            if name in names:
+                act(pltpu.make_async_copy(src, dst, sem.at[n]))
+
+    def fetch(*names):
+        each(names, lambda copy: copy.start())
+
+    def wait(*names):
+        each(names, lambda copy: copy.wait())
+
+    later = [f"{kind}{k}" for k in range(1, steps) for kind in ("part", "x")]
+    fetch("w0", "w1", "part0", "edge", "x0", *later)
+
     low = lax.broadcasted_iota(jnp.int32, (per // 2, 8, 128), 1) < 4
 
     def patch(h, halo, start):
@@ -392,7 +408,9 @@
                 add = jnp.stack([jnp.where(low, p, 0.0), jnp.where(low, q, 0.0)], axis=1)
             else:
                 add = jnp.stack([jnp.where(low, 0.0, q), jnp.where(low, 0.0, p)], axis=1)
-            return rim_ref[k, h].reshape(per, 8, 128) + add.reshape(per, 8, 128)
+            own = pl.ds(rows + (per * 16 if k == fields else 0) + h * per * 8, per * 8)
+            own = x_ref[0 if k == fields else k, own, :].astype(F32)
+            return own.reshape(per, 8, 128) + add.reshape(per, 8, 128)
 
         scale = section_step / total(fields)
         to = pl.ds(start, per * 16)
@@ -402,99 +420,101 @@
             both = jnp.stack([gain, none] if h == 0 else [none, gain], axis=1)
             o_ref[f, to, :] = o_ref[f, to, :] + both.reshape(per * 16, 128)
 
-    copies["place"].wait()
     wide = lax.broadcasted_iota(jnp.int32, (block, sel_ref.shape[1]), 1)
     for k in range(steps):
         sel_ref[rows_of(k), :] = jnp.where(place_ref[rows_of(k), :] == wide, 1.0, 0.0).astype(BF16)
-    for k in (0, 1):
-        copies[f"home{k}"].wait()
-        if k == 0:
-            for n in (0, 1):
-                fetch(f"w{n}", w_hbm.at[:, columns(n, hidden_half)], w_ref.at[:, columns(n, hidden_half)])
-            fetch("part0", part_hbm.at[rows_of(0), :], part_ref.at[rows_of(0), :])
-            fetch("wo", wo_hbm, wo_ref)
-        else:
-            fetch("spread", spread_hbm, spread_ref)
-            fetch("x0", x_hbm.at[:, rows_of(0, 4), :], x_ref.at[:, rows_of(0, 4), :])
-            fetch("rim", rim_hbm, rim_ref)
-            fetch("above", above_hbm, above_ref)
-            fetch("below", below_hbm, below_ref)
-            for m in range(1, steps):
-                fetch(f"part{m}", part_hbm.at[rows_of(m), :], part_ref.at[rows_of(m), :])
-                fetch(f"x{m}", x_hbm.at[:, rows_of(m, 4), :], x_ref.at[:, rows_of(m, 4), :])
-        aux_ref[:, k * half : (k + 1) * half] = jnp.dot(
-            sel_ref[...], home_ref[:, k * half : (k + 1) * half], preferred_element_type=F32
+    def gather(k, carry):
+        lanes = pl.ds(pl.multiple_of(k * half, 128), half)
+        aux_ref[:, lanes] = jnp.dot(
+            sel_ref[...], home_ref[:, lanes], preferred_element_type=F32
         ).astype(BF16)
-    group = spread_ref.shape[1]
-    outs = []
-    for k in range(steps):
-        at = rows_of(k)
-        copies[f"part{k}"].wait()
-        if k == 0:
-            for name in ("w0", "w1", "wo"):
-                copies[name].wait()
-        v = part_ref[at, :].astype(F32) + jnp.dot(aux_ref[at, :], w_ref[...], preferred_element_type=F32)
+        return carry
+
+    lax.fori_loop(0, 2, gather, 0)
+    group = 128
+    row = lax.broadcasted_iota(jnp.int32, (group * 4, group), 0)
+    cell = (row // 16) * 4 + ((row // 8) % 2) * 2 + (row % 4) // 2
+    spread = jnp.where(cell == lax.broadcasted_iota(jnp.int32, cell.shape, 1), 1.0, 0.0).astype(BF16)
+    spread_ref[...] = spread
+    padded = home_ref.shape[1]
+    width = bo_ref.shape[1]
+    wait("w0", "w1", "part0", "edge")
+
+    def out_copy(k):
+        at = pl.ds(pl.multiple_of(k * block * 4, block * 4), block * 4)
+        return pltpu.make_async_copy(o_ref.at[:, at, :], out_hbm.at[:, at, :], out_sem.at[k])
+
+    def layers(k, carry):
+        at = pl.ds(pl.multiple_of(k * block, block), block)
+
+        @pl.when(k == 1)
+        def _():
+            wait(*[f"part{m}" for m in range(1, steps)])
+
+        v = part_ref[at, :].astype(F32) + jnp.dot(
+            aux_ref[at, :], w_ref[:padded, :], preferred_element_type=F32
+        )
         v = 0.5 * v
         hidden = (v + v * jnp.tanh(v)).astype(BF16)
-        inc = jnp.dot(hidden, wo_ref[...], preferred_element_type=F32) + bo_ref[...]
+        inc = bo_ref[...]
+        for n in range(hidden.shape[1] // width):
+            lanes = slice(n * width, (n + 1) * width)
+            inc = inc + jnp.dot(hidden[:, lanes], w_ref[padded:, lanes], preferred_element_type=F32)
         inc = inc.astype(BF16)
-        copies[f"x{k}"].wait()
-        if k == 0:
-            for name in ("spread", "rim", "above", "below"):
-                copies[name].wait()
+
+        @pl.when(k == 0)
+        def _():
+            wait(*[f"x{m}" for m in range(steps)])
+
         for g in range(block // group):
             wide = jnp.dot(
                 spread_ref[...], inc[g * group : (g + 1) * group], preferred_element_type=F32
             )
-            to = pl.ds((k * block + g * group) * 4, group * 4)
+            to = pl.ds(pl.multiple_of((k * block + g * group) * 4, group * 4), group * 4)
             for f in range(fields):
                 o_ref[f, to, :] = x_ref[f, to, :].astype(F32) + wide[:, f * levels : (f + 1) * levels]
-        if k == 0:
+
+        @pl.when(k == 0)
+        def _():
             patch(0, above_ref, 0)
-        if k == steps - 1:
+
+        @pl.when(k == steps - 1)
+        def _():
             patch(1, below_ref, rows - per * 16)
-        done = pltpu.make_async_copy(
-            o_ref.at[:, rows_of(k, 4), :], out_hbm.at[:, rows_of(k, 4), :], out_sem.at[k]
-        )
-        done.start()
-        outs.append(done)
-    for done in outs:
-        done.wait()
-
-
-def spread_table(group):
-    spread = np.zeros((group * 4, group), np.float32)
-    for r in range(group * 4):
-        e, i, j = r // 16, (r // 4) % 4, r % 4
-        spread[r, e * 4 + (i // 2) * 2 + j // 2] = 1.0
-    return spread
-
-
-def finish(place, home, weight, part, weight_out, bias_out, x, rim, above, below):
+
+        out_copy(k).start()
+        return carry
+
+    lax.fori_loop(0, steps, layers, 0)
+    for k in range(steps):
+        out_copy(k).wait()
+
+
+def finish(home, place, weights, part, bias_out, x, above, below):
     cols, slots = place.shape[0], home.shape[0]
-    fields, rows, levels = x.shape
-    block = 256
+    fields, levels = x.shape[0], x.shape[2]
+    result = (fields, cols * 4, levels)
+    block = 384
     steps = cols // block
-    spread = jnp.asarray(spread_table(128), BF16)
-    far = pl.BlockSpec(memory_space=pltpu.HBM)
-    first = (place, home, weight, part, weight_out, x, rim)
-    after = (spread, above, below)
+    far = pl.BlockSpec(memory_space=pl.ANY)
+    near = pl.BlockSpec(memory_space=pltpu.VMEM)
     return pl.pallas_call(
         lambda *refs: finish_body(*refs, block=block),
-        in_specs=[far] * len(first) + [pl.BlockSpec(bias_out.shape, lambda: (0, 0))] + [far] * len(after),
+        in_specs=[near, near, far, far, near, far, near, near],
         out_specs=far,
-        out_shape=jax.ShapeDtypeStruct(x.shape, F32),
-        scratch_shapes=[pltpu.VMEM(a.shape, a.dtype) for a in (*first, *after)]
+        out_shape=jax.ShapeDtypeStruct(result, F32),
+        scratch_shapes=[pltpu.VMEM(a.shape, a.dtype) for a in (weights, part, x)]
         + [
             pltpu.VMEM((cols, slots), BF16),
             pltpu.VMEM((cols, home.shape[1]), BF16),
-            pltpu.VMEM(x.shape, F32),
-            pltpu.SemaphoreType.DMA((10 + 2 * steps,)),
+            pltpu.VMEM((512, 128), BF16),
+            pltpu.VMEM(result, F32),
+            pltpu.SemaphoreType.DMA((3 + 2 * steps,)),
             pltpu.SemaphoreType.DMA((steps,)),
         ],
         name="finish",
-        compiler_params=pltpu.CompilerParams(vmem_limit_bytes=52 << 20),
-    )(*first, bias_out, *after)
+        compiler_params=pltpu.CompilerParams(vmem_limit_bytes=48 << 20),
+    )(home, place, weights, part, bias_out, x, above, below)
 
 
 def shards(
@@ -524,13 +544,13 @@
 
     left = lax.ppermute(right_out, "sub", ahead(n_sub))
     right = lax.ppermute(left_out, "sub", back(n_sub))
-    section, rim, head, tail = section_of(tend, x, mass, left, right, rows_a)
+    section, head, tail = section_of(tend, x, mass, left, right, rows_a)
     above = lax.ppermute(tail, "curve", ahead(n_curve))
     below = lax.ppermute(head, "curve", back(n_curve))
 
     place = places(group_owner, devices, capacity)
-    part, weight_aux = first_part(state, weight_in, bias_in[None], padded)
-    out = finish(place, home, weight_aux, part, weight_out, bias_out[None], section, rim, above, below)
+    part, weights = first_part(state, weight_in, bias_in[None], weight_out, padded)
+    out = finish(home, place, weights, part, bias_out[None], section, above, below)
     return out.reshape(prognostic.shape)
 
 

time: 96.9 us -> 96.1 us (level)
  transfers between devices with their start and end apart: 5 -> 5, of which waited for: 3 -> 3; matrix products, arithmetic and copies ran while one was open for 1% -> 1% of each run, Pallas kernels for 37% -> 38%
where the time goes in v5:
time: 96.1 us; the launch traced here: 95.7 us
  Pallas kernels  53.1 us (55%)
  waiting for transfers between devices  23.3 us (24%)
  starting transfers between devices  17.5 us (18%)
  local copies, waits for them, and re-layouts  1.76 us (2%)
    pallas_call x1, Pallas kernels, tendencies(): pl.pallas_call(tend_body, grid=(rows // block,), in_specs=[pl.BlockSpec((...  16.8 us
    all_to_all x1, waiting for transfers between devices, shards(): home = lax.all_to_all(home, AXES, split_axis=0, concat_axis=0, tiled=True)  13.9 us
    pallas_call x1, Pallas kernels, finish(): pl.pallas_call(lambda *refs: finish_body(*refs, block=block), in_specs=[n...  12.9 us
    ppermute x1, waiting for transfers between devices, shards(): left = lax.ppermute(right_out, 'sub', ahead(n_sub))  9.14 us
    pallas_call x1, Pallas kernels, section_of(): pl.pallas_call(lambda *refs: section_body(*refs, per=per), grid=(fields,)...  8.9 us
    pallas_call x1, Pallas kernels, first_part(): pl.pallas_call(lambda *refs: first_body(*refs, padded=padded), grid=(hidd...  8.5 us
    all_to_all x1, starting transfers between devices, shards(): home = lax.all_to_all(home, AXES, split_axis=0, concat_axis=0, tiled=True)  7.33 us
    ppermute x1, starting transfers between devices, shards(): below = lax.ppermute(head, 'curve', back(n_curve))  5.06 us
  transfers between devices with their start and end apart: 5, of which 3 were waited for; matrix products, arithmetic and copies ran while one was open for 1% of the time, Pallas kernels for 38%

profile of v5, /device:TPU:0, one launch (start us, length us, event | category | flops | bytes accessed | tf_op | source)
XLA Modules:
  0.0 95.7 jit_solution(16698972899248172603)
XLA Ops:
  0.0 3.6 %turn.1 = bf16[1536,1024]{1,0:T(8,128)(2,1)} custom-call(bf16[1013,1536]{1,0:T(8,128)(2,1)} %bitcast.15), custom_call_target="tpu_custom_call" | custom-call | tf_op jit(solution)/shard_map/turn/pallas_call | solution.py:63
  3.6 7.3 %all-to-all-start = ((bf16[32,48,1024]{2,1,0:T(8,128)(2,1)}), bf16[32,48,1024]{2,1,0:T(8,128)(2,1)S(1)}, u32[]{:S(2)}, u32[]{:S(2)}) async-start(bf16[32,48,1024]{2,1,0:T(8,128)(2,1)} %bitcast.12), calls=%async_computation | async-start | bytes 6291456 | tf_op jit(solution)/shard_map/all_to_all | solution.py:532
  11.0 16.8 %tendencies.1 = (bf16[4,3072,128]{2,1,0:T(8,128)(2,1)}, bf16[768,512]{1,0:T(8,128)(2,1)}, bf16[5,192,128]{2,1,0:T(8,128)(2,1)}, bf16[5,192,128]{2,1,0:T(8,128)(2,1)}) custom-call(f32[4,3072,128]{2,1,0:T(8,128)} %bitcast.10, f32[3072,128]{1,0:T(8,128)} %bitcast.13, f32[256,128]{1,0:T(8,128)} %constant.10.clone.q_ref, ...), custom_call_target="tpu_custom_call" | custom-call | tf_op jit(solution)/shard_map/tendencies/pallas_call | solution.py:154
  27.7 0.3 collective-permute-start
  28.0 1.5 %collective-permute-start.1 = (bf16[5,192,128]{2,1,0:T(8,128)(2,1)}, bf16[5,192,128]{2,1,0:T(8,128)(2,1)S(1)}, u32[]{:S(2)}, u32[]{:S(2)}) collective-permute-start(bf16[5,192,128]{2,1,0:T(8,128)(2,1)} %get-tuple-element.19), channel_id=1, source_target_pairs={{1,0},{2,1},{3,2},{0,3},{5,4},{6,5},{7,6},{4,7},{9,8},{10,9},{11,1... | collective-permute-start | bytes 737288 | tf_op jit(solution)/shard_map/ppermute | solution.py:546
  29.5 9.1 %collective-permute-done.refs_4_ = bf16[5,192,128]{2,1,0:T(8,128)(2,1)S(1)} collective-permute-done((bf16[5,192,128]{2,1,0:T(8,128)(2,1)}, bf16[5,192,128]{2,1,0:T(8,128)(2,1)S(1)}, u32[]{:S(2)}, u32[]{:S(2)}) %collective-permute-start) | collective-permute-done | bytes 245792 | tf_op jit(solution)/shard_map/ppermute | solution.py:545
  38.6 0.0 copy-start.2
  38.6 0.0 collective-permute-done.1.refs_5_
  38.6 0.0 copy-start.3
  38.6 0.7 copy-done.2
  39.3 0.1 copy-done.3
  39.4 8.9 %section.1 = (bf16[4,3328,128]{2,1,0:T(8,128)(2,1)}, bf16[5,32,128]{2,1,0:T(8,128)(2,1)}, bf16[5,32,128]{2,1,0:T(8,128)(2,1)}) custom-call(bf16[4,3072,128]{2,1,0:T(8,128)(2,1)} %get-tuple-element.17.refs_0_, f32[4,3072,128]{2,1,0:T(8,128)} %bitcast.11, f32[3072,128]{1,0:T(8,128)} %bitcast.14, f32[2,8,128]{2,1,0:T(8,128)} %constant.11.clone.refs_3_, ...), custom_call_target="tpu_custom_call" | custom-call | tf_op jit(solution)/shard_map/section/pallas_call | solution.py:281
  48.3 3.4 %collective-permute-start.2 = (bf16[5,32,128]{2,1,0:T(8,128)(2,1)}, bf16[5,32,128]{2,1,0:T(8,128)(2,1)}, u32[]{:S(2)}, u32[]{:S(2)}) collective-permute-start(bf16[5,32,128]{2,1,0:T(8,128)(2,1)} %get-tuple-element.21), channel_id=1, source_target_pairs={{0,4},{4,8},{8,12},{12,16},{16,20},{20,24},{24,28},{28,0},{1,5},{5... | collective-permute-start | bytes 122888 | tf_op jit(solution)/shard_map/ppermute | solution.py:548
  51.7 5.1 %collective-permute-start.3 = (bf16[5,32,128]{2,1,0:T(8,128)(2,1)}, bf16[5,32,128]{2,1,0:T(8,128)(2,1)}, u32[]{:S(2)}, u32[]{:S(2)}) collective-permute-start(bf16[5,32,128]{2,1,0:T(8,128)(2,1)} %get-tuple-element.22), channel_id=1, source_target_pairs={{4,0},{8,4},{12,8},{16,12},{20,16},{24,20},{28,24},{0,28},{5,1},{9... | collective-permute-start | bytes 122888 | tf_op jit(solution)/shard_map/ppermute | solution.py:549
  56.8 0.0 copy-done.4
  56.8 0.9 copy.13.a
  57.7 2.4 %places.1.refs_1_ = s32[768,1]{1,0:T(8,128)} custom-call(s32[768,1]{1,0:T(8,128)} %copy.13.a), custom_call_target="tpu_custom_call" | custom-call | tf_op jit(solution)/shard_map/places/pallas_call | solution.py:316
  60.1 8.5 %first_part.1 = (bf16[768,2048]{1,0:T(8,128)(2,1)}, bf16[1536,2048]{1,0:T(8,128)(2,1)}) custom-call(bf16[768,512]{1,0:T(8,128)(2,1)} %get-tuple-element.14.refs_0_, bf16[1525,2048]{1,0:T(8,128)(2,1)} %refs_1_.1, f32[1,2048]{1,0:T(1,128)} %bitcast.16, bf16[2048,512]{1,0:T(8,128)(2,1)} %refs_3_.2), custom_call_target="tpu_custom_call" | custom-call | tf_op jit(solution)/shard_map/first_part/pallas_call | solution.py:339
  68.6 0.2 collective-permute-done.2.refs_6_
  68.9 0.0 collective-permute-done.3.refs_7_
  68.9 13.9 %all-to-all-done = bf16[32,48,1024]{2,1,0:T(8,128)(2,1)S(1)} async-done(((bf16[32,48,1024]{2,1,0:T(8,128)(2,1)}), bf16[32,48,1024]{2,1,0:T(8,128)(2,1)S(1)}, u32[]{:S(2)}, u32[]{:S(2)}) %all-to-all-start) | async-done | bytes 3145760 | tf_op jit(solution)/shard_map/all_to_all | solution.py:532
  82.8 0.0 copy-done
  82.8 0.0 copy-done.1
  82.8 12.9 %finish.1 = f32[4,3072,128]{2,1,0:T(8,128)} custom-call(bf16[1536,1024]{1,0:T(8,128)(2,1)S(1)} %bitcast.8, s32[768,1]{1,0:T(8,128)S(1)} %copy-done, bf16[1536,2048]{1,0:T(8,128)(2,1)} %get-tuple-element.15.refs_2_, bf16[768,2048]{1,0:T(8,128)(2,1)} %get-tuple-element.16.refs_3_, f32[1,512]{1,0:T(1,128)S(1)} %bitcast.9, ...), custom_call_target="tpu_custom_call" | custom-call | tf_op jit(solution)/shard_map/finish/pallas_call | solution.py:501
  (3 shorter events, 0.0 us)
Async XLA Ops:
  3.6 79.1 %all-to-all-start = ((bf16[32,48,1024]{2,1,0:T(8,128)(2,1)}), bf16[32,48,1024]{2,1,0:T(8,128)(2,1)S(1)}, u32[]{:S(2)}, u32[]{:S(2)}) async-start(bf16[32,48,1024]{2,1,0:T(8,128)(2,1)} %bitcast.12), calls=%async_computation | async-start | bytes 6291456 | tf_op jit(solution)/shard_map/all_to_all | solution.py:532
  27.7 10.9 %collective-permute-start = (bf16[5,192,128]{2,1,0:T(8,128)(2,1)}, bf16[5,192,128]{2,1,0:T(8,128)(2,1)S(1)}, u32[]{:S(2)}, u32[]{:S(2)}) collective-permute-start(bf16[5,192,128]{2,1,0:T(8,128)(2,1)} %get-tuple-element.18), channel_id=1, source_target_pairs={{0,1},{1,2},{2,3},{3,0},{4,5},{5,6},{6,7},{7,4},{8,9},{9,10},{10,1... | collective-permute-start | bytes 737288 | tf_op jit(solution)/shard_map/ppermute | solution.py:545
  28.0 10.6 %collective-permute-start.1 = (bf16[5,192,128]{2,1,0:T(8,128)(2,1)}, bf16[5,192,128]{2,1,0:T(8,128)(2,1)S(1)}, u32[]{:S(2)}, u32[]{:S(2)}) collective-permute-start(bf16[5,192,128]{2,1,0:T(8,128)(2,1)} %get-tuple-element.19), channel_id=1, source_target_pairs={{1,0},{2,1},{3,2},{0,3},{5,4},{6,5},{7,6},{4,7},{9,8},{10,9},{11,1... | collective-permute-start | bytes 737288 | tf_op jit(solution)/shard_map/ppermute | solution.py:546
  38.6 0.7 copy-start.2
  38.6 0.8 copy-start.3
  39.4 17.4 %copy-start.4 = (s32[768,1]{0,1:T(1,128)S(1)}, s32[768,1]{0,1:T(1,128)}, u32[]{:S(2)}) copy-start(s32[768,1]{0,1:T(1,128)} %param.15) | copy-start | bytes 9220
  48.3 20.5 %collective-permute-start.2 = (bf16[5,32,128]{2,1,0:T(8,128)(2,1)}, bf16[5,32,128]{2,1,0:T(8,128)(2,1)}, u32[]{:S(2)}, u32[]{:S(2)}) collective-permute-start(bf16[5,32,128]{2,1,0:T(8,128)(2,1)} %get-tuple-element.21), channel_id=1, source_target_pairs={{0,4},{4,8},{8,12},{12,16},{16,20},{20,24},{24,28},{28,0},{1,5},{5... | collective-permute-start | bytes 122888 | tf_op jit(solution)/shard_map/ppermute | solution.py:548
  51.7 17.1 %collective-permute-start.3 = (bf16[5,32,128]{2,1,0:T(8,128)(2,1)}, bf16[5,32,128]{2,1,0:T(8,128)(2,1)}, u32[]{:S(2)}, u32[]{:S(2)}) collective-permute-start(bf16[5,32,128]{2,1,0:T(8,128)(2,1)} %get-tuple-element.22), channel_id=1, source_target_pairs={{4,0},{8,4},{12,8},{16,12},{20,16},{24,20},{28,24},{0,28},{5,1},{9... | collective-permute-start | bytes 122888 | tf_op jit(solution)/shard_map/ppermute | solution.py:549
  60.1 22.6 %copy-start = (s32[768,1]{1,0:T(8,128)S(1)}, s32[768,1]{1,0:T(8,128)}, u32[]{:S(2)}) copy-start(s32[768,1]{1,0:T(8,128)} %places.1.refs_1_) | copy-start | bytes 9220
  60.1 22.6 %copy-start.1 = (f32[512]{0:T(512)S(1)}, f32[512]{0:T(512)}, u32[]{:S(2)}) copy-start(f32[512]{0:T(512)} %param.19) | copy-start | bytes 6148

commit v6 on v5

--- a/solution.py
+++ b/solution.py
@@ -51,21 +51,46 @@
     return pltpu.roll(x, shift % 8, axis=1)
 
 
-def turn_body(x_ref, o_ref):
-    width = x_ref.shape[0]
-    o_ref[:, :width] = x_ref[...].T
-    o_ref[:, width:] = jnp.zeros((o_ref.shape[0], o_ref.shape[1] - width), BF16)
+def turn_body(x_hbm, o_hbm, x_ref, o_ref, in_sem, out_sem):
+    pieces = in_sem.shape[0]
+    width, rows = x_ref.shape
+    n = rows // pieces
+
+    def take(k):
+        lanes = pl.ds(k * n, n)
+        return pltpu.make_async_copy(x_hbm.at[:, lanes], x_ref.at[:, lanes], in_sem.at[k])
+
+    def give(k):
+        at = pl.ds(k * n, n)
+        return pltpu.make_async_copy(o_ref.at[at, :], o_hbm.at[at, :], out_sem.at[k])
+
+    for k in range(pieces):
+        take(k).start()
+    o_ref[:, width:] = jnp.zeros((rows, o_ref.shape[1] - width), BF16)
+    for k in range(pieces):
+        take(k).wait()
+        at = slice(k * n, (k + 1) * n)
+        o_ref[at, :width] = x_ref[:, at].T
+        give(k).start()
+    for k in range(pieces):
+        give(k).wait()
 
 
 def turn(aux_t, padded):
     width, rows = aux_t.shape
-    block = rows // 2
+    pieces = 3
+    far = pl.BlockSpec(memory_space=pltpu.HBM)
     return pl.pallas_call(
         turn_body,
-        grid=(rows // block,),
-        in_specs=[pl.BlockSpec((width, block), lambda i: (0, i))],
-        out_specs=pl.BlockSpec((block, padded), lambda i: (i, 0)),
+        in_specs=[far],
+        out_specs=far,
         out_shape=jax.ShapeDtypeStruct((rows, padded), BF16),
+        scratch_shapes=[
+            pltpu.VMEM((width, rows), BF16),
+            pltpu.VMEM((rows, padded), BF16),
+            pltpu.SemaphoreType.DMA((pieces,)),
+            pltpu.SemaphoreType.DMA((pieces,)),
+        ],
         name="turn",
         compiler_params=pltpu.CompilerParams(vmem_limit_bytes=56 << 20),
     )(aux_t)
@@ -441,7 +466,7 @@
     wait("w0", "w1", "part0", "edge")
 
     def out_copy(k):
-        at = pl.ds(pl.multiple_of(k * block * 4, block * 4), block * 4)
+        at = pl.ds(pl.multiple_of(k * group * 4, group * 4), group * 4)
         return pltpu.make_async_copy(o_ref.at[:, at, :], out_hbm.at[:, at, :], out_sem.at[k])
 
     def layers(k, carry):
@@ -473,21 +498,25 @@
             to = pl.ds(pl.multiple_of((k * block + g * group) * 4, group * 4), group * 4)
             for f in range(fields):
                 o_ref[f, to, :] = x_ref[f, to, :].astype(F32) + wide[:, f * levels : (f + 1) * levels]
-
-        @pl.when(k == 0)
-        def _():
-            patch(0, above_ref, 0)
-
-        @pl.when(k == steps - 1)
-        def _():
-            patch(1, below_ref, rows - per * 16)
-
-        out_copy(k).start()
+            if g == 0:
+
+                @pl.when(k == 0)
+                def _():
+                    patch(0, above_ref, 0)
+
+            if g == block // group - 1:
+
+                @pl.when(k == steps - 1)
+                def _():
+                    patch(1, below_ref, rows - per * 16)
+
+            out_copy(k * (block // group) + g).start()
+
         return carry
 
     lax.fori_loop(0, steps, layers, 0)
-    for k in range(steps):
-        out_copy(k).wait()
+    for g in range(cols // group):
+        out_copy(g).wait()
 
 
 def finish(home, place, weights, part, bias_out, x, above, below):
@@ -510,7 +539,7 @@
             pltpu.VMEM((512, 128), BF16),
             pltpu.VMEM(result, F32),
             pltpu.SemaphoreType.DMA((3 + 2 * steps,)),
-            pltpu.SemaphoreType.DMA((steps,)),
+            pltpu.SemaphoreType.DMA((cols // 128,)),
         ],
         name="finish",
         compiler_params=pltpu.CompilerParams(vmem_limit_bytes=48 << 20),

time: 96.1 us -> 95.6 us (level)
  no operation moved by 1% of the time
where the time goes in v6:
time: 95.6 us; the launch traced here: 95.2 us
  Pallas kernels  52.6 us (55%)
  waiting for transfers between devices  23.3 us (24%)
  starting transfers between devices  17.6 us (18%)
  local copies, waits for them, and re-layouts  1.76 us (2%)
    pallas_call x1, Pallas kernels, tendencies(): pl.pallas_call(tend_body, grid=(rows // block,), in_specs=[pl.BlockSpec((...  16.8 us
    all_to_all x1, waiting for transfers between devices, shards(): home = lax.all_to_all(home, AXES, split_axis=0, concat_axis=0, tiled=True)  13.9 us
    pallas_call x1, Pallas kernels, finish(): pl.pallas_call(lambda *refs: finish_body(*refs, block=block), in_specs=[n...  12.8 us
    ppermute x1, waiting for transfers between devices, shards(): left = lax.ppermute(right_out, 'sub', ahead(n_sub))  9.14 us
    pallas_call x1, Pallas kernels, section_of(): pl.pallas_call(lambda *refs: section_body(*refs, per=per), grid=(fields,)...  8.9 us
    pallas_call x1, Pallas kernels, first_part(): pl.pallas_call(lambda *refs: first_body(*refs, padded=padded), grid=(hidd...  8.5 us
    all_to_all x1, starting transfers between devices, shards(): home = lax.all_to_all(home, AXES, split_axis=0, concat_axis=0, tiled=True)  7.33 us
    ppermute x1, starting transfers between devices, shards(): below = lax.ppermute(head, 'curve', back(n_curve))  5.06 us
  transfers between devices with their start and end apart: 5, of which 3 were waited for; matrix products, arithmetic and copies ran while one was open for 1% of the time, Pallas kernels for 38%

profile of v6, /device:TPU:0, one launch (start us, length us, event | category | flops | bytes accessed | tf_op | source)
XLA Modules:
  0.0 95.2 jit_solution(14579495509555929166)
XLA Ops:
  0.0 3.3 %turn.1 = bf16[1536,1024]{1,0:T(8,128)(2,1)} custom-call(bf16[1013,1536]{1,0:T(8,128)(2,1)} %bitcast.15), custom_call_target="tpu_custom_call" | custom-call | tf_op jit(solution)/shard_map/turn/pallas_call | solution.py:83
  3.3 7.3 %all-to-all-start = ((bf16[32,48,1024]{2,1,0:T(8,128)(2,1)}), bf16[32,48,1024]{2,1,0:T(8,128)(2,1)S(1)}, u32[]{:S(2)}, u32[]{:S(2)}) async-start(bf16[32,48,1024]{2,1,0:T(8,128)(2,1)} %bitcast.12), calls=%async_computation | async-start | bytes 6291456 | tf_op jit(solution)/shard_map/all_to_all | solution.py:561
  10.6 16.8 %tendencies.1 = (bf16[4,3072,128]{2,1,0:T(8,128)(2,1)}, bf16[768,512]{1,0:T(8,128)(2,1)}, bf16[5,192,128]{2,1,0:T(8,128)(2,1)}, bf16[5,192,128]{2,1,0:T(8,128)(2,1)}) custom-call(f32[4,3072,128]{2,1,0:T(8,128)} %bitcast.10, f32[3072,128]{1,0:T(8,128)} %bitcast.13, f32[256,128]{1,0:T(8,128)} %constant.10.clone.q_ref, ...), custom_call_target="tpu_custom_call" | custom-call | tf_op jit(solution)/shard_map/tendencies/pallas_call | solution.py:179
  27.4 0.2 collective-permute-start
  27.6 1.5 %collective-permute-start.1 = (bf16[5,192,128]{2,1,0:T(8,128)(2,1)}, bf16[5,192,128]{2,1,0:T(8,128)(2,1)S(1)}, u32[]{:S(2)}, u32[]{:S(2)}) collective-permute-start(bf16[5,192,128]{2,1,0:T(8,128)(2,1)} %get-tuple-element.19), channel_id=1, source_target_pairs={{1,0},{2,1},{3,2},{0,3},{5,4},{6,5},{7,6},{4,7},{9,8},{10,9},{11,1... | collective-permute-start | bytes 737288 | tf_op jit(solution)/shard_map/ppermute | solution.py:575
  29.1 9.1 %collective-permute-done.refs_4_ = bf16[5,192,128]{2,1,0:T(8,128)(2,1)S(1)} collective-permute-done((bf16[5,192,128]{2,1,0:T(8,128)(2,1)}, bf16[5,192,128]{2,1,0:T(8,128)(2,1)S(1)}, u32[]{:S(2)}, u32[]{:S(2)}) %collective-permute-start) | collective-permute-done | bytes 245792 | tf_op jit(solution)/shard_map/ppermute | solution.py:574
  38.3 0.0 copy-start.2
  38.3 0.0 collective-permute-done.1.refs_5_
  38.3 0.0 copy-start.3
  38.3 0.7 copy-done.2
  39.0 0.1 copy-done.3
  39.1 8.9 %section.1 = (bf16[4,3328,128]{2,1,0:T(8,128)(2,1)}, bf16[5,32,128]{2,1,0:T(8,128)(2,1)}, bf16[5,32,128]{2,1,0:T(8,128)(2,1)}) custom-call(bf16[4,3072,128]{2,1,0:T(8,128)(2,1)} %get-tuple-element.17.refs_0_, f32[4,3072,128]{2,1,0:T(8,128)} %bitcast.11, f32[3072,128]{1,0:T(8,128)} %bitcast.14, f32[2,8,128]{2,1,0:T(8,128)} %constant.11.clone.refs_3_, ...), custom_call_target="tpu_custom_call" | custom-call | tf_op jit(solution)/shard_map/section/pallas_call | solution.py:306
  48.0 3.4 %collective-permute-start.2 = (bf16[5,32,128]{2,1,0:T(8,128)(2,1)}, bf16[5,32,128]{2,1,0:T(8,128)(2,1)}, u32[]{:S(2)}, u32[]{:S(2)}) collective-permute-start(bf16[5,32,128]{2,1,0:T(8,128)(2,1)} %get-tuple-element.21), channel_id=1, source_target_pairs={{0,4},{4,8},{8,12},{12,16},{16,20},{20,24},{24,28},{28,0},{1,5},{5... | collective-permute-start | bytes 122888 | tf_op jit(solution)/shard_map/ppermute | solution.py:577
  51.4 5.1 %collective-permute-start.3 = (bf16[5,32,128]{2,1,0:T(8,128)(2,1)}, bf16[5,32,128]{2,1,0:T(8,128)(2,1)}, u32[]{:S(2)}, u32[]{:S(2)}) collective-permute-start(bf16[5,32,128]{2,1,0:T(8,128)(2,1)} %get-tuple-element.22), channel_id=1, source_target_pairs={{4,0},{8,4},{12,8},{16,12},{20,16},{24,20},{28,24},{0,28},{5,1},{9... | collective-permute-start | bytes 122888 | tf_op jit(solution)/shard_map/ppermute | solution.py:578
  56.5 0.0 copy-done.4
  56.5 0.9 copy.13.a
  57.4 2.4 %places.1.refs_1_ = s32[768,1]{1,0:T(8,128)} custom-call(s32[768,1]{1,0:T(8,128)} %copy.13.a), custom_call_target="tpu_custom_call" | custom-call | tf_op jit(solution)/shard_map/places/pallas_call | solution.py:341
  59.8 8.5 %first_part.1 = (bf16[768,2048]{1,0:T(8,128)(2,1)}, bf16[1536,2048]{1,0:T(8,128)(2,1)}) custom-call(bf16[768,512]{1,0:T(8,128)(2,1)} %get-tuple-element.14.refs_0_, bf16[1525,2048]{1,0:T(8,128)(2,1)} %refs_1_.1, f32[1,2048]{1,0:T(1,128)} %bitcast.16, bf16[2048,512]{1,0:T(8,128)(2,1)} %refs_3_.2), custom_call_target="tpu_custom_call" | custom-call | tf_op jit(solution)/shard_map/first_part/pallas_call | solution.py:364
  68.3 0.2 collective-permute-done.2.refs_6_
  68.5 0.0 collective-permute-done.3.refs_7_
  68.6 13.9 %all-to-all-done = bf16[32,48,1024]{2,1,0:T(8,128)(2,1)S(1)} async-done(((bf16[32,48,1024]{2,1,0:T(8,128)(2,1)}), bf16[32,48,1024]{2,1,0:T(8,128)(2,1)S(1)}, u32[]{:S(2)}, u32[]{:S(2)}) %all-to-all-start) | async-done | bytes 3145760 | tf_op jit(solution)/shard_map/all_to_all | solution.py:561
  82.5 0.0 copy-done
  82.5 0.0 copy-done.1
  82.5 12.8 %finish.1 = f32[4,3072,128]{2,1,0:T(8,128)} custom-call(bf16[1536,1024]{1,0:T(8,128)(2,1)S(1)} %bitcast.8, s32[768,1]{1,0:T(8,128)S(1)} %copy-done, bf16[1536,2048]{1,0:T(8,128)(2,1)} %get-tuple-element.15.refs_2_, bf16[768,2048]{1,0:T(8,128)(2,1)} %get-tuple-element.16.refs_3_, f32[1,512]{1,0:T(1,128)S(1)} %bitcast.9, ...), custom_call_target="tpu_custom_call" | custom-call | tf_op jit(solution)/shard_map/finish/pallas_call | solution.py:530
  (3 shorter events, 0.0 us)
Async XLA Ops:
  3.3 79.2 %all-to-all-start = ((bf16[32,48,1024]{2,1,0:T(8,128)(2,1)}), bf16[32,48,1024]{2,1,0:T(8,128)(2,1)S(1)}, u32[]{:S(2)}, u32[]{:S(2)}) async-start(bf16[32,48,1024]{2,1,0:T(8,128)(2,1)} %bitcast.12), calls=%async_computation | async-start | bytes 6291456 | tf_op jit(solution)/shard_map/all_to_all | solution.py:561
  27.4 10.9 %collective-permute-start = (bf16[5,192,128]{2,1,0:T(8,128)(2,1)}, bf16[5,192,128]{2,1,0:T(8,128)(2,1)S(1)}, u32[]{:S(2)}, u32[]{:S(2)}) collective-permute-start(bf16[5,192,128]{2,1,0:T(8,128)(2,1)} %get-tuple-element.18), channel_id=1, source_target_pairs={{0,1},{1,2},{2,3},{3,0},{4,5},{5,6},{6,7},{7,4},{8,9},{9,10},{10,1... | collective-permute-start | bytes 737288 | tf_op jit(solution)/shard_map/ppermute | solution.py:574
  27.6 10.6 %collective-permute-start.1 = (bf16[5,192,128]{2,1,0:T(8,128)(2,1)}, bf16[5,192,128]{2,1,0:T(8,128)(2,1)S(1)}, u32[]{:S(2)}, u32[]{:S(2)}) collective-permute-start(bf16[5,192,128]{2,1,0:T(8,128)(2,1)} %get-tuple-element.19), channel_id=1, source_target_pairs={{1,0},{2,1},{3,2},{0,3},{5,4},{6,5},{7,6},{4,7},{9,8},{10,9},{11,1... | collective-permute-start | bytes 737288 | tf_op jit(solution)/shard_map/ppermute | solution.py:575
  38.3 0.7 copy-start.2
  38.3 0.8 copy-start.3
  39.1 17.4 %copy-start.4 = (s32[768,1]{0,1:T(1,128)S(1)}, s32[768,1]{0,1:T(1,128)}, u32[]{:S(2)}) copy-start(s32[768,1]{0,1:T(1,128)} %param.15) | copy-start | bytes 9220
  48.0 20.5 %collective-permute-start.2 = (bf16[5,32,128]{2,1,0:T(8,128)(2,1)}, bf16[5,32,128]{2,1,0:T(8,128)(2,1)}, u32[]{:S(2)}, u32[]{:S(2)}) collective-permute-start(bf16[5,32,128]{2,1,0:T(8,128)(2,1)} %get-tuple-element.21), channel_id=1, source_target_pairs={{0,4},{4,8},{8,12},{12,16},{16,20},{20,24},{24,28},{28,0},{1,5},{5... | collective-permute-start | bytes 122888 | tf_op jit(solution)/shard_map/ppermute | solution.py:577
  51.4 17.1 %collective-permute-start.3 = (bf16[5,32,128]{2,1,0:T(8,128)(2,1)}, bf16[5,32,128]{2,1,0:T(8,128)(2,1)}, u32[]{:S(2)}, u32[]{:S(2)}) collective-permute-start(bf16[5,32,128]{2,1,0:T(8,128)(2,1)} %get-tuple-element.22), channel_id=1, source_target_pairs={{4,0},{8,4},{12,8},{16,12},{20,16},{24,20},{28,24},{0,28},{5,1},{9... | collective-permute-start | bytes 122888 | tf_op jit(solution)/shard_map/ppermute | solution.py:578
  59.8 22.6 %copy-start = (s32[768,1]{1,0:T(8,128)S(1)}, s32[768,1]{1,0:T(8,128)}, u32[]{:S(2)}) copy-start(s32[768,1]{1,0:T(8,128)} %places.1.refs_1_) | copy-start | bytes 9220
  59.8 22.6 %copy-start.1 = (f32[512]{0:T(512)S(1)}, f32[512]{0:T(512)}, u32[]{:S(2)}) copy-start(f32[512]{0:T(512)} %param.19) | copy-start | bytes 6148

commit v7 on v6

--- a/solution.py
+++ b/solution.py
@@ -78,7 +78,7 @@
 
 def turn(aux_t, padded):
     width, rows = aux_t.shape
-    pieces = 3
+    pieces = 6
     far = pl.BlockSpec(memory_space=pltpu.HBM)
     return pl.pallas_call(
         turn_body,

time: 95.6 us -> 95.4 us (level)
  no operation moved by 1% of the time
where the time goes in v7:
time: 95.4 us; the launch traced here: 95.1 us
  Pallas kernels  52.4 us (55%)
  waiting for transfers between devices  23.3 us (24%)
  starting transfers between devices  17.6 us (18%)
  local copies, waits for them, and re-layouts  1.76 us (2%)
    pallas_call x1, Pallas kernels, tendencies(): pl.pallas_call(tend_body, grid=(rows // block,), in_specs=[pl.BlockSpec((...  16.8 us
    all_to_all x1, waiting for transfers between devices, shards(): home = lax.all_to_all(home, AXES, split_axis=0, concat_axis=0, tiled=True)  13.9 us
    pallas_call x1, Pallas kernels, finish(): pl.pallas_call(lambda *refs: finish_body(*refs, block=block), in_specs=[n...  12.7 us
    ppermute x1, waiting for transfers between devices, shards(): left = lax.ppermute(right_out, 'sub', ahead(n_sub))  9.14 us
    pallas_call x1, Pallas kernels, section_of(): pl.pallas_call(lambda *refs: section_body(*refs, per=per), grid=(fields,)...  8.9 us
    pallas_call x1, Pallas kernels, first_part(): pl.pallas_call(lambda *refs: first_body(*refs, padded=padded), grid=(hidd...  8.5 us
    all_to_all x1, starting transfers between devices, shards(): home = lax.all_to_all(home, AXES, split_axis=0, concat_axis=0, tiled=True)  7.33 us
    ppermute x1, starting transfers between devices, shards(): below = lax.ppermute(head, 'curve', back(n_curve))  5.05 us
  transfers between devices with their start and end apart: 5, of which 3 were waited for; matrix products, arithmetic and copies ran while one was open for 1% of the time, Pallas kernels for 38%

profile of v7, /device:TPU:0, one launch (start us, length us, event | category | flops | bytes accessed | tf_op | source)
XLA Modules:
  0.0 95.1 jit_solution(16354233011576709530)
XLA Ops:
  0.0 3.1 %turn.1 = bf16[1536,1024]{1,0:T(8,128)(2,1)} custom-call(bf16[1013,1536]{1,0:T(8,128)(2,1)} %bitcast.15), custom_call_target="tpu_custom_call" | custom-call | tf_op jit(solution)/shard_map/turn/pallas_call | solution.py:83
  3.2 7.3 %all-to-all-start = ((bf16[32,48,1024]{2,1,0:T(8,128)(2,1)}), bf16[32,48,1024]{2,1,0:T(8,128)(2,1)S(1)}, u32[]{:S(2)}, u32[]{:S(2)}) async-start(bf16[32,48,1024]{2,1,0:T(8,128)(2,1)} %bitcast.12), calls=%async_computation | async-start | bytes 6291456 | tf_op jit(solution)/shard_map/all_to_all | solution.py:561
  10.5 16.8 %tendencies.1 = (bf16[4,3072,128]{2,1,0:T(8,128)(2,1)}, bf16[768,512]{1,0:T(8,128)(2,1)}, bf16[5,192,128]{2,1,0:T(8,128)(2,1)}, bf16[5,192,128]{2,1,0:T(8,128)(2,1)}) custom-call(f32[4,3072,128]{2,1,0:T(8,128)} %bitcast.10, f32[3072,128]{1,0:T(8,128)} %bitcast.13, f32[256,128]{1,0:T(8,128)} %constant.10.clone.q_ref, ...), custom_call_target="tpu_custom_call" | custom-call | tf_op jit(solution)/shard_map/tendencies/pallas_call | solution.py:179
  27.3 0.3 collective-permute-start
  27.5 1.5 %collective-permute-start.1 = (bf16[5,192,128]{2,1,0:T(8,128)(2,1)}, bf16[5,192,128]{2,1,0:T(8,128)(2,1)S(1)}, u32[]{:S(2)}, u32[]{:S(2)}) collective-permute-start(bf16[5,192,128]{2,1,0:T(8,128)(2,1)} %get-tuple-element.19), channel_id=1, source_target_pairs={{1,0},{2,1},{3,2},{0,3},{5,4},{6,5},{7,6},{4,7},{9,8},{10,9},{11,1... | collective-permute-start | bytes 737288 | tf_op jit(solution)/shard_map/ppermute | solution.py:575
  29.0 9.1 %collective-permute-done.refs_4_ = bf16[5,192,128]{2,1,0:T(8,128)(2,1)S(1)} collective-permute-done((bf16[5,192,128]{2,1,0:T(8,128)(2,1)}, bf16[5,192,128]{2,1,0:T(8,128)(2,1)S(1)}, u32[]{:S(2)}, u32[]{:S(2)}) %collective-permute-start) | collective-permute-done | bytes 245792 | tf_op jit(solution)/shard_map/ppermute | solution.py:574
  38.1 0.0 copy-start.2
  38.1 0.0 collective-permute-done.1.refs_5_
  38.1 0.0 copy-start.3
  38.2 0.7 copy-done.2
  38.8 0.1 copy-done.3
  39.0 8.9 %section.1 = (bf16[4,3328,128]{2,1,0:T(8,128)(2,1)}, bf16[5,32,128]{2,1,0:T(8,128)(2,1)}, bf16[5,32,128]{2,1,0:T(8,128)(2,1)}) custom-call(bf16[4,3072,128]{2,1,0:T(8,128)(2,1)} %get-tuple-element.17.refs_0_, f32[4,3072,128]{2,1,0:T(8,128)} %bitcast.11, f32[3072,128]{1,0:T(8,128)} %bitcast.14, f32[2,8,128]{2,1,0:T(8,128)} %constant.11.clone.refs_3_, ...), custom_call_target="tpu_custom_call" | custom-call | tf_op jit(solution)/shard_map/section/pallas_call | solution.py:306
  47.9 3.4 %collective-permute-start.2 = (bf16[5,32,128]{2,1,0:T(8,128)(2,1)}, bf16[5,32,128]{2,1,0:T(8,128)(2,1)}, u32[]{:S(2)}, u32[]{:S(2)}) collective-permute-start(bf16[5,32,128]{2,1,0:T(8,128)(2,1)} %get-tuple-element.21), channel_id=1, source_target_pairs={{0,4},{4,8},{8,12},{12,16},{16,20},{20,24},{24,28},{28,0},{1,5},{5... | collective-permute-start | bytes 122888 | tf_op jit(solution)/shard_map/ppermute | solution.py:577
  51.3 5.1 %collective-permute-start.3 = (bf16[5,32,128]{2,1,0:T(8,128)(2,1)}, bf16[5,32,128]{2,1,0:T(8,128)(2,1)}, u32[]{:S(2)}, u32[]{:S(2)}) collective-permute-start(bf16[5,32,128]{2,1,0:T(8,128)(2,1)} %get-tuple-element.22), channel_id=1, source_target_pairs={{4,0},{8,4},{12,8},{16,12},{20,16},{24,20},{28,24},{0,28},{5,1},{9... | collective-permute-start | bytes 122888 | tf_op jit(solution)/shard_map/ppermute | solution.py:578
  56.3 0.0 copy-done.4
  56.3 0.9 copy.13.a
  57.3 2.4 %places.1.refs_1_ = s32[768,1]{1,0:T(8,128)} custom-call(s32[768,1]{1,0:T(8,128)} %copy.13.a), custom_call_target="tpu_custom_call" | custom-call | tf_op jit(solution)/shard_map/places/pallas_call | solution.py:341
  59.7 8.5 %first_part.1 = (bf16[768,2048]{1,0:T(8,128)(2,1)}, bf16[1536,2048]{1,0:T(8,128)(2,1)}) custom-call(bf16[768,512]{1,0:T(8,128)(2,1)} %get-tuple-element.14.refs_0_, bf16[1525,2048]{1,0:T(8,128)(2,1)} %refs_1_.1, f32[1,2048]{1,0:T(1,128)} %bitcast.16, bf16[2048,512]{1,0:T(8,128)(2,1)} %refs_3_.2), custom_call_target="tpu_custom_call" | custom-call | tf_op jit(solution)/shard_map/first_part/pallas_call | solution.py:364
  68.2 0.2 collective-permute-done.2.refs_6_
  68.4 0.0 collective-permute-done.3.refs_7_
  68.4 13.9 %all-to-all-done = bf16[32,48,1024]{2,1,0:T(8,128)(2,1)S(1)} async-done(((bf16[32,48,1024]{2,1,0:T(8,128)(2,1)}), bf16[32,48,1024]{2,1,0:T(8,128)(2,1)S(1)}, u32[]{:S(2)}, u32[]{:S(2)}) %all-to-all-start) | async-done | bytes 3145760 | tf_op jit(solution)/shard_map/all_to_all | solution.py:561
  82.3 0.0 copy-done
  82.3 0.0 copy-done.1
  82.3 12.7 %finish.1 = f32[4,3072,128]{2,1,0:T(8,128)} custom-call(bf16[1536,1024]{1,0:T(8,128)(2,1)S(1)} %bitcast.8, s32[768,1]{1,0:T(8,128)S(1)} %copy-done, bf16[1536,2048]{1,0:T(8,128)(2,1)} %get-tuple-element.15.refs_2_, bf16[768,2048]{1,0:T(8,128)(2,1)} %get-tuple-element.16.refs_3_, f32[1,512]{1,0:T(1,128)S(1)} %bitcast.9, ...), custom_call_target="tpu_custom_call" | custom-call | tf_op jit(solution)/shard_map/finish/pallas_call | solution.py:530
  (3 shorter events, 0.0 us)
Async XLA Ops:
  3.2 79.2 %all-to-all-start = ((bf16[32,48,1024]{2,1,0:T(8,128)(2,1)}), bf16[32,48,1024]{2,1,0:T(8,128)(2,1)S(1)}, u32[]{:S(2)}, u32[]{:S(2)}) async-start(bf16[32,48,1024]{2,1,0:T(8,128)(2,1)} %bitcast.12), calls=%async_computation | async-start | bytes 6291456 | tf_op jit(solution)/shard_map/all_to_all | solution.py:561
  27.3 10.9 %collective-permute-start = (bf16[5,192,128]{2,1,0:T(8,128)(2,1)}, bf16[5,192,128]{2,1,0:T(8,128)(2,1)S(1)}, u32[]{:S(2)}, u32[]{:S(2)}) collective-permute-start(bf16[5,192,128]{2,1,0:T(8,128)(2,1)} %get-tuple-element.18), channel_id=1, source_target_pairs={{0,1},{1,2},{2,3},{3,0},{4,5},{5,6},{6,7},{7,4},{8,9},{9,10},{10,1... | collective-permute-start | bytes 737288 | tf_op jit(solution)/shard_map/ppermute | solution.py:574
  27.5 10.6 %collective-permute-start.1 = (bf16[5,192,128]{2,1,0:T(8,128)(2,1)}, bf16[5,192,128]{2,1,0:T(8,128)(2,1)S(1)}, u32[]{:S(2)}, u32[]{:S(2)}) collective-permute-start(bf16[5,192,128]{2,1,0:T(8,128)(2,1)} %get-tuple-element.19), channel_id=1, source_target_pairs={{1,0},{2,1},{3,2},{0,3},{5,4},{6,5},{7,6},{4,7},{9,8},{10,9},{11,1... | collective-permute-start | bytes 737288 | tf_op jit(solution)/shard_map/ppermute | solution.py:575
  38.1 0.7 copy-start.2
  38.1 0.8 copy-start.3
  39.0 17.4 %copy-start.4 = (s32[768,1]{0,1:T(1,128)S(1)}, s32[768,1]{0,1:T(1,128)}, u32[]{:S(2)}) copy-start(s32[768,1]{0,1:T(1,128)} %param.15) | copy-start | bytes 9220
  47.9 20.5 %collective-permute-start.2 = (bf16[5,32,128]{2,1,0:T(8,128)(2,1)}, bf16[5,32,128]{2,1,0:T(8,128)(2,1)}, u32[]{:S(2)}, u32[]{:S(2)}) collective-permute-start(bf16[5,32,128]{2,1,0:T(8,128)(2,1)} %get-tuple-element.21), channel_id=1, source_target_pairs={{0,4},{4,8},{8,12},{12,16},{16,20},{20,24},{24,28},{28,0},{1,5},{5... | collective-permute-start | bytes 122888 | tf_op jit(solution)/shard_map/ppermute | solution.py:577
  51.3 17.1 %collective-permute-start.3 = (bf16[5,32,128]{2,1,0:T(8,128)(2,1)}, bf16[5,32,128]{2,1,0:T(8,128)(2,1)}, u32[]{:S(2)}, u32[]{:S(2)}) collective-permute-start(bf16[5,32,128]{2,1,0:T(8,128)(2,1)} %get-tuple-element.22), channel_id=1, source_target_pairs={{4,0},{8,4},{12,8},{16,12},{20,16},{24,20},{28,24},{0,28},{5,1},{9... | collective-permute-start | bytes 122888 | tf_op jit(solution)/shard_map/ppermute | solution.py:578
  59.7 22.6 %copy-start = (s32[768,1]{1,0:T(8,128)S(1)}, s32[768,1]{1,0:T(8,128)}, u32[]{:S(2)}) copy-start(s32[768,1]{1,0:T(8,128)} %places.1.refs_1_) | copy-start | bytes 9220
  59.7 22.6 %copy-start.1 = (f32[512]{0:T(512)S(1)}, f32[512]{0:T(512)}, u32[]{:S(2)}) copy-start(f32[512]{0:T(512)} %param.19) | copy-start | bytes 6148
